TPU v7x, 32 devices: a whole 2x2x4 slice. The times are simulated.
32 devices in a mesh: fsdp: 4 (over y, core), sp: 8 (over z, x).
Axes of the slice: x: 2, y: 2, z: 4, core: 2. Of those that a mesh axis runs over, the one named last changes fastest.
Arguments:
- hidden: bfloat16 [4, 2048, 5120], P('fsdp', 'sp'), may hold values from -6 to 6
- queries: bfloat16 [4, 2048, 4096], P('fsdp', 'sp'), may hold values from -240 to 240
- norm_gain: float32 [5120], replicated, may hold values from 0.5 to 1.5
- kv_weight: bfloat16 [5120, 2048], P('fsdp'), may hold values from -0.078125 to 0.078125
- value_bias: float32 [1024], replicated, may hold values from -3 to 3
- doc_lengths: int32 [4, 16], P('fsdp'), may hold values from 1 to 512, 2048 in all within a row
Outputs:
- attended: bfloat16 [4, 2048, 4096], P('fsdp', 'sp')
Inputs may be any that keep to these rules, and one draw needn't show every extreme that they name: `doc_lengths`: each row sums to 2048 and its largest entry is 512.
All inputs are finite; a program needn't handle non-finite values.
Results may differ from a plain program's by a relative error of at most 0.0067.
Values may be sent and summed in bfloat16 or wider, within the bound.
No kernel may reach another device: no remote copies, remote signals or barrier semaphores. Data moves between devices by JAX's collectives and lax.ppermute only.
A program may use at most 128 MiB of HBM per device.

v0:
```python
import jax
import jax.numpy as jnp
from jax import lax
from jax.sharding import PartitionSpec as P

QH = 32
KVH = 8
HD = 128


EPS = 1e-06


def from_behind(value, axis, by):
    count = lax.axis_size(axis)
    pairs = [(i, i + by) for i in range(count) if 0 <= i + by < count]
    return lax.ppermute(value, axis, pairs)


def attend_near(query_rows, key_all, value_all, query_pos, key_pos, query_ids, key_ids):
    token_count = query_rows.shape[0]
    ratio = QH // KVH
    scale = HD ** (-0.5)
    allowed = (
        (key_pos[None, :] >= 0)
        & (key_pos[None, :] <= query_pos[:, None])
        & (key_ids[None, :] == query_ids[:, None])
    )
    query_groups = jnp.transpose(query_rows.reshape(token_count, KVH, ratio, HD), (1, 0, 2, 3))
    key_groups = jnp.transpose(key_all, (1, 0, 2))
    value_groups = jnp.transpose(value_all, (1, 0, 2))

    def one_group(operands):
        query_one, key_one, value_one = operands
        scores = (
            jnp.einsum("qrd,kd->rqk", query_one, key_one, preferred_element_type=jnp.float32)
            * scale
        )
        scores = jnp.where(allowed[None], scores, -jnp.inf)
        highest = jnp.max(scores, axis=-1, keepdims=True)
        probs = jnp.exp(scores - highest)
        probs = (probs / jnp.sum(probs, axis=-1, keepdims=True)).astype(jnp.bfloat16)
        output = jnp.einsum("rqk,kd->qrd", probs, value_one, preferred_element_type=jnp.float32)
        return output.astype(jnp.bfloat16)

    outputs = lax.map(one_group, (query_groups, key_groups, value_groups))
    return jnp.transpose(outputs, (1, 0, 2, 3)).reshape(token_count, QH * HD)


def shards(hidden, queries, norm_gain, kv_weight, value_bias, doc_lengths):
    token_count = hidden.shape[1]
    group_size = lax.axis_size("sp")
    query_rows = queries[0]
    wide = hidden[0].astype(jnp.float32)
    normed = (
        wide * lax.rsqrt(jnp.mean(wide * wide, axis=-1, keepdims=True) + EPS) * norm_gain
    ).astype(jnp.bfloat16)
    projected = jnp.dot(
        normed,
        lax.all_gather(kv_weight, "fsdp", axis=0, tiled=True),
        preferred_element_type=jnp.float32,
    )
    keys = projected[:, : KVH * HD].astype(jnp.bfloat16).reshape(token_count, KVH, HD)
    values = (
        (projected[:, KVH * HD :] + value_bias).astype(jnp.bfloat16).reshape(token_count, KVH, HD)
    )
    ends = jnp.cumsum(doc_lengths[0])
    reach = group_size // 4
    first = lax.axis_index("sp") * token_count
    key_parts = [keys]
    value_parts = [values]
    for back in range(1, reach + 1):
        key_far, value_far = from_behind((keys, values), "sp", back)
        key_parts.insert(0, key_far)
        value_parts.insert(0, value_far)
    key_all = jnp.concatenate(key_parts, axis=0)
    value_all = jnp.concatenate(value_parts, axis=0)
    query_pos = first + jnp.arange(token_count, dtype=jnp.int32)
    key_pos = first - reach * token_count + jnp.arange(key_all.shape[0], dtype=jnp.int32)
    query_ids = jnp.sum((query_pos[:, None] >= ends[None, :]).astype(jnp.int32), axis=1)
    key_ids = jnp.sum((key_pos[:, None] >= ends[None, :]).astype(jnp.int32), axis=1)
    result = attend_near(query_rows, key_all, value_all, query_pos, key_pos, query_ids, key_ids)
    return result.reshape(1, token_count, QH * HD)


def solution(mesh):
    in_specs = (
        P("fsdp", "sp", None),
        P("fsdp", "sp", None),
        P(),
        P("fsdp", None),
        P(),
        P("fsdp", None),
    )
    out_specs = P("fsdp", "sp", None)
    return jax.shard_map(shards, mesh=mesh, in_specs=in_specs, out_specs=out_specs, check_vma=False)
```

profile of v0, /device:TPU:8, one launch (start us, length us, event | category | flops | bytes accessed | tf_op | source)
XLA Modules:
  0.0 270.5 jit_solution(13247042923140272168)
XLA Ops:
  6.5 0.0 copy-start
  6.5 0.0 all-gather.2.cloned.1.call-start
  6.5 0.7 all-gather.2.cloned.1.call-update
  7.3 0.0 copy-start.6
  7.3 1.0 copy-done
  8.3 0.6 fusion.41
  8.9 0.0 copy-start.4
  8.9 132.8 %all-gather.2.cloned.1.call-done = bf16[5120,2048]{1,0:T(8,128)(2,1)} async-done(((bf16[1280,2048]{1,0:T(8,128)(2,1)}), bf16[5120,2048]{1,0:T(8,128)(2,1)}) %all-gather.2.cloned.1.call-update) | async-done | bytes 20971536 | tf_op jit(solution)/shard_map/all_gather | solution.py:60
  141.7 0.0 copy-done.6
  141.7 9.9 %fusion.44 = f32[256,2048]{1,0:T(8,128)S(1)} fusion(bf16[5120,2048]{1,0:T(8,128)(2,1)} %all-gather.2.cloned.1.call-done, bf16[1,256,5120]{2,1,0:T(8,128)(2,1)S(1)} %copy-done, f32[5120]{0:T(1024)S(1)} %copy-done.6, f32[256]{0:T(256)S(1)} %add_rsqrt_fusion), kind=kOutput, calls=%fused_computation.36 | convolution fusion | flops 5373952000 | bytes 25711616 | tf_op jit(solution)/shard_map/dot_general | solution.py:58
  151.6 0.0 copy-start.5
  151.7 0.0 copy-start.1
  151.7 0.1 copy_bitcast_fusion
  151.7 3.5 %collective-permute-start.2 = (bf16[256,8,128]{2,0,1:T(8,128)(2,1)S(1)}, bf16[256,8,128]{2,0,1:T(8,128)(2,1)}, u32[]{:S(2)}, u32[]{:S(2)}) collective-permute-start(bf16[256,8,128]{2,0,1:T(8,128)(2,1)S(1)} %copy_bitcast_fusion), channel_id=1, source_target_pairs={{0,2},{1,3},{2,4},{3,5},{4,6},{5,7},{8,10},{9,11},{10,12},{11,13},... | collective-permute-start | bytes 1572872 | tf_op jit(solution)/shard_map/ppermute | solution.py:17
  155.3 3.4 %collective-permute-start.3 = (bf16[256,8,128]{2,0,1:T(8,128)(2,1)S(1)}, bf16[256,8,128]{2,0,1:T(8,128)(2,1)}, u32[]{:S(2)}, u32[]{:S(2)}) collective-permute-start(bf16[256,8,128]{2,0,1:T(8,128)(2,1)S(1)} %copy_bitcast_fusion), channel_id=1, source_target_pairs={{0,1},{1,2},{2,3},{3,4},{4,5},{5,6},{6,7},{8,9},{9,10},{10,11},{11... | collective-permute-start | bytes 1572872 | tf_op jit(solution)/shard_map/ppermute | solution.py:17
  158.7 0.0 copy-done.4
  158.7 0.1 fusion.49
  158.8 1.0 copy.40
  159.8 3.4 %collective-permute-start = (bf16[256,8,128]{0,2,1:T(8,128)(2,1)}, bf16[256,8,128]{0,2,1:T(8,128)(2,1)S(1)}, u32[]{:S(2)}, u32[]{:S(2)}) collective-permute-start(bf16[256,8,128]{0,2,1:T(8,128)(2,1)} %bitcast.84), channel_id=1, source_target_pairs={{0,2},{1,3},{2,4},{3,5},{4,6},{5,7},{8,10},{9,11},{10,12},{11,13},... | collective-permute-start | bytes 1572872 | tf_op jit(solution)/shard_map/ppermute | solution.py:17
  163.2 1.9 collective-permute-start.1
  165.1 0.0 copy-done.5
  165.2 0.1 copy.35
  165.3 0.1 reduce
  165.4 0.0 copy-done.1
  165.4 2.5 copy.34
  167.9 0.0 copy-start.3
  167.9 0.1 convert_reduce_fusion.1
  168.0 0.1 convert_reduce_fusion
  168.1 0.0 copy-start.2
  168.1 0.6 collective-permute-done.2
  168.7 12.1 %collective-permute-done.3 = bf16[256,8,128]{2,0,1:T(8,128)(2,1)} collective-permute-done((bf16[256,8,128]{2,0,1:T(8,128)(2,1)S(1)}, bf16[256,8,128]{2,0,1:T(8,128)(2,1)}, u32[]{:S(2)}, u32[]{:S(2)}) %collective-permute-start.3) | collective-permute-done | bytes 524320 | tf_op jit(solution)/shard_map/ppermute | solution.py:17
  180.8 2.5 maximum_bitcast_fusion.1
  183.3 0.0 collective-permute-done
  183.3 19.2 %collective-permute-done.1 = bf16[256,8,128]{0,2,1:T(8,128)(2,1)} collective-permute-done((bf16[256,8,128]{0,2,1:T(8,128)(2,1)}, bf16[256,8,128]{0,2,1:T(8,128)(2,1)}, u32[]{:S(2)}, u32[]{:S(2)}) %collective-permute-start.1) | collective-permute-done | bytes 524320 | tf_op jit(solution)/shard_map/ppermute | solution.py:17
  202.6 0.0 copy-done.3
  202.6 2.3 maximum_bitcast_fusion
  204.9 0.0 copy-done.2
  204.9 55.9 %while.11 = (s32[]{:T(128)}, bf16[8,256,4,128]{1,3,2,0:T(8,128)(2,1)S(1)}, bf16[8,768,128]{1,2,0:T(8,128)(2,1)}, bf16[8,768,128]{2,1,0:T(8,128)(2,1)}, bf16[8,25...) while((s32[]{:T(128)}, ...), condition=%wide.region_7.8_spmd.clone, body=%wide.region_4.7_spmd.clone.sunk | while | flops 408290048 | bytes 7621485 | solution.py:46
  204.9 0.7 compare_and_fusion.2
  205.6 3.9 %fusion.70 = (f32[4,256]{1,0:T(4,128)S(1)}, f32[4,256,768]{1,2,0:T(8,128)}) fusion(pred[256,768]{0,1:T(8,128)(4,1)S(1)} %compare_and_fusion.2, bf16[8,256,4,128]{1,3,2,0:T(8,128)(2,1)} %get-tuple-element.198, s32[]{:T(128)} %get-tuple-element.183, bf16[8,768,128]{2,1,0:T(8,128)(2,1)} %get-tuple-element.197), kind=kOutput, calls=%fused_computation.53.clone.1 | convolution fusion | flops 204473088 | bytes 3806208 | tf_op jit(solution)/shard_map/while/body/eval_jaxpr/sub | solution.py:41
  209.4 2.4 fusion.71
  211.8 0.7 compare_and_fusion.2
  212.6 3.9 %fusion.70 = (f32[4,256]{1,0:T(4,128)S(1)}, f32[4,256,768]{1,2,0:T(8,128)}) fusion(pred[256,768]{0,1:T(8,128)(4,1)S(1)} %compare_and_fusion.2, bf16[8,256,4,128]{1,3,2,0:T(8,128)(2,1)} %get-tuple-element.198, s32[]{:T(128)} %get-tuple-element.183, bf16[8,768,128]{2,1,0:T(8,128)(2,1)} %get-tuple-element.197), kind=kOutput, calls=%fused_computation.53.clone.1 | convolution fusion | flops 204473088 | bytes 3806208 | tf_op jit(solution)/shard_map/while/body/eval_jaxpr/sub | solution.py:41
  216.4 2.4 fusion.71
  218.8 0.7 compare_and_fusion.2
  219.6 3.9 %fusion.70 = (f32[4,256]{1,0:T(4,128)S(1)}, f32[4,256,768]{1,2,0:T(8,128)}) fusion(pred[256,768]{0,1:T(8,128)(4,1)S(1)} %compare_and_fusion.2, bf16[8,256,4,128]{1,3,2,0:T(8,128)(2,1)} %get-tuple-element.198, s32[]{:T(128)} %get-tuple-element.183, bf16[8,768,128]{2,1,0:T(8,128)(2,1)} %get-tuple-element.197), kind=kOutput, calls=%fused_computation.53.clone.1 | convolution fusion | flops 204473088 | bytes 3806208 | tf_op jit(solution)/shard_map/while/body/eval_jaxpr/sub | solution.py:41
  223.4 2.4 fusion.71
  225.8 0.7 compare_and_fusion.2
  226.6 3.9 %fusion.70 = (f32[4,256]{1,0:T(4,128)S(1)}, f32[4,256,768]{1,2,0:T(8,128)}) fusion(pred[256,768]{0,1:T(8,128)(4,1)S(1)} %compare_and_fusion.2, bf16[8,256,4,128]{1,3,2,0:T(8,128)(2,1)} %get-tuple-element.198, s32[]{:T(128)} %get-tuple-element.183, bf16[8,768,128]{2,1,0:T(8,128)(2,1)} %get-tuple-element.197), kind=kOutput, calls=%fused_computation.53.clone.1 | convolution fusion | flops 204473088 | bytes 3806208 | tf_op jit(solution)/shard_map/while/body/eval_jaxpr/sub | solution.py:41
  230.4 2.4 fusion.71
  232.8 0.7 compare_and_fusion.2
  233.6 3.9 %fusion.70 = (f32[4,256]{1,0:T(4,128)S(1)}, f32[4,256,768]{1,2,0:T(8,128)}) fusion(pred[256,768]{0,1:T(8,128)(4,1)S(1)} %compare_and_fusion.2, bf16[8,256,4,128]{1,3,2,0:T(8,128)(2,1)} %get-tuple-element.198, s32[]{:T(128)} %get-tuple-element.183, bf16[8,768,128]{2,1,0:T(8,128)(2,1)} %get-tuple-element.197), kind=kOutput, calls=%fused_computation.53.clone.1 | convolution fusion | flops 204473088 | bytes 3806208 | tf_op jit(solution)/shard_map/while/body/eval_jaxpr/sub | solution.py:41
  237.4 2.4 fusion.71
  239.8 0.7 compare_and_fusion.2
  240.6 3.9 %fusion.70 = (f32[4,256]{1,0:T(4,128)S(1)}, f32[4,256,768]{1,2,0:T(8,128)}) fusion(pred[256,768]{0,1:T(8,128)(4,1)S(1)} %compare_and_fusion.2, bf16[8,256,4,128]{1,3,2,0:T(8,128)(2,1)} %get-tuple-element.198, s32[]{:T(128)} %get-tuple-element.183, bf16[8,768,128]{2,1,0:T(8,128)(2,1)} %get-tuple-element.197), kind=kOutput, calls=%fused_computation.53.clone.1 | convolution fusion | flops 204473088 | bytes 3806208 | tf_op jit(solution)/shard_map/while/body/eval_jaxpr/sub | solution.py:41
  244.4 2.4 fusion.71
  246.8 0.7 compare_and_fusion.2
  247.6 3.9 %fusion.70 = (f32[4,256]{1,0:T(4,128)S(1)}, f32[4,256,768]{1,2,0:T(8,128)}) fusion(pred[256,768]{0,1:T(8,128)(4,1)S(1)} %compare_and_fusion.2, bf16[8,256,4,128]{1,3,2,0:T(8,128)(2,1)} %get-tuple-element.198, s32[]{:T(128)} %get-tuple-element.183, bf16[8,768,128]{2,1,0:T(8,128)(2,1)} %get-tuple-element.197), kind=kOutput, calls=%fused_computation.53.clone.1 | convolution fusion | flops 204473088 | bytes 3806208 | tf_op jit(solution)/shard_map/while/body/eval_jaxpr/sub | solution.py:41
  251.4 2.4 fusion.71
  253.8 0.7 compare_and_fusion.2
  254.6 3.9 %fusion.70 = (f32[4,256]{1,0:T(4,128)S(1)}, f32[4,256,768]{1,2,0:T(8,128)}) fusion(pred[256,768]{0,1:T(8,128)(4,1)S(1)} %compare_and_fusion.2, bf16[8,256,4,128]{1,3,2,0:T(8,128)(2,1)} %get-tuple-element.198, s32[]{:T(128)} %get-tuple-element.183, bf16[8,768,128]{2,1,0:T(8,128)(2,1)} %get-tuple-element.197), kind=kOutput, calls=%fused_computation.53.clone.1 | convolution fusion | flops 204473088 | bytes 3806208 | tf_op jit(solution)/shard_map/while/body/eval_jaxpr/sub | solution.py:41
  258.4 2.4 fusion.71
  260.8 2.9 %copy.39 = bf16[1,256,4096]{2,1,0:T(8,128)(2,1)} copy(bf16[1,256,4096]{1,2,0:T(8,128)(2,1)S(1)} %bitcast.83) | data formatting | bytes 4194304 | tf_op jit(solution)/shard_map/reshape;reshape | solution.py:83
  (6 shorter events, 0.1 us)
Async XLA Ops:
  6.5 1.7 copy-start
  6.5 135.1 %all-gather.2.cloned.1.call-start = ((), (), s32[]{:S(2)}) async-start(), calls=%async_computation | async-start | bytes 26214400 | tf_op jit(solution)/shard_map/all_gather | solution.py:60
  7.3 134.4 %copy-start.6 = (f32[5120]{0:T(1024)S(1)}, f32[5120]{0:T(1024)}, u32[]{:S(2)}) copy-start(f32[5120]{0:T(1024)} %param.10) | copy-start | bytes 61444
  8.9 149.8 %copy-start.4 = (f32[1024]{0:T(1024)S(1)}, f32[1024]{0:T(1024)}, u32[]{:S(2)}) copy-start(f32[1024]{0:T(1024)} %param.12) | copy-start | bytes 12292
  151.6 13.5 %copy-start.5 = (s32[1,16]{1,0:T(1,128)S(1)}, s32[1,16]{1,0:T(1,128)}, u32[]{:S(2)}) copy-start(s32[1,16]{1,0:T(1,128)} %param.13) | copy-start | bytes 196
  151.7 13.7 %copy-start.1 = (bf16[1,256,4096]{2,1,0:T(8,128)(2,1)S(1)}, bf16[1,256,4096]{2,1,0:T(8,128)(2,1)}, u32[]{:S(2)}) copy-start(bf16[1,256,4096]{2,1,0:T(8,128)(2,1)} %param.9) | copy-start | bytes 6291460
  151.7 16.9 %collective-permute-start.2 = (bf16[256,8,128]{2,0,1:T(8,128)(2,1)S(1)}, bf16[256,8,128]{2,0,1:T(8,128)(2,1)}, u32[]{:S(2)}, u32[]{:S(2)}) collective-permute-start(bf16[256,8,128]{2,0,1:T(8,128)(2,1)S(1)} %copy_bitcast_fusion), channel_id=1, source_target_pairs={{0,2},{1,3},{2,4},{3,5},{4,6},{5,7},{8,10},{9,11},{10,12},{11,13},... | collective-permute-start | bytes 1572872 | tf_op jit(solution)/shard_map/ppermute | solution.py:17
  155.3 25.5 %collective-permute-start.3 = (bf16[256,8,128]{2,0,1:T(8,128)(2,1)S(1)}, bf16[256,8,128]{2,0,1:T(8,128)(2,1)}, u32[]{:S(2)}, u32[]{:S(2)}) collective-permute-start(bf16[256,8,128]{2,0,1:T(8,128)(2,1)S(1)} %copy_bitcast_fusion), channel_id=1, source_target_pairs={{0,1},{1,2},{2,3},{3,4},{4,5},{5,6},{6,7},{8,9},{9,10},{10,11},{11... | collective-permute-start | bytes 1572872 | tf_op jit(solution)/shard_map/ppermute | solution.py:17
  159.8 23.5 %collective-permute-start = (bf16[256,8,128]{0,2,1:T(8,128)(2,1)}, bf16[256,8,128]{0,2,1:T(8,128)(2,1)S(1)}, u32[]{:S(2)}, u32[]{:S(2)}) collective-permute-start(bf16[256,8,128]{0,2,1:T(8,128)(2,1)} %bitcast.84), channel_id=1, source_target_pairs={{0,2},{1,3},{2,4},{3,5},{4,6},{5,7},{8,10},{9,11},{10,12},{11,13},... | collective-permute-start | bytes 1572872 | tf_op jit(solution)/shard_map/ppermute | solution.py:17
  163.2 39.4 %collective-permute-start.1 = (bf16[256,8,128]{0,2,1:T(8,128)(2,1)}, bf16[256,8,128]{0,2,1:T(8,128)(2,1)}, u32[]{:S(2)}, u32[]{:S(2)}) collective-permute-start(bf16[256,8,128]{0,2,1:T(8,128)(2,1)} %bitcast.85), channel_id=1, source_target_pairs={{0,1},{1,2},{2,3},{3,4},{4,5},{5,6},{6,7},{8,9},{9,10},{10,11},{11... | collective-permute-start | bytes 1572872 | tf_op jit(solution)/shard_map/ppermute | solution.py:17
  167.9 34.7 %copy-start.3 = (bf16[256,1024]{0,1:T(8,128)(2,1)S(1)}, bf16[256,1024]{0,1:T(8,128)(2,1)}, u32[]{:S(2)}) copy-start(bf16[256,1024]{0,1:T(8,128)(2,1)} %copy.40) | copy-start | bytes 1572868
  168.1 36.8 %copy-start.2 = (bf16[8,256,4,128]{1,3,2,0:T(8,128)(2,1)S(1)}, bf16[8,256,4,128]{1,3,2,0:T(8,128)(2,1)}, u32[]{:S(2)}) copy-start(bf16[8,256,4,128]{1,3,2,0:T(8,128)(2,1)} %custom-call) | copy-start | bytes 6291460
Sparse Core Ops, SparseCore 0:
  8.9 132.7 all-gather.1
where the time goes:
time: 271 us
  waiting for transfers between devices  165 us (61%)
  matrix products  59.9 us (22%)
  between operations  13.5 us (5%)
  starting transfers between devices  12.2 us (5%)
  other arithmetic  11.6 us (4%)
  local copies, waits for them, and re-layouts  7.56 us (3%)
    all_gather x1, waiting for transfers between devices, shards(): lax.all_gather(kv_weight, 'fsdp', axis=0, tiled=True)  133 us
    ppermute x4, waiting for transfers between devices, from_behind(): return lax.ppermute(value, axis, pairs)  32 us
    sub x8, matrix products, one_group(): probs = jnp.exp(scores - highest)  30.8 us
    dot_general x8, matrix products, one_group(): jnp.einsum('rqk,kd->qrd', probs, value_one, preferred_element_type=jnp.fl...  19.1 us
    ppermute x4, starting transfers between devices, from_behind(): return lax.ppermute(value, axis, pairs)  12.2 us
    dot_general x1, matrix products, shards(): jnp.dot(normed, lax.all_gather(kv_weight, 'fsdp', axis=0, tiled=True), pr...  9.95 us
    and x8, other arithmetic, attend_near(): (key_pos[None, :] >= 0) & (key_pos[None, :] <= query_pos[:, None])  5.76 us
  transfers between devices with their start and end apart: 5, of which 4 were waited for; matrix products, arithmetic and copies ran while one was open for 3% of the time, Pallas kernels for 0%

commit v1 on v0

v1 whole, which is shorter than its diff:
```python
import functools

import jax
import jax.numpy as jnp
from jax import lax
from jax.experimental import pallas as pl
from jax.experimental.pallas import tpu as pltpu
from jax.sharding import PartitionSpec as P

QH = 32
KVH = 8
HD = 128
EPS = 1e-06
RATIO = QH // KVH
LOG2E = 1.4426950408889634
CHUNKS = 4
TILE = 128
HIDDEN = -1e30


def project_kernel(rows_ref, own_ref, other_ref, out_ref):
    depth = own_ref.shape[0]
    total = jnp.dot(rows_ref[:, :depth], own_ref[...], preferred_element_type=jnp.float32)
    total += jnp.dot(rows_ref[:, depth:], other_ref[...], preferred_element_type=jnp.float32)
    out_ref[...] = total.astype(out_ref.dtype)


def project(rows, weight_own, weight_other, chunk, heads, dtype):
    tokens, depth = rows.shape
    width = heads * HD
    chunks = KVH // heads
    held = weight_own.shape[0]
    spec = pl.BlockSpec((held, width), lambda i: (0, i * chunks + chunk))
    return pl.pallas_call(
        project_kernel,
        grid=(2,),
        in_specs=[pl.BlockSpec((tokens, depth), lambda i: (0, 0)), spec, spec],
        out_specs=pl.BlockSpec((tokens, width), lambda i: (0, i)),
        out_shape=jax.ShapeDtypeStruct((tokens, 2 * width), dtype),
        cost_estimate=pl.CostEstimate(
            flops=4 * tokens * depth * width,
            bytes_accessed=4 * depth * width + 2 * tokens * depth,
            transcendentals=0,
        ),
        name="project",
    )(rows, weight_own, weight_other)


def attend_kernel(reach, first_out, lengths_ref, query_ref, *refs):
    blocks = reach + 1
    keys, values = refs[:blocks], refs[blocks : 2 * blocks]
    out_ref, bias = refs[-2], refs[-1]
    tokens = query_ref.shape[0]
    window = blocks * tokens
    first = lax.axis_index("sp") * tokens

    @pl.when(pl.program_id(0) == 0)
    def _():
        query_pos = first + lax.broadcasted_iota(jnp.int32, (tokens, TILE), 0)
        start = jnp.zeros((tokens, TILE), jnp.int32)
        end = jnp.int32(0)
        for i in range(lengths_ref.shape[1]):
            end = end + lengths_ref[0, i]
            start = jnp.where(query_pos >= end, end, start)
        for j in range(0, window, TILE):
            key_pos = (
                first - reach * tokens + j + lax.broadcasted_iota(jnp.int32, (tokens, TILE), 1)
            )
            allowed = (key_pos >= start) & (key_pos <= query_pos)
            bias[:, j : j + TILE] = jnp.where(allowed, 0.0, HIDDEN).astype(jnp.float32)

    scale = HD ** (-0.5) * LOG2E
    for t in range(0, tokens, TILE):
        low, high = t, t + reach * tokens + TILE
        queries = jnp.concatenate(
            [query_ref[t : t + TILE, h * HD : (h + 1) * HD] for h in range(RATIO)], axis=0
        )
        spans = []
        for b in range(blocks):
            a, z = max(low - b * tokens, 0), min(high - b * tokens, tokens)
            if a < z:
                spans.append((b, a, z))
        scores = jnp.concatenate(
            [
                lax.dot_general(
                    queries,
                    keys[b][a:z, :],
                    (((1,), (1,)), ((), ())),
                    preferred_element_type=jnp.float32,
                )
                for b, a, z in spans
            ],
            axis=1,
        )
        mask = bias[t : t + TILE, low:high]
        scores = scores * scale + jnp.concatenate([mask] * RATIO, axis=0)
        highest = jnp.max(scores, axis=1, keepdims=True)
        probs = jnp.exp2(scores - highest).astype(jnp.bfloat16)
        total = jnp.zeros((RATIO * TILE, 2 * HD), jnp.float32)
        for b, a, z in spans:
            at = b * tokens + a - low
            value = jnp.concatenate(
                [values[b][a:z, :], jnp.ones((z - a, HD), jnp.bfloat16)], axis=1
            )
            total += jnp.dot(
                probs[:, at : at + z - a], value, preferred_element_type=jnp.float32
            )
        result = (total[:, :HD] / total[:, HD:]).astype(out_ref.dtype)
        for h in range(RATIO):
            out_ref[t : t + TILE, h * HD : (h + 1) * HD] = result[h * TILE : (h + 1) * TILE]


def attend(lengths, queries, blocks, chunk, heads, partial):
    tokens = queries.shape[0]
    reach = len(blocks) - 1
    in_specs = [
        pl.BlockSpec(memory_space=pltpu.SMEM),
        pl.BlockSpec((tokens, RATIO * HD), lambda i: (0, chunk * heads + i)),
    ]
    in_specs += [pl.BlockSpec((tokens, HD), lambda i: (0, i))] * len(blocks)
    in_specs += [pl.BlockSpec((tokens, HD), lambda i: (0, heads + i))] * len(blocks)
    operands = [lengths, queries, *blocks, *blocks]
    aliases = {}
    if partial is not None:
        aliases = {len(operands): 0}
        operands.append(partial)
        in_specs.append(pl.BlockSpec(memory_space=pl.ANY))
    keys = tokens * (reach + 1)
    return pl.pallas_call(
        functools.partial(attend_kernel, reach, partial is None),
        grid=(heads,),
        in_specs=in_specs,
        out_specs=pl.BlockSpec((tokens, RATIO * HD), lambda i: (0, chunk * heads + i)),
        out_shape=jax.ShapeDtypeStruct((tokens, QH * HD), jnp.bfloat16),
        scratch_shapes=[pltpu.VMEM((tokens, keys), jnp.float32)],
        input_output_aliases=aliases,
        cost_estimate=pl.CostEstimate(
            flops=6 * heads * RATIO * tokens * keys * HD,
            bytes_accessed=4 * tokens * heads * (RATIO + reach + 1) * HD,
            transcendentals=heads * RATIO * tokens * keys,
        ),
        name="attend",
    )(*operands)


def shards(hidden, queries, norm_gain, kv_weight, value_bias, doc_lengths):
    tokens = hidden.shape[1]
    parts = lax.axis_size("fsdp")
    length = lax.axis_size("sp")
    held = kv_weight.shape[0]
    pair = 2 if parts % 2 == 0 else 1
    groups = parts // pair
    me = lax.axis_index("fsdp")
    place = lax.axis_index("sp")
    group, core = me // pair, me % pair
    reach = length // 4
    heads = KVH // CHUNKS
    width = heads * HD

    wide = hidden[0].astype(jnp.float32)
    power = lax.rsqrt(jnp.mean(wide * wide, axis=-1, keepdims=True) + EPS)

    def normed(whose):
        def part(quarter):
            rows = lax.dynamic_slice_in_dim(hidden[0], quarter * held, held, 1)
            gain = lax.dynamic_slice_in_dim(norm_gain, quarter * held, held, 0)
            return (rows.astype(jnp.float32) * power * gain).astype(jnp.bfloat16)

        quarters = [whose * pair + core, whose * pair + (pair - 1 - core)]
        return jnp.concatenate([part(q) for q in quarters[:pair]], axis=1)

    arrived = []
    for d in range(1, groups):
        there = [(i, (i + d * pair) % parts) for i in range(parts)]
        arrived.append(lax.ppermute(normed((group + d) % groups), "fsdp", there))
    if pair == 2:
        weight_other = lax.ppermute(kv_weight, "fsdp", [(i, i ^ 1) for i in range(parts)])
    else:
        weight_other = jnp.zeros_like(kv_weight)
    mine = normed(group)
    if pair == 1:
        mine = jnp.concatenate([mine, jnp.zeros_like(mine)], axis=1)
        arrived = [jnp.concatenate([a, jnp.zeros_like(a)], axis=1) for a in arrived]

    out = None
    for c in range(CHUNKS):
        total = project(mine, kv_weight, weight_other, c, heads, jnp.float32)
        for d in range(1, groups):
            back = [(i, (i - d * pair) % parts) for i in range(parts)]
            part = project(arrived[d - 1], kv_weight, weight_other, c, heads, jnp.bfloat16)
            total = total + lax.ppermute(part, "fsdp", back).astype(jnp.float32)
        bias = lax.dynamic_slice_in_dim(value_bias, c * width, width, 0)
        total = total + jnp.concatenate([jnp.zeros_like(bias), bias])
        own = total.astype(jnp.bfloat16)
        blocks = [own]
        if reach % 2 == 0 and length % 2 == 0:
            far = []
            for b in range(2, reach + 1, 2):
                far.append(lax.ppermute(own, "sp", [(i, i + b) for i in range(length - b)]))
            swap = [(i, i ^ 1) for i in range(length)]
            odd = place % 2 == 1
            chain = [own] + far
            near = [
                lax.ppermute(jnp.where(odd, chain[b + 1], chain[b]), "sp", swap)
                for b in range(reach // 2)
            ]
            for b in range(reach // 2):
                blocks = [far[b], near[b]] + blocks
        else:
            for b in range(1, reach + 1):
                blocks = [
                    lax.ppermute(own, "sp", [(i, i + b) for i in range(length - b)])
                ] + blocks
        out = attend(doc_lengths, queries[0], blocks, c, heads, out)
    return out.reshape(1, tokens, QH * HD)


def solution(mesh):
    in_specs = (
        P("fsdp", "sp", None),
        P("fsdp", "sp", None),
        P(),
        P("fsdp", None),
        P(),
        P("fsdp", None),
    )
    out_specs = P("fsdp", "sp", None)
    return jax.shard_map(shards, mesh=mesh, in_specs=in_specs, out_specs=out_specs, check_vma=False)
```

time: 271 us -> 121 us (0.45)
  waiting for transfers between devices: 165 us -> 38 us
  matrix products: 59.9 us -> 0 us
  Pallas kernels: 0 us -> 47.8 us
  between operations: 13.5 us -> 0.33 us
  starting transfers between devices: 12.2 us -> 22.9 us
  other arithmetic: 11.6 us -> 6.12 us
    all_gather x1 -> x0, waiting for transfers between devices: 133 us -> none  [shards(): lax.all_gather(kv_weight, 'fsdp', axis=0, tiled=True)]
    pallas_call x0 -> x12, Pallas kernels: none -> 47.8 us  [the longest x8 28 us: project(): pl.pallas_call(project_kernel, grid=(2,), in_specs=[pl.BlockSpec((tokens,...]
    sub x8 -> x0, matrix products: 30.8 us -> none  [one_group(): probs = jnp.exp(scores - highest)]
    dot_general x9 -> x0, matrix products: 29.1 us -> none  [the longest x8 19.1 us: one_group(): jnp.einsum('rqk,kd->qrd', probs, value_one, preferred_element_type=jnp.fl...]
    ppermute x4 -> x14, starting transfers between devices: 12.2 us -> 22.9 us  [the longest x4 11.1 us: shards(): far.append(lax.ppermute(own, 'sp', [(i, i + b) for i in range(length - b)]))]
    ppermute x4 -> x14, waiting for transfers between devices: 32 us -> 38 us  [the longest x1 28.7 us: shards(): arrived.append(lax.ppermute(normed((group + d) % groups), 'fsdp', there))]
    and x8 -> x0, other arithmetic: 5.76 us -> none  [attend_near(): (key_pos[None, :] >= 0) & (key_pos[None, :] <= query_pos[:, None])]
    transpose x2 -> x0, other arithmetic: 4.81 us -> none  [the longest x1 2.52 us: attend_near(): key_groups = jnp.transpose(key_all, (1, 0, 2))]
  transfers between devices with their start and end apart: 5 -> 14, of which waited for: 4 -> 4; matrix products, arithmetic and copies ran while one was open for 3% -> 6% of each run, Pallas kernels for 0% -> 33%
where the time goes in v1:
time: 121 us; the launch traced here: 120 us
  Pallas kernels  47.8 us (40%)
  waiting for transfers between devices  38 us (31%)
  starting transfers between devices  22.9 us (19%)
  other arithmetic  6.12 us (5%)
  local copies, waits for them, and re-layouts  4.9 us (4%)
    ppermute x1, waiting for transfers between devices, shards(): arrived.append(lax.ppermute(normed((group + d) % groups), 'fsdp', there))  28.7 us
    pallas_call x8, Pallas kernels, project(): pl.pallas_call(project_kernel, grid=(2,), in_specs=[pl.BlockSpec((tokens,...  28 us
    pallas_call x4, Pallas kernels, attend(): pl.pallas_call(functools.partial(attend_kernel, reach, partial is None),...  19.8 us
    ppermute x4, starting transfers between devices, shards(): far.append(lax.ppermute(own, 'sp', [(i, i + b) for i in range(length - b)]))  11.1 us
    ppermute x4, waiting for transfers between devices, shards(): far.append(lax.ppermute(own, 'sp', [(i, i + b) for i in range(length - b)]))  9.28 us
    ppermute x4, starting transfers between devices, shards(): lax.ppermute(jnp.where(odd, chain[b + 1], chain[b]), 'sp', swap)  6.22 us
    ppermute x4, starting transfers between devices, shards(): total = total + lax.ppermute(part, 'fsdp', back).astype(jnp.float32)  4.05 us
    unnamed x38, local copies, waits for them, and re-layouts  3.97 us
  transfers between devices with their start and end apart: 14, of which 4 were waited for; matrix products, arithmetic and copies ran while one was open for 6% of the time, Pallas kernels for 33%

profile of v1, /device:TPU:8, one launch (start us, length us, event | category | flops | bytes accessed | tf_op | source)
XLA Modules:
  0.0 120.0 jit_solution(9788342283522221955)
XLA Ops:
  0.0 0.0 collective-permute-start
  0.0 0.9 fusion.8
  0.9 0.0 copy-start.1
  0.9 2.5 %multiply_reduce_fusion = f32[256]{0:T(256)S(1)} fusion(bf16[1,256,5120]{2,1,0:T(8,128)(2,1)} %param.6), kind=kLoop, calls=%fused_computation | loop fusion | flops 3931904 | bytes 2622464 | tf_op jit(solution)/shard_map/reduce_sum | solution.py:161
  3.4 0.0 copy-done.1
  3.4 0.9 fusion.3
  4.3 0.0 copy-start.18
  4.3 1.1 pad_maximum_fusion.1
  5.5 1.5 %collective-permute-start.1 = (bf16[256,2560]{1,0:T(8,128)(2,1)}, bf16[256,2560]{1,0:T(8,128)(2,1)S(1)}, u32[]{:S(2)}, u32[]{:S(2)}) collective-permute-start(bf16[256,2560]{1,0:T(8,128)(2,1)} %pad_maximum_fusion.1), channel_id=1, source_target_pairs={{0,16},{8,24},{16,0},{24,8},{1,17},{9,25},{17,1},{25,9},{2,18},{10... | collective-permute-start | bytes 3932168 | tf_op jit(solution)/shard_map/ppermute | solution.py:175
  7.0 0.0 copy-done.18
  7.0 1.1 pad_maximum_fusion.rows_ref
  8.2 28.7 %collective-permute-done.1.rows_ref = bf16[256,2560]{1,0:T(8,128)(2,1)S(1)} collective-permute-done((bf16[256,2560]{1,0:T(8,128)(2,1)}, bf16[256,2560]{1,0:T(8,128)(2,1)S(1)}, u32[]{:S(2)}, u32[]{:S(2)}) %collective-permute-start.1) | collective-permute-done | bytes 1310752 | tf_op jit(solution)/shard_map/ppermute | solution.py:175
  36.9 0.0 collective-permute-done.other_ref
  36.9 1.1 copy-done
  37.9 3.4 %project.9 = bf16[256,512]{1,0:T(8,128)(2,1)} custom-call(bf16[256,2560]{1,0:T(8,128)(2,1)} %copy-done, bf16[1280,2048]{1,0:T(8,128)(2,1)} %own_ref.15, bf16[1280,2048]{1,0:T(8,128)(2,1)} %collective-permute-done.other_ref), custom_call_target="tpu_custom_call" | custom-call | flops 671088640 | bytes 3932160 | tf_op jit(solution)/shard_map/project/pallas_call | solution.py:34
  41.4 1.5 %collective-permute-start.2 = (bf16[256,512]{1,0:T(8,128)(2,1)}, bf16[256,512]{1,0:T(8,128)(2,1)S(1)}, u32[]{:S(2)}, u32[]{:S(2)}) collective-permute-start(bf16[256,512]{1,0:T(8,128)(2,1)} %project.9), channel_id=1, source_target_pairs={{0,16},{8,24},{16,0},{24,8},{1,17},{9,25},{17,1},{25,9},{2,18},{10... | collective-permute-start | bytes 786440 | tf_op jit(solution)/shard_map/ppermute | solution.py:191
  42.9 3.5 %project.11 = bf16[256,512]{1,0:T(8,128)(2,1)} custom-call(bf16[256,2560]{1,0:T(8,128)(2,1)} %copy-done, bf16[1280,2048]{1,0:T(8,128)(2,1)} %own_ref.15, bf16[1280,2048]{1,0:T(8,128)(2,1)} %collective-permute-done.other_ref), custom_call_target="tpu_custom_call" | custom-call | flops 671088640 | bytes 3932160 | tf_op jit(solution)/shard_map/project/pallas_call | solution.py:34
  46.4 0.5 collective-permute-start.5
  46.9 3.5 %project.15 = bf16[256,512]{1,0:T(8,128)(2,1)} custom-call(bf16[256,2560]{1,0:T(8,128)(2,1)} %copy-done, bf16[1280,2048]{1,0:T(8,128)(2,1)} %own_ref.15, bf16[1280,2048]{1,0:T(8,128)(2,1)} %collective-permute-done.other_ref), custom_call_target="tpu_custom_call" | custom-call | flops 671088640 | bytes 3932160 | tf_op jit(solution)/shard_map/project/pallas_call | solution.py:34
  50.3 1.5 %collective-permute-start.11 = (bf16[256,512]{1,0:T(8,128)(2,1)}, bf16[256,512]{1,0:T(8,128)(2,1)S(1)}, u32[]{:S(2)}, u32[]{:S(2)}) collective-permute-start(bf16[256,512]{1,0:T(8,128)(2,1)} %project.15), channel_id=1, source_target_pairs={{0,16},{8,24},{16,0},{24,8},{1,17},{9,25},{17,1},{25,9},{2,18},{10... | collective-permute-start | bytes 786440 | tf_op jit(solution)/shard_map/ppermute | solution.py:191
  51.8 3.5 %project.13 = bf16[256,512]{1,0:T(8,128)(2,1)} custom-call(bf16[256,2560]{1,0:T(8,128)(2,1)} %copy-done, bf16[1280,2048]{1,0:T(8,128)(2,1)} %own_ref.15, bf16[1280,2048]{1,0:T(8,128)(2,1)} %collective-permute-done.other_ref), custom_call_target="tpu_custom_call" | custom-call | flops 671088640 | bytes 3932160 | tf_op jit(solution)/shard_map/project/pallas_call | solution.py:34
  55.3 0.5 collective-permute-start.8
  55.8 3.5 %project.14 = f32[256,512]{1,0:T(8,128)} custom-call(bf16[256,2560]{1,0:T(8,128)(2,1)} %pad_maximum_fusion.rows_ref, bf16[1280,2048]{1,0:T(8,128)(2,1)} %own_ref.15, bf16[1280,2048]{1,0:T(8,128)(2,1)} %collective-permute-done.other_ref), custom_call_target="tpu_custom_call" | custom-call | flops 671088640 | bytes 3932160 | tf_op jit(solution)/shard_map/project/pallas_call | solution.py:34
  59.3 3.5 %project.12 = f32[256,512]{1,0:T(8,128)} custom-call(bf16[256,2560]{1,0:T(8,128)(2,1)} %pad_maximum_fusion.rows_ref, bf16[1280,2048]{1,0:T(8,128)(2,1)} %own_ref.15, bf16[1280,2048]{1,0:T(8,128)(2,1)} %collective-permute-done.other_ref), custom_call_target="tpu_custom_call" | custom-call | flops 671088640 | bytes 3932160 | tf_op jit(solution)/shard_map/project/pallas_call | solution.py:34
  62.8 3.5 %project.10 = f32[256,512]{1,0:T(8,128)} custom-call(bf16[256,2560]{1,0:T(8,128)(2,1)} %pad_maximum_fusion.rows_ref, bf16[1280,2048]{1,0:T(8,128)(2,1)} %own_ref.15, bf16[1280,2048]{1,0:T(8,128)(2,1)} %collective-permute-done.other_ref), custom_call_target="tpu_custom_call" | custom-call | flops 671088640 | bytes 3932160 | tf_op jit(solution)/shard_map/project/pallas_call | solution.py:34
  66.4 3.6 %project.8 = f32[256,512]{1,0:T(8,128)} custom-call(bf16[256,2560]{1,0:T(8,128)(2,1)} %pad_maximum_fusion.rows_ref, bf16[1280,2048]{1,0:T(8,128)(2,1)} %own_ref.15, bf16[1280,2048]{1,0:T(8,128)(2,1)} %collective-permute-done.other_ref), custom_call_target="tpu_custom_call" | custom-call | flops 671088640 | bytes 3932160 | tf_op jit(solution)/shard_map/project/pallas_call | solution.py:34
  70.0 0.0 collective-permute-done.11
  70.0 0.0 copy-done.13
  70.0 0.1 add_convert_fusion.refs_2_.refs_5_
  70.1 0.0 copy-start.2
  70.1 0.0 copy-start.10
  70.1 3.6 %collective-permute-start.12 = (bf16[256,512]{1,0:T(8,128)(2,1)S(1)}, bf16[256,512]{1,0:T(8,128)(2,1)S(1)}, u32[]{:S(2)}, u32[]{:S(2)}) collective-permute-start(bf16[256,512]{1,0:T(8,128)(2,1)S(1)} %add_convert_fusion.refs_2_.refs_5_), channel_id=1, source_target_pairs={{0,2},{1,3},{2,4},{3,5},{4,6},{5,7},{8,10},{9,11},{10,12},{11,13},... | collective-permute-start | bytes 786440 | tf_op jit(solution)/shard_map/ppermute | solution.py:199
  73.7 0.0 collective-permute-done.8
  73.7 0.1 add_convert_fusion.1.refs_2_.refs_5_
  73.8 3.5 %collective-permute-start.9 = (bf16[256,512]{1,0:T(8,128)(2,1)S(1)}, bf16[256,512]{1,0:T(8,128)(2,1)S(1)}, u32[]{:S(2)}, u32[]{:S(2)}) collective-permute-start(bf16[256,512]{1,0:T(8,128)(2,1)S(1)} %add_convert_fusion.1.refs_2_.refs_5_), channel_id=1, source_target_pairs={{0,2},{1,3},{2,4},{3,5},{4,6},{5,7},{8,10},{9,11},{10,12},{11,13},... | collective-permute-start | bytes 786440 | tf_op jit(solution)/shard_map/ppermute | solution.py:199
  77.3 0.0 collective-permute-done.5
  77.3 0.1 add_convert_fusion.2.refs_2_.refs_5_
  77.4 1.9 %collective-permute-start.6 = (bf16[256,512]{1,0:T(8,128)(2,1)S(1)}, bf16[256,512]{1,0:T(8,128)(2,1)S(1)}, u32[]{:S(2)}, u32[]{:S(2)}) collective-permute-start(bf16[256,512]{1,0:T(8,128)(2,1)S(1)} %add_convert_fusion.2.refs_2_.refs_5_), channel_id=1, source_target_pairs={{0,2},{1,3},{2,4},{3,5},{4,6},{5,7},{8,10},{9,11},{10,12},{11,13},... | collective-permute-start | bytes 786440 | tf_op jit(solution)/shard_map/ppermute | solution.py:199
  79.4 0.0 collective-permute-done.2
  79.4 0.0 copy-done.10
  79.4 0.1 add_convert_fusion.3.refs_2_.refs_5_
  79.5 2.1 %collective-permute-start.3 = (bf16[256,512]{1,0:T(8,128)(2,1)S(1)}, bf16[256,512]{1,0:T(8,128)(2,1)S(1)}, u32[]{:S(2)}, u32[]{:S(2)}) collective-permute-start(bf16[256,512]{1,0:T(8,128)(2,1)S(1)} %add_convert_fusion.3.refs_2_.refs_5_), channel_id=1, source_target_pairs={{0,2},{1,3},{2,4},{3,5},{4,6},{5,7},{8,10},{9,11},{10,12},{11,13},... | collective-permute-start | bytes 786440 | tf_op jit(solution)/shard_map/ppermute | solution.py:199
  81.6 0.0 collective-permute-done.12.refs_0_.refs_3_
  81.7 1.6 %collective-permute-start.13 = (bf16[256,512]{1,0:T(8,128)(2,1)S(1)}, bf16[256,512]{1,0:T(8,128)(2,1)S(1)}, u32[]{:S(2)}, u32[]{:S(2)}) collective-permute-start(bf16[256,512]{1,0:T(8,128)(2,1)S(1)} %broadcast_select_fusion), channel_id=1, source_target_pairs={{0,1},{1,0},{2,3},{3,2},{4,5},{5,4},{6,7},{7,6},{8,9},{9,8},{10,11... | collective-permute-start | bytes 786440 | tf_op jit(solution)/shard_map/ppermute | solution.py:204
  83.2 3.5 %collective-permute-done.9.refs_0_.refs_3_ = bf16[256,512]{1,0:T(8,128)(2,1)S(1)} collective-permute-done((bf16[256,512]{1,0:T(8,128)(2,1)S(1)}, bf16[256,512]{1,0:T(8,128)(2,1)S(1)}, u32[]{:S(2)}, u32[]{:S(2)}) %collective-permute-start.9) | collective-permute-done | bytes 262176 | tf_op jit(solution)/shard_map/ppermute | solution.py:199
  86.8 1.6 %collective-permute-start.10 = (bf16[256,512]{1,0:T(8,128)(2,1)S(1)}, bf16[256,512]{1,0:T(8,128)(2,1)S(1)}, u32[]{:S(2)}, u32[]{:S(2)}) collective-permute-start(bf16[256,512]{1,0:T(8,128)(2,1)S(1)} %broadcast_select_fusion.1), channel_id=1, source_target_pairs={{0,1},{1,0},{2,3},{3,2},{4,5},{5,4},{6,7},{7,6},{8,9},{9,8},{10,11... | collective-permute-start | bytes 786440 | tf_op jit(solution)/shard_map/ppermute | solution.py:204
  88.3 4.0 %collective-permute-done.6.refs_0_.refs_3_ = bf16[256,512]{1,0:T(8,128)(2,1)S(1)} collective-permute-done((bf16[256,512]{1,0:T(8,128)(2,1)S(1)}, bf16[256,512]{1,0:T(8,128)(2,1)S(1)}, u32[]{:S(2)}, u32[]{:S(2)}) %collective-permute-start.6) | collective-permute-done | bytes 262176 | tf_op jit(solution)/shard_map/ppermute | solution.py:199
  92.4 1.6 %collective-permute-start.7 = (bf16[256,512]{1,0:T(8,128)(2,1)S(1)}, bf16[256,512]{1,0:T(8,128)(2,1)S(1)}, u32[]{:S(2)}, u32[]{:S(2)}) collective-permute-start(bf16[256,512]{1,0:T(8,128)(2,1)S(1)} %broadcast_select_fusion.2), channel_id=1, source_target_pairs={{0,1},{1,0},{2,3},{3,2},{4,5},{5,4},{6,7},{7,6},{8,9},{9,8},{10,11... | collective-permute-start | bytes 786440 | tf_op jit(solution)/shard_map/ppermute | solution.py:204
  94.0 1.7 %collective-permute-done.3.refs_0_.refs_3_ = bf16[256,512]{1,0:T(8,128)(2,1)S(1)} collective-permute-done((bf16[256,512]{1,0:T(8,128)(2,1)S(1)}, bf16[256,512]{1,0:T(8,128)(2,1)S(1)}, u32[]{:S(2)}, u32[]{:S(2)}) %collective-permute-start.3) | collective-permute-done | bytes 262176 | tf_op jit(solution)/shard_map/ppermute | solution.py:199
  95.8 1.6 %collective-permute-start.4 = (bf16[256,512]{1,0:T(8,128)(2,1)S(1)}, bf16[256,512]{1,0:T(8,128)(2,1)S(1)}, u32[]{:S(2)}, u32[]{:S(2)}) collective-permute-start(bf16[256,512]{1,0:T(8,128)(2,1)S(1)} %broadcast_select_fusion.3), channel_id=1, source_target_pairs={{0,1},{1,0},{2,3},{3,2},{4,5},{5,4},{6,7},{7,6},{8,9},{9,8},{10,11... | collective-permute-start | bytes 786440 | tf_op jit(solution)/shard_map/ppermute | solution.py:204
  97.3 0.0 collective-permute-done.13.refs_1_.refs_4_
  97.3 0.7 copy-done.16
  98.0 4.9 %attend.4.refs_6_ = bf16[256,4096]{1,0:T(8,128)(2,1)} custom-call(s32[1,16]{1,0:T(1,128)} %lengths_ref.7, bf16[256,4096]{1,0:T(8,128)(2,1)} %bitcast.14, bf16[256,512]{1,0:T(8,128)(2,1)} %copy-done.6, bf16[256,512]{1,0:T(8,128)(2,1)} %copy-done.16, bf16[256,512]{1,0:T(8,128)(2,1)} %copy-done.2, bf16[256,512]{1,0:T(8,128)(2,1)} %copy-done.6, ...), custom_call_target="tpu_custom_call" | custom-call | flops 1207959552 | bytes 1835008 | tf_op jit(solution)/shard_map/attend/pallas_call | solution.py:129
  103.0 0.0 copy-done.8
  103.0 0.0 copy-done.9
  103.0 0.0 collective-permute-done.10.refs_1_.refs_4_
  103.0 0.7 copy-done.17
  103.7 4.9 %attend.5.refs_6_ = bf16[256,4096]{1,0:T(8,128)(2,1)} custom-call(s32[1,16]{1,0:T(1,128)} %lengths_ref.7, bf16[256,4096]{1,0:T(8,128)(2,1)} %bitcast.15, bf16[256,512]{1,0:T(8,128)(2,1)} %copy-done.7, bf16[256,512]{1,0:T(8,128)(2,1)} %copy-done.17, bf16[256,512]{1,0:T(8,128)(2,1)} %copy-done.3, ...), custom_call_target="tpu_custom_call", output_to_operand_aliasing={{}: (8, {})} | custom-call | flops 1207959552 | bytes 1835008 | tf_op jit(solution)/shard_map/attend/pallas_call | solution.py:129
  108.7 0.0 collective-permute-done.7.refs_1_.refs_4_
  108.7 0.7 copy-done.14
  109.4 5.0 %attend.6.refs_6_ = bf16[256,4096]{1,0:T(8,128)(2,1)} custom-call(s32[1,16]{1,0:T(1,128)} %lengths_ref.7, bf16[256,4096]{1,0:T(8,128)(2,1)} %bitcast.16, bf16[256,512]{1,0:T(8,128)(2,1)} %copy-done.8, bf16[256,512]{1,0:T(8,128)(2,1)} %copy-done.14, bf16[256,512]{1,0:T(8,128)(2,1)} %copy-done.4, ...), custom_call_target="tpu_custom_call", output_to_operand_aliasing={{}: (8, {})} | custom-call | flops 1207959552 | bytes 1835008 | tf_op jit(solution)/shard_map/attend/pallas_call | solution.py:129
  114.4 0.0 collective-permute-done.4.refs_1_.refs_4_
  114.4 0.7 copy-done.15
  115.1 5.0 %attend.7 = bf16[256,4096]{1,0:T(8,128)(2,1)} custom-call(s32[1,16]{1,0:T(1,128)} %lengths_ref.7, bf16[256,4096]{1,0:T(8,128)(2,1)} %bitcast.17, bf16[256,512]{1,0:T(8,128)(2,1)} %copy-done.9, bf16[256,512]{1,0:T(8,128)(2,1)} %copy-done.15, bf16[256,512]{1,0:T(8,128)(2,1)} %copy-done.5, bf16[256,512]{1,0:T(8,128)(2,1)} %copy-done.9, ...), custom_call_target="tpu_custom_call", output_to_operand_aliasing={{}: (8, {})} | custom-call | flops 1207959552 | bytes 1835008 | tf_op jit(solution)/shard_map/attend/pallas_call | solution.py:129
  (33 shorter events, 0.2 us)
Async XLA Ops:
  0.0 36.9 %collective-permute-start = (bf16[1280,2048]{1,0:T(8,128)(2,1)}, bf16[1280,2048]{1,0:T(8,128)(2,1)}, u32[]{:S(2)}, u32[]{:S(2)}) collective-permute-start(bf16[1280,2048]{1,0:T(8,128)(2,1)} %own_ref.15), channel_id=1, source_target_pairs={{0,8},{8,0},{16,24},{24,16},{1,9},{9,1},{17,25},{25,17},{2,10},{10... | collective-permute-start | bytes 15728648 | tf_op jit(solution)/shard_map/ppermute | solution.py:177
  0.9 2.5 %copy-start.1 = (bf16[1,256,5120]{2,1,0:T(8,128)(2,1)S(1)}, bf16[1,256,5120]{2,1,0:T(8,128)(2,1)}, u32[]{:S(2)}) copy-start(bf16[1,256,5120]{2,1,0:T(8,128)(2,1)} %param.6) | copy-start | bytes 7864324
  4.3 2.7 %copy-start.18 = (f32[1024]{0:T(1024)S(1)}, f32[1024]{0:T(1024)}, u32[]{:S(2)}) copy-start(f32[1024]{0:T(1024)} %param.10) | copy-start | bytes 12292
  5.5 31.4 %collective-permute-start.1 = (bf16[256,2560]{1,0:T(8,128)(2,1)}, bf16[256,2560]{1,0:T(8,128)(2,1)S(1)}, u32[]{:S(2)}, u32[]{:S(2)}) collective-permute-start(bf16[256,2560]{1,0:T(8,128)(2,1)} %pad_maximum_fusion.1), channel_id=1, source_target_pairs={{0,16},{8,24},{16,0},{24,8},{1,17},{9,25},{17,1},{25,9},{2,18},{10... | collective-permute-start | bytes 3932168 | tf_op jit(solution)/shard_map/ppermute | solution.py:175
  36.9 1.1 copy-start
  41.4 38.0 %collective-permute-start.2 = (bf16[256,512]{1,0:T(8,128)(2,1)}, bf16[256,512]{1,0:T(8,128)(2,1)S(1)}, u32[]{:S(2)}, u32[]{:S(2)}) collective-permute-start(bf16[256,512]{1,0:T(8,128)(2,1)} %project.9), channel_id=1, source_target_pairs={{0,16},{8,24},{16,0},{24,8},{1,17},{9,25},{17,1},{25,9},{2,18},{10... | collective-permute-start | bytes 786440 | tf_op jit(solution)/shard_map/ppermute | solution.py:191
  46.4 31.0 %collective-permute-start.5 = (bf16[256,512]{1,0:T(8,128)(2,1)}, bf16[256,512]{1,0:T(8,128)(2,1)S(1)}, u32[]{:S(2)}, u32[]{:S(2)}) collective-permute-start(bf16[256,512]{1,0:T(8,128)(2,1)} %project.11), channel_id=1, source_target_pairs={{0,16},{8,24},{16,0},{24,8},{1,17},{9,25},{17,1},{25,9},{2,18},{10... | collective-permute-start | bytes 786440 | tf_op jit(solution)/shard_map/ppermute | solution.py:191
  50.3 19.6 %collective-permute-start.11 = (bf16[256,512]{1,0:T(8,128)(2,1)}, bf16[256,512]{1,0:T(8,128)(2,1)S(1)}, u32[]{:S(2)}, u32[]{:S(2)}) collective-permute-start(bf16[256,512]{1,0:T(8,128)(2,1)} %project.15), channel_id=1, source_target_pairs={{0,16},{8,24},{16,0},{24,8},{1,17},{9,25},{17,1},{25,9},{2,18},{10... | collective-permute-start | bytes 786440 | tf_op jit(solution)/shard_map/ppermute | solution.py:191
  55.3 18.4 %collective-permute-start.8 = (bf16[256,512]{1,0:T(8,128)(2,1)}, bf16[256,512]{1,0:T(8,128)(2,1)S(1)}, u32[]{:S(2)}, u32[]{:S(2)}) collective-permute-start(bf16[256,512]{1,0:T(8,128)(2,1)} %project.13), channel_id=1, source_target_pairs={{0,16},{8,24},{16,0},{24,8},{1,17},{9,25},{17,1},{25,9},{2,18},{10... | collective-permute-start | bytes 786440 | tf_op jit(solution)/shard_map/ppermute | solution.py:191
  66.4 3.6 %copy-start.13 = (f32[256,512]{1,0:T(8,128)S(1)}, f32[256,512]{1,0:T(8,128)}, u32[]{:S(2)}) copy-start(f32[256,512]{1,0:T(8,128)} %project.14) | copy-start | bytes 1572868
  70.0 3.8 %copy-start.12 = (f32[256,512]{1,0:T(8,128)S(1)}, f32[256,512]{1,0:T(8,128)}, u32[]{:S(2)}) copy-start(f32[256,512]{1,0:T(8,128)} %project.12) | copy-start | bytes 1572868
  70.0 7.4 %copy-start.11 = (f32[256,512]{1,0:T(8,128)S(1)}, f32[256,512]{1,0:T(8,128)}, u32[]{:S(2)}) copy-start(f32[256,512]{1,0:T(8,128)} %project.10) | copy-start | bytes 1572868
  70.1 11.5 %copy-start.2 = (bf16[256,512]{1,0:T(8,128)(2,1)}, bf16[256,512]{1,0:T(8,128)(2,1)S(1)}, u32[]{:S(2)}) copy-start(bf16[256,512]{1,0:T(8,128)(2,1)S(1)} %add_convert_fusion.refs_2_.refs_5_) | copy-start | bytes 786436
  70.1 9.3 %copy-start.10 = (f32[256,512]{1,0:T(8,128)S(1)}, f32[256,512]{1,0:T(8,128)}, u32[]{:S(2)}) copy-start(f32[256,512]{1,0:T(8,128)} %project.8) | copy-start | bytes 1572868
  70.1 11.5 %collective-permute-start.12 = (bf16[256,512]{1,0:T(8,128)(2,1)S(1)}, bf16[256,512]{1,0:T(8,128)(2,1)S(1)}, u32[]{:S(2)}, u32[]{:S(2)}) collective-permute-start(bf16[256,512]{1,0:T(8,128)(2,1)S(1)} %add_convert_fusion.refs_2_.refs_5_), channel_id=1, source_target_pairs={{0,2},{1,3},{2,4},{3,5},{4,6},{5,7},{8,10},{9,11},{10,12},{11,13},... | collective-permute-start | bytes 786440 | tf_op jit(solution)/shard_map/ppermute | solution.py:199
  73.8 12.9 %copy-start.3 = (bf16[256,512]{1,0:T(8,128)(2,1)}, bf16[256,512]{1,0:T(8,128)(2,1)S(1)}, u32[]{:S(2)}) copy-start(bf16[256,512]{1,0:T(8,128)(2,1)S(1)} %add_convert_fusion.1.refs_2_.refs_5_) | copy-start | bytes 786436
  73.8 12.9 %collective-permute-start.9 = (bf16[256,512]{1,0:T(8,128)(2,1)S(1)}, bf16[256,512]{1,0:T(8,128)(2,1)S(1)}, u32[]{:S(2)}, u32[]{:S(2)}) collective-permute-start(bf16[256,512]{1,0:T(8,128)(2,1)S(1)} %add_convert_fusion.1.refs_2_.refs_5_), channel_id=1, source_target_pairs={{0,2},{1,3},{2,4},{3,5},{4,6},{5,7},{8,10},{9,11},{10,12},{11,13},... | collective-permute-start | bytes 786440 | tf_op jit(solution)/shard_map/ppermute | solution.py:199
  77.4 14.9 %copy-start.4 = (bf16[256,512]{1,0:T(8,128)(2,1)}, bf16[256,512]{1,0:T(8,128)(2,1)S(1)}, u32[]{:S(2)}) copy-start(bf16[256,512]{1,0:T(8,128)(2,1)S(1)} %add_convert_fusion.2.refs_2_.refs_5_) | copy-start | bytes 786436
  77.4 14.9 %collective-permute-start.6 = (bf16[256,512]{1,0:T(8,128)(2,1)S(1)}, bf16[256,512]{1,0:T(8,128)(2,1)S(1)}, u32[]{:S(2)}, u32[]{:S(2)}) collective-permute-start(bf16[256,512]{1,0:T(8,128)(2,1)S(1)} %add_convert_fusion.2.refs_2_.refs_5_), channel_id=1, source_target_pairs={{0,2},{1,3},{2,4},{3,5},{4,6},{5,7},{8,10},{9,11},{10,12},{11,13},... | collective-permute-start | bytes 786440 | tf_op jit(solution)/shard_map/ppermute | solution.py:199
  79.5 16.3 %copy-start.5 = (bf16[256,512]{1,0:T(8,128)(2,1)}, bf16[256,512]{1,0:T(8,128)(2,1)S(1)}, u32[]{:S(2)}) copy-start(bf16[256,512]{1,0:T(8,128)(2,1)S(1)} %add_convert_fusion.3.refs_2_.refs_5_) | copy-start | bytes 786436
  79.5 16.2 %collective-permute-start.3 = (bf16[256,512]{1,0:T(8,128)(2,1)S(1)}, bf16[256,512]{1,0:T(8,128)(2,1)S(1)}, u32[]{:S(2)}, u32[]{:S(2)}) collective-permute-start(bf16[256,512]{1,0:T(8,128)(2,1)S(1)} %add_convert_fusion.3.refs_2_.refs_5_), channel_id=1, source_target_pairs={{0,2},{1,3},{2,4},{3,5},{4,6},{5,7},{8,10},{9,11},{10,12},{11,13},... | collective-permute-start | bytes 786440 | tf_op jit(solution)/shard_map/ppermute | solution.py:199
  81.6 14.1 %copy-start.6 = (bf16[256,512]{1,0:T(8,128)(2,1)}, bf16[256,512]{1,0:T(8,128)(2,1)S(1)}, u32[]{:S(2)}) copy-start(bf16[256,512]{1,0:T(8,128)(2,1)S(1)} %collective-permute-done.12.refs_0_.refs_3_) | copy-start | bytes 786436
  81.7 15.7 %collective-permute-start.13 = (bf16[256,512]{1,0:T(8,128)(2,1)S(1)}, bf16[256,512]{1,0:T(8,128)(2,1)S(1)}, u32[]{:S(2)}, u32[]{:S(2)}) collective-permute-start(bf16[256,512]{1,0:T(8,128)(2,1)S(1)} %broadcast_select_fusion), channel_id=1, source_target_pairs={{0,1},{1,0},{2,3},{3,2},{4,5},{5,4},{6,7},{7,6},{8,9},{9,8},{10,11... | collective-permute-start | bytes 786440 | tf_op jit(solution)/shard_map/ppermute | solution.py:204
  86.7 16.2 %copy-start.7 = (bf16[256,512]{1,0:T(8,128)(2,1)}, bf16[256,512]{1,0:T(8,128)(2,1)S(1)}, u32[]{:S(2)}) copy-start(bf16[256,512]{1,0:T(8,128)(2,1)S(1)} %collective-permute-done.9.refs_0_.refs_3_) | copy-start | bytes 786436
  86.8 16.2 %collective-permute-start.10 = (bf16[256,512]{1,0:T(8,128)(2,1)S(1)}, bf16[256,512]{1,0:T(8,128)(2,1)S(1)}, u32[]{:S(2)}, u32[]{:S(2)}) collective-permute-start(bf16[256,512]{1,0:T(8,128)(2,1)S(1)} %broadcast_select_fusion.1), channel_id=1, source_target_pairs={{0,1},{1,0},{2,3},{3,2},{4,5},{5,4},{6,7},{7,6},{8,9},{9,8},{10,11... | collective-permute-start | bytes 786440 | tf_op jit(solution)/shard_map/ppermute | solution.py:204
  92.4 10.6 %copy-start.8 = (bf16[256,512]{1,0:T(8,128)(2,1)}, bf16[256,512]{1,0:T(8,128)(2,1)S(1)}, u32[]{:S(2)}) copy-start(bf16[256,512]{1,0:T(8,128)(2,1)S(1)} %collective-permute-done.6.refs_0_.refs_3_) | copy-start | bytes 786436
  92.4 16.3 %collective-permute-start.7 = (bf16[256,512]{1,0:T(8,128)(2,1)S(1)}, bf16[256,512]{1,0:T(8,128)(2,1)S(1)}, u32[]{:S(2)}, u32[]{:S(2)}) collective-permute-start(bf16[256,512]{1,0:T(8,128)(2,1)S(1)} %broadcast_select_fusion.2), channel_id=1, source_target_pairs={{0,1},{1,0},{2,3},{3,2},{4,5},{5,4},{6,7},{7,6},{8,9},{9,8},{10,11... | collective-permute-start | bytes 786440 | tf_op jit(solution)/shard_map/ppermute | solution.py:204
  95.7 7.3 %copy-start.9 = (bf16[256,512]{1,0:T(8,128)(2,1)}, bf16[256,512]{1,0:T(8,128)(2,1)S(1)}, u32[]{:S(2)}) copy-start(bf16[256,512]{1,0:T(8,128)(2,1)S(1)} %collective-permute-done.3.refs_0_.refs_3_) | copy-start | bytes 786436
  95.8 18.6 %collective-permute-start.4 = (bf16[256,512]{1,0:T(8,128)(2,1)S(1)}, bf16[256,512]{1,0:T(8,128)(2,1)S(1)}, u32[]{:S(2)}, u32[]{:S(2)}) collective-permute-start(bf16[256,512]{1,0:T(8,128)(2,1)S(1)} %broadcast_select_fusion.3), channel_id=1, source_target_pairs={{0,1},{1,0},{2,3},{3,2},{4,5},{5,4},{6,7},{7,6},{8,9},{9,8},{10,11... | collective-permute-start | bytes 786440 | tf_op jit(solution)/shard_map/ppermute | solution.py:204
  97.3 0.7 copy-start.16
  103.0 0.7 copy-start.17
  108.7 0.7 copy-start.14
  114.4 0.7 copy-start.15

commit v2 on v0

v2 whole, which is shorter than its diff:
```python
import functools

import jax
import jax.numpy as jnp
from jax import lax
from jax.experimental import pallas as pl
from jax.experimental.pallas import tpu as pltpu
from jax.sharding import PartitionSpec as P

QH = 32
KVH = 8
HD = 128
EPS = 1e-06
RATIO = QH // KVH
LOG2E = 1.4426950408889634
CHUNKS = 4
TILE = 128
HIDDEN = -1e30
MIB = 1 << 20
VMEM = pl.BlockSpec(memory_space=pltpu.VMEM)


def place_in(pair):
    me = lax.axis_index("fsdp")
    return lax.div(me, jnp.int32(pair)), lax.rem(me, jnp.int32(pair))


def scale_part(hidden_ref, gain_ref, out_ref, quarter, slot, held):
    columns = pl.ds(pl.multiple_of(quarter * held, HD), held)
    rows = hidden_ref[:, columns].astype(jnp.float32) * gain_ref[:, columns]
    out_ref[:, slot * held : (slot + 1) * held] = rows.astype(jnp.bfloat16)


def away_kernel(parts, pair, ahead, hidden_ref, gain_ref, out_ref):
    group, core = place_in(pair)
    there = lax.rem(group + ahead, jnp.int32(parts // pair)) * pair
    held = out_ref.shape[1] // pair
    scale_part(hidden_ref, gain_ref, out_ref, there + core, 0, held)
    if pair == 2:
        scale_part(hidden_ref, gain_ref, out_ref, there + 1 - core, 1, held)


def home_kernel(pair, hidden_ref, gain_ref, out_ref, power_ref):
    group, core = place_in(pair)
    held = out_ref.shape[1] // pair
    scale_part(hidden_ref, gain_ref, out_ref, group * pair + core, 0, held)
    if pair == 2:
        scale_part(hidden_ref, gain_ref, out_ref, group * pair + 1 - core, 1, held)
    tokens, model = hidden_ref.shape
    total = jnp.zeros((tokens, HD), jnp.float32)
    for j in range(0, model, HD):
        wide = hidden_ref[:, j : j + HD].astype(jnp.float32)
        total += wide * wide
    mean = jnp.sum(total, axis=1, keepdims=True) / model
    power_ref[...] = lax.rsqrt(mean + EPS)


def scaled(kernel, hidden, gain, width, powers):
    tokens = hidden.shape[0]
    out_shape = [jax.ShapeDtypeStruct((tokens, width), jnp.bfloat16)]
    if powers:
        out_shape.append(jax.ShapeDtypeStruct((tokens, 1), jnp.float32))
    return pl.pallas_call(
        kernel,
        in_specs=[VMEM, VMEM],
        out_specs=[VMEM] * len(out_shape),
        out_shape=out_shape,
        compiler_params=pltpu.CompilerParams(vmem_limit_bytes=16 * MIB),
        cost_estimate=pl.CostEstimate(
            flops=4 * tokens * width, bytes_accessed=4 * tokens * width, transcendentals=0
        ),
        name="scaled",
    )(hidden, gain)


def project_kernel(starts, width, rows_ref, *refs):
    weights, out_ref = refs[:-1], refs[-1]
    depth = weights[0].shape[0]
    for i, start in enumerate(starts):
        total = None
        for w, weight in enumerate(weights):
            term = jnp.dot(
                rows_ref[:, w * depth : (w + 1) * depth],
                weight[:, start : start + width],
                preferred_element_type=jnp.float32,
            )
            total = term if total is None else total + term
        out_ref[:, i * width : (i + 1) * width] = total.astype(out_ref.dtype)


def project(rows, weights, chunks, heads, dtype):
    tokens, depth = rows.shape
    width = heads * HD
    starts = [half * KVH * HD + c * width for c in chunks for half in range(2)]
    columns = len(starts) * width
    return pl.pallas_call(
        functools.partial(project_kernel, starts, width),
        in_specs=[VMEM] * (1 + len(weights)),
        out_specs=VMEM,
        out_shape=jax.ShapeDtypeStruct((tokens, columns), dtype),
        compiler_params=pltpu.CompilerParams(vmem_limit_bytes=24 * MIB),
        cost_estimate=pl.CostEstimate(
            flops=2 * tokens * depth * columns,
            bytes_accessed=2 * depth * columns,
            transcendentals=0,
        ),
        name="project",
    )(rows, *weights)


def merge_kernel(chunk, heads, home_ref, power_ref, bias_ref, *refs):
    parts, out_ref = refs[:-1], refs[-1]
    width = heads * HD
    total = home_ref[:, 2 * chunk * width : 2 * (chunk + 1) * width]
    for part in parts:
        total = total + part[...].astype(jnp.float32)
    total = total * power_ref[...]
    out_ref[:, :width] = total[:, :width].astype(jnp.bfloat16)
    bias = bias_ref[:, chunk * width : (chunk + 1) * width]
    out_ref[:, width:] = (total[:, width:] + bias).astype(jnp.bfloat16)


def merge(home, power, bias, parts, chunk, heads):
    tokens = home.shape[0]
    return pl.pallas_call(
        functools.partial(merge_kernel, chunk, heads),
        in_specs=[VMEM] * (3 + len(parts)),
        out_specs=VMEM,
        out_shape=jax.ShapeDtypeStruct((tokens, 2 * heads * HD), jnp.bfloat16),
        compiler_params=pltpu.CompilerParams(vmem_limit_bytes=4 * MIB),
        name="merge",
    )(home, power, bias, *parts)


def pick_kernel(even_ref, odd_ref, out_ref):
    odd = lax.rem(lax.axis_index("sp"), jnp.int32(2)) == 1

    @pl.when(odd)
    def _():
        out_ref[...] = odd_ref[...]

    @pl.when(jnp.logical_not(odd))
    def _():
        out_ref[...] = even_ref[...]


def pick(even, odd):
    return pl.pallas_call(
        pick_kernel,
        in_specs=[VMEM] * 2,
        out_specs=VMEM,
        out_shape=jax.ShapeDtypeStruct(even.shape, even.dtype),
        compiler_params=pltpu.CompilerParams(vmem_limit_bytes=4 * MIB),
        name="pick",
    )(even, odd)


def attend_kernel(reach, lengths_ref, query_ref, *refs):
    blocks = refs[: reach + 1]
    out_ref, bias = refs[-2], refs[-1]
    tokens = query_ref.shape[0]
    heads = blocks[0].shape[1] // (2 * HD)
    window = (reach + 1) * tokens
    first = lax.axis_index("sp") * tokens
    query_pos = first + lax.broadcasted_iota(jnp.int32, (tokens, TILE), 0)
    start = jnp.zeros((tokens, TILE), jnp.int32)
    end = jnp.int32(0)
    for i in range(lengths_ref.shape[1]):
        end = end + lengths_ref[0, i]
        start = jnp.where(query_pos >= end, end, start)
    for j in range(0, window, TILE):
        key_pos = first - reach * tokens + j + lax.broadcasted_iota(jnp.int32, (tokens, TILE), 1)
        allowed = (key_pos >= start) & (key_pos <= query_pos)
        bias[:, j : j + TILE] = jnp.where(allowed, 0.0, HIDDEN).astype(jnp.float32)

    scale = HD ** (-0.5) * LOG2E
    for head in range(heads):
        for t in range(0, tokens, TILE):
            low, high = t, t + reach * tokens + TILE
            wide = head * RATIO * HD
            queries = jnp.concatenate(
                [
                    query_ref[t : t + TILE, wide + h * HD : wide + (h + 1) * HD]
                    for h in range(RATIO)
                ],
                axis=0,
            )
            spans = []
            for b in range(reach + 1):
                a, z = max(low - b * tokens, 0), min(high - b * tokens, tokens)
                if a < z:
                    spans.append((b, a, z))
            scores = jnp.concatenate(
                [
                    lax.dot_general(
                        queries,
                        blocks[b][a:z, head * HD : (head + 1) * HD],
                        (((1,), (1,)), ((), ())),
                        preferred_element_type=jnp.float32,
                    )
                    for b, a, z in spans
                ],
                axis=1,
            )
            mask = bias[t : t + TILE, low:high]
            scores = scores * scale + jnp.concatenate([mask] * RATIO, axis=0)
            highest = jnp.max(scores, axis=1, keepdims=True)
            probs = jnp.exp2(scores - highest).astype(jnp.bfloat16)
            total = jnp.zeros((RATIO * TILE, 2 * HD), jnp.float32)
            for b, a, z in spans:
                at = b * tokens + a - low
                value = blocks[b][a:z, (heads + head) * HD : (heads + head + 1) * HD]
                value = jnp.concatenate([value, jnp.ones((z - a, HD), jnp.bfloat16)], axis=1)
                total += jnp.dot(
                    probs[:, at : at + z - a], value, preferred_element_type=jnp.float32
                )
            result = (total[:, :HD] / total[:, HD:]).astype(out_ref.dtype)
            for h in range(RATIO):
                out_ref[t : t + TILE, wide + h * HD : wide + (h + 1) * HD] = result[
                    h * TILE : (h + 1) * TILE
                ]


def attend(lengths, queries, blocks, chunk, heads, partial):
    tokens = queries.shape[0]
    reach = len(blocks) - 1
    width = heads * RATIO * HD
    columns = pl.BlockSpec((tokens, width), lambda i: (0, chunk))
    in_specs = [pl.BlockSpec(memory_space=pltpu.SMEM), columns] + [VMEM] * len(blocks)
    operands = [lengths, queries, *blocks]
    aliases = {}
    if partial is not None:
        aliases = {len(operands): 0}
        operands.append(partial)
        in_specs.append(pl.BlockSpec(memory_space=pl.ANY))
    keys = tokens * (reach + 1)
    return pl.pallas_call(
        functools.partial(attend_kernel, reach),
        grid=(1,),
        in_specs=in_specs,
        out_specs=columns,
        out_shape=jax.ShapeDtypeStruct((tokens, QH * HD), jnp.bfloat16),
        scratch_shapes=[pltpu.VMEM((tokens, keys), jnp.float32)],
        input_output_aliases=aliases,
        compiler_params=pltpu.CompilerParams(vmem_limit_bytes=24 * MIB),
        cost_estimate=pl.CostEstimate(
            flops=6 * heads * RATIO * tokens * keys * HD,
            bytes_accessed=4 * tokens * heads * (RATIO + reach + 1) * HD,
            transcendentals=heads * RATIO * tokens * keys,
        ),
        name="attend",
    )(*operands)


def shards(hidden, queries, norm_gain, kv_weight, value_bias, doc_lengths):
    return layer(hidden[0], queries[0], norm_gain, kv_weight, value_bias, doc_lengths)[None]


def layer(hidden, queries, norm_gain, kv_weight, value_bias, doc_lengths):
    parts = lax.axis_size("fsdp")
    length = lax.axis_size("sp")
    held = kv_weight.shape[0]
    pair = 2 if parts % 2 == 0 else 1
    groups = parts // pair
    reach = length // 4
    heads = KVH // CHUNKS
    gain = norm_gain[None]

    arrived = []
    for d in range(1, groups):
        there = [(i, (i + d * pair) % parts) for i in range(parts)]
        kernel = functools.partial(away_kernel, parts, pair, d)
        sent = scaled(kernel, hidden, gain, pair * held, False)[0]
        arrived.append(lax.ppermute(sent, "fsdp", there))
    weights = [kv_weight]
    if pair == 2:
        weights.append(lax.ppermute(kv_weight, "fsdp", [(i, i ^ 1) for i in range(parts)]))
    kernel = functools.partial(home_kernel, pair)
    mine, power = scaled(kernel, hidden, gain, pair * held, True)
    totals = project(mine, weights, range(CHUNKS), heads, jnp.float32)

    sums = []
    for c in range(CHUNKS):
        returned = []
        for d in range(1, groups):
            back = [(i, (i - d * pair) % parts) for i in range(parts)]
            part = project(arrived[d - 1], weights, [c], heads, jnp.bfloat16)
            returned.append(lax.ppermute(part, "fsdp", back))
        sums.append(merge(totals, power, value_bias[None], returned, c, heads))

    out = None
    for c, own in enumerate(sums):
        blocks = [own]
        if reach % 2 == 0 and length % 2 == 0:
            chain = [own]
            for b in range(2, reach + 1, 2):
                ahead = [(i, i + b) for i in range(length - b)]
                chain.append(lax.ppermute(own, "sp", ahead))
            swap = [(i, i ^ 1) for i in range(length)]
            for b in range(reach // 2):
                near = lax.ppermute(pick(chain[b], chain[b + 1]), "sp", swap)
                blocks = [chain[b + 1], near] + blocks
        else:
            for b in range(1, reach + 1):
                ahead = [(i, i + b) for i in range(length - b)]
                blocks = [lax.ppermute(own, "sp", ahead)] + blocks
        out = attend(doc_lengths, queries, blocks, c, heads, out)
    return out


def solution(mesh):
    in_specs = (
        P("fsdp", "sp", None),
        P("fsdp", "sp", None),
        P(),
        P("fsdp", None),
        P(),
        P("fsdp", None),
    )
    out_specs = P("fsdp", "sp", None)
    return jax.shard_map(shards, mesh=mesh, in_specs=in_specs, out_specs=out_specs, check_vma=False)
```

time: 271 us -> 100 us (0.37)
  the two profiles are of different devices: /device:TPU:8 before, /device:TPU:0 now
where the time goes in v2:
time: 100 us
  waiting for transfers between devices  47 us (47%)
  starting transfers between devices  26.9 us (27%)
  Pallas kernels  23.5 us (24%)
  local copies, waits for them, and re-layouts  2.49 us (2%)
    ppermute x1, waiting for transfers between devices, layer(): arrived.append(lax.ppermute(sent, 'fsdp', there))  28.5 us
    pallas_call x4, Pallas kernels, attend(): pl.pallas_call(functools.partial(attend_kernel, reach), grid=(1,), in_spe...  15.4 us
    ppermute x4, starting transfers between devices, layer(): chain.append(lax.ppermute(own, 'sp', ahead))  14.3 us
    ppermute x4, waiting for transfers between devices, layer(): returned.append(lax.ppermute(part, 'fsdp', back))  11.5 us
    pallas_call x5, Pallas kernels, project(): pl.pallas_call(functools.partial(project_kernel, starts, width), in_specs...  6.24 us
    ppermute x4, starting transfers between devices, layer(): near = lax.ppermute(pick(chain[b], chain[b + 1]), 'sp', swap)  5.28 us
    ppermute x4, waiting for transfers between devices, layer(): chain.append(lax.ppermute(own, 'sp', ahead))  5.21 us
    ppermute x4, starting transfers between devices, layer(): returned.append(lax.ppermute(part, 'fsdp', back))  4.32 us
  transfers between devices with their start and end apart: 14, of which 7 were waited for; matrix products, arithmetic and copies ran while one was open for 0% of the time, Pallas kernels for 19%

profile of v2, /device:TPU:0, one launch (start us, length us, event | category | flops | bytes accessed | tf_op | source)
XLA Modules:
  0.0 100.1 jit_solution(16735636988797305253)
XLA Ops:
  0.0 0.5 collective-permute-start
  0.5 0.0 copy-start.2
  0.5 1.7 %copy-done.2 = bf16[1,256,5120]{2,1,0:T(8,128)(2,1)S(1)} copy-done((bf16[1,256,5120]{2,1,0:T(8,128)(2,1)S(1)}, bf16[1,256,5120]{2,1,0:T(8,128)(2,1)}, u32[]{:S(2)}) %copy-start.2) | copy-done | bytes 2621464
  2.2 0.0 copy-start.3
  2.2 0.7 copy-done.3
  3.0 0.0 copy-start
  3.0 0.2 scaled.3
  3.2 2.6 %collective-permute-start.1 = (bf16[256,2560]{1,0:T(8,128)(2,1)S(1)}, bf16[256,2560]{1,0:T(8,128)(2,1)S(1)}, u32[]{:S(2)}, u32[]{:S(2)}) collective-permute-start(bf16[256,2560]{1,0:T(8,128)(2,1)S(1)} %scaled.3), channel_id=1, source_target_pairs={{0,16},{8,24},{16,0},{24,8},{1,17},{9,25},{17,1},{25,9},{2,18},{10... | collective-permute-start | bytes 3932168 | tf_op jit(solution)/shard_map/ppermute | solution.py:274
  5.8 1.0 scaled.2
  6.7 28.5 %collective-permute-done.1.rows_ref = bf16[256,2560]{1,0:T(8,128)(2,1)S(1)} collective-permute-done((bf16[256,2560]{1,0:T(8,128)(2,1)S(1)}, bf16[256,2560]{1,0:T(8,128)(2,1)S(1)}, u32[]{:S(2)}, u32[]{:S(2)}) %collective-permute-start.1) | collective-permute-done | bytes 1310752 | tf_op jit(solution)/shard_map/ppermute | solution.py:274
  35.2 0.0 collective-permute-done.refs_1_
  35.2 0.0 copy-done
  35.2 0.8 project.6
  36.1 1.8 %collective-permute-start.2 = (bf16[256,512]{1,0:T(8,128)(2,1)S(1)}, bf16[256,512]{1,0:T(8,128)(2,1)S(1)}, u32[]{:S(2)}, u32[]{:S(2)}) collective-permute-start(bf16[256,512]{1,0:T(8,128)(2,1)S(1)} %project.6), channel_id=1, source_target_pairs={{0,16},{8,24},{16,0},{24,8},{1,17},{9,25},{17,1},{25,9},{2,18},{10... | collective-permute-start | bytes 786440 | tf_op jit(solution)/shard_map/ppermute | solution.py:288
  37.9 0.8 project.7
  38.7 0.4 collective-permute-start.5
  39.1 0.9 project.9
  39.9 1.8 %collective-permute-start.11 = (bf16[256,512]{1,0:T(8,128)(2,1)S(1)}, bf16[256,512]{1,0:T(8,128)(2,1)S(1)}, u32[]{:S(2)}, u32[]{:S(2)}) collective-permute-start(bf16[256,512]{1,0:T(8,128)(2,1)S(1)} %project.9), channel_id=1, source_target_pairs={{0,16},{8,24},{16,0},{24,8},{1,17},{9,25},{17,1},{25,9},{2,18},{10... | collective-permute-start | bytes 786440 | tf_op jit(solution)/shard_map/ppermute | solution.py:288
  41.7 0.8 project.8
  42.6 0.4 collective-permute-start.8
  42.9 0.0 copy-start.4
  42.9 2.9 %project.5.home_ref = f32[256,2048]{1,0:T(8,128)S(1)} custom-call(bf16[256,2560]{1,0:T(8,128)(2,1)S(1)} %get-tuple-element.7.rows_ref, bf16[1280,2048]{1,0:T(8,128)(2,1)S(1)} %copy-done, bf16[1280,2048]{1,0:T(8,128)(2,1)S(1)} %collective-permute-done.refs_1_), custom_call_target="tpu_custom_call" | custom-call | flops 2684354560 | bytes 10485760 | tf_op jit(solution)/shard_map/project/pallas_call | solution.py:96
  45.8 10.7 %collective-permute-done.11.refs_0_ = bf16[256,512]{1,0:T(8,128)(2,1)S(1)} collective-permute-done((bf16[256,512]{1,0:T(8,128)(2,1)S(1)}, bf16[256,512]{1,0:T(8,128)(2,1)S(1)}, u32[]{:S(2)}, u32[]{:S(2)}) %collective-permute-start.11) | collective-permute-done | bytes 262176 | tf_op jit(solution)/shard_map/ppermute | solution.py:288
  56.5 0.0 copy-done.4
  56.5 0.1 merge.7.even_ref.refs_2_
  56.6 3.7 %collective-permute-start.12 = (bf16[256,512]{1,0:T(8,128)(2,1)S(1)}, bf16[256,512]{1,0:T(8,128)(2,1)S(1)}, u32[]{:S(2)}, u32[]{:S(2)}) collective-permute-start(bf16[256,512]{1,0:T(8,128)(2,1)S(1)} %merge.7.even_ref.refs_2_), channel_id=1, source_target_pairs={{0,2},{1,3},{2,4},{3,5},{4,6},{5,7},{8,10},{9,11},{10,12},{11,13},... | collective-permute-start | bytes 786440 | tf_op jit(solution)/shard_map/ppermute | solution.py:298
  60.4 0.7 collective-permute-done.8.refs_0_
  61.1 0.1 merge.6.even_ref.refs_2_
  61.2 3.4 %collective-permute-start.9 = (bf16[256,512]{1,0:T(8,128)(2,1)S(1)}, bf16[256,512]{1,0:T(8,128)(2,1)S(1)}, u32[]{:S(2)}, u32[]{:S(2)}) collective-permute-start(bf16[256,512]{1,0:T(8,128)(2,1)S(1)} %merge.6.even_ref.refs_2_), channel_id=1, source_target_pairs={{0,2},{1,3},{2,4},{3,5},{4,6},{5,7},{8,10},{9,11},{10,12},{11,13},... | collective-permute-start | bytes 786440 | tf_op jit(solution)/shard_map/ppermute | solution.py:298
  64.7 0.0 collective-permute-done.5.refs_0_
  64.7 0.1 merge.5.even_ref.refs_2_
  64.8 3.5 %collective-permute-start.6 = (bf16[256,512]{1,0:T(8,128)(2,1)S(1)}, bf16[256,512]{1,0:T(8,128)(2,1)S(1)}, u32[]{:S(2)}, u32[]{:S(2)}) collective-permute-start(bf16[256,512]{1,0:T(8,128)(2,1)S(1)} %merge.5.even_ref.refs_2_), channel_id=1, source_target_pairs={{0,2},{1,3},{2,4},{3,5},{4,6},{5,7},{8,10},{9,11},{10,12},{11,13},... | collective-permute-start | bytes 786440 | tf_op jit(solution)/shard_map/ppermute | solution.py:298
  68.3 0.0 collective-permute-done.2.refs_0_
  68.3 0.1 merge.4.even_ref.refs_2_
  68.4 0.0 copy-start.1
  68.4 0.0 copy-start.5
  68.4 3.6 %collective-permute-start.3 = (bf16[256,512]{1,0:T(8,128)(2,1)S(1)}, bf16[256,512]{1,0:T(8,128)(2,1)S(1)}, u32[]{:S(2)}, u32[]{:S(2)}) collective-permute-start(bf16[256,512]{1,0:T(8,128)(2,1)S(1)} %merge.4.even_ref.refs_2_), channel_id=1, source_target_pairs={{0,2},{1,3},{2,4},{3,5},{4,6},{5,7},{8,10},{9,11},{10,12},{11,13},... | collective-permute-start | bytes 786440 | tf_op jit(solution)/shard_map/ppermute | solution.py:298
  72.1 0.0 collective-permute-done.12.odd_ref.refs_0_
  72.1 1.6 %collective-permute-start.13 = (bf16[256,512]{1,0:T(8,128)(2,1)S(1)}, bf16[256,512]{1,0:T(8,128)(2,1)S(1)}, u32[]{:S(2)}, u32[]{:S(2)}) collective-permute-start(bf16[256,512]{1,0:T(8,128)(2,1)S(1)} %pick.7), channel_id=1, source_target_pairs={{0,1},{1,0},{2,3},{3,2},{4,5},{5,4},{6,7},{7,6},{8,9},{9,8},{10,11... | collective-permute-start | bytes 786440 | tf_op jit(solution)/shard_map/ppermute | solution.py:301
  73.7 0.0 collective-permute-done.9.odd_ref.refs_0_
  73.7 0.6 collective-permute-start.10
  74.3 2.7 %collective-permute-done.6.odd_ref.refs_0_ = bf16[256,512]{1,0:T(8,128)(2,1)S(1)} collective-permute-done((bf16[256,512]{1,0:T(8,128)(2,1)S(1)}, bf16[256,512]{1,0:T(8,128)(2,1)S(1)}, u32[]{:S(2)}, u32[]{:S(2)}) %collective-permute-start.6) | collective-permute-done | bytes 262176 | tf_op jit(solution)/shard_map/ppermute | solution.py:298
  77.0 1.6 %collective-permute-start.7 = (bf16[256,512]{1,0:T(8,128)(2,1)S(1)}, bf16[256,512]{1,0:T(8,128)(2,1)S(1)}, u32[]{:S(2)}, u32[]{:S(2)}) collective-permute-start(bf16[256,512]{1,0:T(8,128)(2,1)S(1)} %pick.5), channel_id=1, source_target_pairs={{0,1},{1,0},{2,3},{3,2},{4,5},{5,4},{6,7},{7,6},{8,9},{9,8},{10,11... | collective-permute-start | bytes 786440 | tf_op jit(solution)/shard_map/ppermute | solution.py:301
  78.5 2.5 %collective-permute-done.3.odd_ref.refs_0_ = bf16[256,512]{1,0:T(8,128)(2,1)S(1)} collective-permute-done((bf16[256,512]{1,0:T(8,128)(2,1)S(1)}, bf16[256,512]{1,0:T(8,128)(2,1)S(1)}, u32[]{:S(2)}, u32[]{:S(2)}) %collective-permute-start.3) | collective-permute-done | bytes 262176 | tf_op jit(solution)/shard_map/ppermute | solution.py:298
  81.1 0.2 pick.4
  81.3 1.6 %collective-permute-start.4 = (bf16[256,512]{1,0:T(8,128)(2,1)S(1)}, bf16[256,512]{1,0:T(8,128)(2,1)S(1)}, u32[]{:S(2)}, u32[]{:S(2)}) collective-permute-start(bf16[256,512]{1,0:T(8,128)(2,1)S(1)} %pick.4), channel_id=1, source_target_pairs={{0,1},{1,0},{2,3},{3,2},{4,5},{5,4},{6,7},{7,6},{8,9},{9,8},{10,11... | collective-permute-start | bytes 786440 | tf_op jit(solution)/shard_map/ppermute | solution.py:301
  82.8 0.0 collective-permute-done.13.refs_1_
  82.9 0.0 copy-done.1
  82.9 0.0 copy-done.5
  82.9 3.9 %attend.4.refs_3_ = bf16[256,4096]{1,0:T(8,128)(2,1)} custom-call(s32[1,16]{1,0:T(1,128)S(1)} %copy-done.5, bf16[256,4096]{1,0:T(8,128)(2,1)S(1)} %bitcast.5, bf16[256,512]{1,0:T(8,128)(2,1)S(1)} %collective-permute-done.12.odd_ref.refs_0_, bf16[256,512]{1,0:T(8,128)(2,1)S(1)} %collective-permute-done.13.refs_1_, bf16[256,512]{1,0:T(8,128)(2,1)S(1)} %merge.7.even_ref.refs_2_), custom_call_target="tpu_custom_call" | custom-call | flops 1207959552 | bytes 1835008 | tf_op jit(solution)/shard_map/attend/pallas_call | solution.py:237
  86.7 0.2 collective-permute-done.10.refs_1_
  87.0 3.8 %attend.5.refs_3_ = bf16[256,4096]{1,0:T(8,128)(2,1)} custom-call(s32[1,16]{1,0:T(1,128)S(1)} %copy-done.5, bf16[256,4096]{1,0:T(8,128)(2,1)S(1)} %bitcast.6, bf16[256,512]{1,0:T(8,128)(2,1)S(1)} %collective-permute-done.9.odd_ref.refs_0_, bf16[256,512]{1,0:T(8,128)(2,1)S(1)} %collective-permute-done.10.refs_1_, ...), custom_call_target="tpu_custom_call", output_to_operand_aliasing={{}: (5, {})} | custom-call | flops 1207959552 | bytes 1835008 | tf_op jit(solution)/shard_map/attend/pallas_call | solution.py:237
  90.8 1.6 %collective-permute-done.7.refs_1_ = bf16[256,512]{1,0:T(8,128)(2,1)S(1)} collective-permute-done((bf16[256,512]{1,0:T(8,128)(2,1)S(1)}, bf16[256,512]{1,0:T(8,128)(2,1)S(1)}, u32[]{:S(2)}, u32[]{:S(2)}) %collective-permute-start.7) | collective-permute-done | bytes 262176 | tf_op jit(solution)/shard_map/ppermute | solution.py:301
  92.4 3.9 %attend.6.refs_3_ = bf16[256,4096]{1,0:T(8,128)(2,1)} custom-call(s32[1,16]{1,0:T(1,128)S(1)} %copy-done.5, bf16[256,4096]{1,0:T(8,128)(2,1)S(1)} %bitcast.7, bf16[256,512]{1,0:T(8,128)(2,1)S(1)} %collective-permute-done.6.odd_ref.refs_0_, bf16[256,512]{1,0:T(8,128)(2,1)S(1)} %collective-permute-done.7.refs_1_, ...), custom_call_target="tpu_custom_call", output_to_operand_aliasing={{}: (5, {})} | custom-call | flops 1207959552 | bytes 1835008 | tf_op jit(solution)/shard_map/attend/pallas_call | solution.py:237
  96.2 0.0 collective-permute-done.4.refs_1_
  96.3 3.9 %attend.7 = bf16[256,4096]{1,0:T(8,128)(2,1)} custom-call(s32[1,16]{1,0:T(1,128)S(1)} %copy-done.5, bf16[256,4096]{1,0:T(8,128)(2,1)S(1)} %bitcast.8, bf16[256,512]{1,0:T(8,128)(2,1)S(1)} %collective-permute-done.3.odd_ref.refs_0_, bf16[256,512]{1,0:T(8,128)(2,1)S(1)} %collective-permute-done.4.refs_1_, ...), custom_call_target="tpu_custom_call", output_to_operand_aliasing={{}: (5, {})} | custom-call | flops 1207959552 | bytes 1835008 | tf_op jit(solution)/shard_map/attend/pallas_call | solution.py:237
  (3 shorter events, 0.1 us)
Async XLA Ops:
  0.0 35.2 %collective-permute-start = (bf16[1280,2048]{1,0:T(8,128)(2,1)}, bf16[1280,2048]{1,0:T(8,128)(2,1)S(1)}, u32[]{:S(2)}, u32[]{:S(2)}) collective-permute-start(bf16[1280,2048]{1,0:T(8,128)(2,1)} %refs_0_.9), channel_id=1, source_target_pairs={{0,8},{8,0},{16,24},{24,16},{1,9},{9,1},{17,25},{25,17},{2,10},{10... | collective-permute-start | bytes 15728648 | tf_op jit(solution)/shard_map/ppermute | solution.py:277
  0.5 1.7 %copy-start.2 = (bf16[1,256,5120]{2,1,0:T(8,128)(2,1)S(1)}, bf16[1,256,5120]{2,1,0:T(8,128)(2,1)}, u32[]{:S(2)}) copy-start(bf16[1,256,5120]{2,1,0:T(8,128)(2,1)} %param.6) | copy-start | bytes 7864324
  2.2 0.7 copy-start.3
  3.0 32.2 %copy-start = (bf16[1280,2048]{1,0:T(8,128)(2,1)S(1)}, bf16[1280,2048]{1,0:T(8,128)(2,1)}, u32[]{:S(2)}) copy-start(bf16[1280,2048]{1,0:T(8,128)(2,1)} %refs_0_.9) | copy-start | bytes 15728644
  3.2 32.0 %collective-permute-start.1 = (bf16[256,2560]{1,0:T(8,128)(2,1)S(1)}, bf16[256,2560]{1,0:T(8,128)(2,1)S(1)}, u32[]{:S(2)}, u32[]{:S(2)}) collective-permute-start(bf16[256,2560]{1,0:T(8,128)(2,1)S(1)} %scaled.3), channel_id=1, source_target_pairs={{0,16},{8,24},{16,0},{24,8},{1,17},{9,25},{17,1},{25,9},{2,18},{10... | collective-permute-start | bytes 3932168 | tf_op jit(solution)/shard_map/ppermute | solution.py:274
  36.1 32.2 %collective-permute-start.2 = (bf16[256,512]{1,0:T(8,128)(2,1)S(1)}, bf16[256,512]{1,0:T(8,128)(2,1)S(1)}, u32[]{:S(2)}, u32[]{:S(2)}) collective-permute-start(bf16[256,512]{1,0:T(8,128)(2,1)S(1)} %project.6), channel_id=1, source_target_pairs={{0,16},{8,24},{16,0},{24,8},{1,17},{9,25},{17,1},{25,9},{2,18},{10... | collective-permute-start | bytes 786440 | tf_op jit(solution)/shard_map/ppermute | solution.py:288
  38.7 26.0 %collective-permute-start.5 = (bf16[256,512]{1,0:T(8,128)(2,1)S(1)}, bf16[256,512]{1,0:T(8,128)(2,1)S(1)}, u32[]{:S(2)}, u32[]{:S(2)}) collective-permute-start(bf16[256,512]{1,0:T(8,128)(2,1)S(1)} %project.7), channel_id=1, source_target_pairs={{0,16},{8,24},{16,0},{24,8},{1,17},{9,25},{17,1},{25,9},{2,18},{10... | collective-permute-start | bytes 786440 | tf_op jit(solution)/shard_map/ppermute | solution.py:288
  39.9 16.6 %collective-permute-start.11 = (bf16[256,512]{1,0:T(8,128)(2,1)S(1)}, bf16[256,512]{1,0:T(8,128)(2,1)S(1)}, u32[]{:S(2)}, u32[]{:S(2)}) collective-permute-start(bf16[256,512]{1,0:T(8,128)(2,1)S(1)} %project.9), channel_id=1, source_target_pairs={{0,16},{8,24},{16,0},{24,8},{1,17},{9,25},{17,1},{25,9},{2,18},{10... | collective-permute-start | bytes 786440 | tf_op jit(solution)/shard_map/ppermute | solution.py:288
  42.6 18.5 %collective-permute-start.8 = (bf16[256,512]{1,0:T(8,128)(2,1)S(1)}, bf16[256,512]{1,0:T(8,128)(2,1)S(1)}, u32[]{:S(2)}, u32[]{:S(2)}) collective-permute-start(bf16[256,512]{1,0:T(8,128)(2,1)S(1)} %project.8), channel_id=1, source_target_pairs={{0,16},{8,24},{16,0},{24,8},{1,17},{9,25},{17,1},{25,9},{2,18},{10... | collective-permute-start | bytes 786440 | tf_op jit(solution)/shard_map/ppermute | solution.py:288
  42.9 13.6 %copy-start.4 = (f32[1024]{0:T(1024)S(1)}, f32[1024]{0:T(1024)}, u32[]{:S(2)}) copy-start(f32[1024]{0:T(1024)} %param.10) | copy-start | bytes 12292
  56.6 15.4 %collective-permute-start.12 = (bf16[256,512]{1,0:T(8,128)(2,1)S(1)}, bf16[256,512]{1,0:T(8,128)(2,1)S(1)}, u32[]{:S(2)}, u32[]{:S(2)}) collective-permute-start(bf16[256,512]{1,0:T(8,128)(2,1)S(1)} %merge.7.even_ref.refs_2_), channel_id=1, source_target_pairs={{0,2},{1,3},{2,4},{3,5},{4,6},{5,7},{8,10},{9,11},{10,12},{11,13},... | collective-permute-start | bytes 786440 | tf_op jit(solution)/shard_map/ppermute | solution.py:298
  61.2 12.4 %collective-permute-start.9 = (bf16[256,512]{1,0:T(8,128)(2,1)S(1)}, bf16[256,512]{1,0:T(8,128)(2,1)S(1)}, u32[]{:S(2)}, u32[]{:S(2)}) collective-permute-start(bf16[256,512]{1,0:T(8,128)(2,1)S(1)} %merge.6.even_ref.refs_2_), channel_id=1, source_target_pairs={{0,2},{1,3},{2,4},{3,5},{4,6},{5,7},{8,10},{9,11},{10,12},{11,13},... | collective-permute-start | bytes 786440 | tf_op jit(solution)/shard_map/ppermute | solution.py:298
  64.8 12.2 %collective-permute-start.6 = (bf16[256,512]{1,0:T(8,128)(2,1)S(1)}, bf16[256,512]{1,0:T(8,128)(2,1)S(1)}, u32[]{:S(2)}, u32[]{:S(2)}) collective-permute-start(bf16[256,512]{1,0:T(8,128)(2,1)S(1)} %merge.5.even_ref.refs_2_), channel_id=1, source_target_pairs={{0,2},{1,3},{2,4},{3,5},{4,6},{5,7},{8,10},{9,11},{10,12},{11,13},... | collective-permute-start | bytes 786440 | tf_op jit(solution)/shard_map/ppermute | solution.py:298
  68.4 14.4 %copy-start.1 = (bf16[1,256,4096]{2,1,0:T(8,128)(2,1)S(1)}, bf16[1,256,4096]{2,1,0:T(8,128)(2,1)}, u32[]{:S(2)}) copy-start(bf16[1,256,4096]{2,1,0:T(8,128)(2,1)} %param.7) | copy-start | bytes 6291460
  68.4 14.4 %copy-start.5 = (s32[1,16]{1,0:T(1,128)S(1)}, s32[1,16]{1,0:T(1,128)}, u32[]{:S(2)}) copy-start(s32[1,16]{1,0:T(1,128)} %lengths_ref.7) | copy-start | bytes 196
  68.4 12.7 %collective-permute-start.3 = (bf16[256,512]{1,0:T(8,128)(2,1)S(1)}, bf16[256,512]{1,0:T(8,128)(2,1)S(1)}, u32[]{:S(2)}, u32[]{:S(2)}) collective-permute-start(bf16[256,512]{1,0:T(8,128)(2,1)S(1)} %merge.4.even_ref.refs_2_), channel_id=1, source_target_pairs={{0,2},{1,3},{2,4},{3,5},{4,6},{5,7},{8,10},{9,11},{10,12},{11,13},... | collective-permute-start | bytes 786440 | tf_op jit(solution)/shard_map/ppermute | solution.py:298
  72.1 10.7 %collective-permute-start.13 = (bf16[256,512]{1,0:T(8,128)(2,1)S(1)}, bf16[256,512]{1,0:T(8,128)(2,1)S(1)}, u32[]{:S(2)}, u32[]{:S(2)}) collective-permute-start(bf16[256,512]{1,0:T(8,128)(2,1)S(1)} %pick.7), channel_id=1, source_target_pairs={{0,1},{1,0},{2,3},{3,2},{4,5},{5,4},{6,7},{7,6},{8,9},{9,8},{10,11... | collective-permute-start | bytes 786440 | tf_op jit(solution)/shard_map/ppermute | solution.py:301
  73.7 13.3 %collective-permute-start.10 = (bf16[256,512]{1,0:T(8,128)(2,1)S(1)}, bf16[256,512]{1,0:T(8,128)(2,1)S(1)}, u32[]{:S(2)}, u32[]{:S(2)}) collective-permute-start(bf16[256,512]{1,0:T(8,128)(2,1)S(1)} %pick.6), channel_id=1, source_target_pairs={{0,1},{1,0},{2,3},{3,2},{4,5},{5,4},{6,7},{7,6},{8,9},{9,8},{10,11... | collective-permute-start | bytes 786440 | tf_op jit(solution)/shard_map/ppermute | solution.py:301
  77.0 15.4 %collective-permute-start.7 = (bf16[256,512]{1,0:T(8,128)(2,1)S(1)}, bf16[256,512]{1,0:T(8,128)(2,1)S(1)}, u32[]{:S(2)}, u32[]{:S(2)}) collective-permute-start(bf16[256,512]{1,0:T(8,128)(2,1)S(1)} %pick.5), channel_id=1, source_target_pairs={{0,1},{1,0},{2,3},{3,2},{4,5},{5,4},{6,7},{7,6},{8,9},{9,8},{10,11... | collective-permute-start | bytes 786440 | tf_op jit(solution)/shard_map/ppermute | solution.py:301
  81.3 15.0 %collective-permute-start.4 = (bf16[256,512]{1,0:T(8,128)(2,1)S(1)}, bf16[256,512]{1,0:T(8,128)(2,1)S(1)}, u32[]{:S(2)}, u32[]{:S(2)}) collective-permute-start(bf16[256,512]{1,0:T(8,128)(2,1)S(1)} %pick.4), channel_id=1, source_target_pairs={{0,1},{1,0},{2,3},{3,2},{4,5},{5,4},{6,7},{7,6},{8,9},{9,8},{10,11... | collective-permute-start | bytes 786440 | tf_op jit(solution)/shard_map/ppermute | solution.py:301

commit v3 on v0

v3 whole, which is shorter than its diff:
```python
import functools

import jax
import jax.numpy as jnp
from jax import lax
from jax.experimental import pallas as pl
from jax.experimental.pallas import tpu as pltpu
from jax.sharding import PartitionSpec as P

QH = 32
KVH = 8
HD = 128
EPS = 1e-06
RATIO = QH // KVH
LOG2E = 1.4426950408889634
SUMS = ((0, 1), (2, 3), (4, 5), (6, 7))
BLOCKS = ((0, 1), (2, 3), (4, 5), (6,), (7,))
PIECES = 2
TILE = 128
STRIP = 32
AHEAD = 2
MASKED = -1e30
MIB = 1 << 20
VMEM = pl.BlockSpec(memory_space=pltpu.VMEM)
SMEM = pl.BlockSpec(memory_space=pltpu.SMEM)
HBM = pl.BlockSpec(memory_space=pltpu.HBM)


def in_hbm(value):
    return pltpu.with_memory_space_constraint(value, pltpu.HBM)


def place_of(parts, pair, ahead, held):
    me = lax.axis_index("fsdp")
    group, core = lax.div(me, jnp.int32(pair)), lax.rem(me, jnp.int32(pair))
    there = lax.rem(group + ahead, jnp.int32(parts // pair))
    return pl.multiple_of(there * (pair * held), HD), core


def put_scaled(out_ref, rows_ref, gain_ref, some, core):
    held = out_ref.shape[1] // 2

    @pl.when(core == 0)
    def _():
        out_ref[...] = (rows_ref[some, :].astype(jnp.float32) * gain_ref[...]).astype(jnp.bfloat16)

    @pl.when(core == 1)
    def _():
        for a, b in ((0, held), (held, 0)):
            wide = rows_ref[some, a : a + held].astype(jnp.float32)
            scaled = wide * gain_ref[:, a : a + held]
            out_ref[:, b : b + held] = scaled.astype(jnp.bfloat16)


def away_kernel(parts, pair, ahead, piece, hidden_ref, gain_ref, out_ref, rows, gains, sems):
    step, width = rows.shape
    first, core = place_of(parts, pair, ahead, width // pair)
    columns = pl.ds(first, width)
    some = pl.ds(piece * step, step)
    copies = [
        pltpu.make_async_copy(gain_ref.at[:, columns], gains, sems.at[0]),
        pltpu.make_async_copy(hidden_ref.at[some, columns], rows, sems.at[1]),
    ]
    for copy in copies:
        copy.start()
    for copy in copies:
        copy.wait()
    put_scaled(out_ref, rows, gains, slice(None), core)


def away(hidden, gain, parts, pair, held, ahead, piece):
    step, width = hidden.shape[0] // PIECES, pair * held
    return pl.pallas_call(
        functools.partial(away_kernel, parts, pair, ahead, piece),
        in_specs=[HBM, HBM],
        out_specs=VMEM,
        out_shape=jax.ShapeDtypeStruct((step, width), jnp.bfloat16),
        scratch_shapes=[
            pltpu.VMEM((step, width), jnp.bfloat16),
            pltpu.VMEM((1, width), jnp.float32),
            pltpu.SemaphoreType.DMA((2,)),
        ],
        compiler_params=pltpu.CompilerParams(vmem_limit_bytes=8 * MIB),
        name="away",
    )(in_hbm(hidden), in_hbm(gain))


def home_kernel(parts, pair, hidden_ref, gain_ref, weight_ref, *refs):
    out_ref, power_ref, held_ref, rows, gains, sems = refs
    copies = [
        pltpu.make_async_copy(gain_ref, gains, sems.at[0]),
        pltpu.make_async_copy(hidden_ref, rows, sems.at[1]),
        pltpu.make_async_copy(weight_ref, held_ref, sems.at[2]),
    ]
    for copy in copies:
        copy.start()
    for copy in copies[:2]:
        copy.wait()
    width = out_ref.shape[1]
    first, core = place_of(parts, pair, 0, width // pair)
    columns = pl.ds(first, width)
    put_scaled(out_ref, rows.at[:, columns], gains.at[:, columns], slice(None), core)
    tokens, model = rows.shape
    total = jnp.zeros((tokens, HD), jnp.float32)
    for j in range(0, model, HD):
        wide = rows[:, j : j + HD].astype(jnp.float32)
        total += wide * wide
    mean = jnp.sum(total, axis=1, keepdims=True) / model
    power_ref[...] = lax.rsqrt(mean + EPS)
    copies[2].wait()


def home(hidden, gain, weight, parts, pair):
    tokens, model = hidden.shape
    return pl.pallas_call(
        functools.partial(home_kernel, parts, pair),
        in_specs=[HBM] * 3,
        out_specs=[VMEM] * 3,
        out_shape=[
            jax.ShapeDtypeStruct((tokens, pair * weight.shape[0]), jnp.bfloat16),
            jax.ShapeDtypeStruct((tokens, 1), jnp.float32),
            jax.ShapeDtypeStruct(weight.shape, weight.dtype),
        ],
        scratch_shapes=[
            pltpu.VMEM((tokens, model), jnp.bfloat16),
            pltpu.VMEM((1, model), jnp.float32),
            pltpu.SemaphoreType.DMA((3,)),
        ],
        compiler_params=pltpu.CompilerParams(vmem_limit_bytes=16 * MIB),
        name="home",
    )(in_hbm(hidden), in_hbm(gain), in_hbm(weight))


def columns_of(chunks):
    return [
        (half * KVH * HD + heads[0] * HD, len(heads) * HD) for heads in chunks for half in range(2)
    ]


def project_kernel(runs, skip, counts, *refs):
    ready, rows = refs[: counts[0]], refs[counts[0] : sum(counts[:2])]
    weights, out_ref = refs[sum(counts[:2]) : -1], refs[-1]
    depth = weights[0].shape[0]
    row = 0
    for ready_ref in ready:
        row = ready_ref.shape[0]
        out_ref[:row, :] = ready_ref[:, skip : skip + out_ref.shape[1]]
    for rows_ref in rows:
        some = slice(row, row + rows_ref.shape[0])
        row = some.stop
        column = 0
        for start, width in runs:
            total = None
            for w, weight in enumerate(weights):
                term = jnp.dot(
                    rows_ref[:, w * depth : (w + 1) * depth],
                    weight[:, start : start + width],
                    preferred_element_type=jnp.float32,
                )
                total = term if total is None else total + term
            out_ref[some, column : column + width] = total.astype(out_ref.dtype)
            column += width


def project(rows, weights, chunks, dtype, ready=(), skip=0):
    tokens = sum(r.shape[0] for r in (*ready, *rows))
    depth = rows[0].shape[1]
    runs = columns_of(chunks)
    columns = sum(width for _, width in runs)
    operands = [*ready, *rows, *weights]
    return pl.pallas_call(
        functools.partial(project_kernel, runs, skip, (len(ready), len(rows))),
        in_specs=[VMEM] * len(operands),
        out_specs=VMEM,
        out_shape=jax.ShapeDtypeStruct((tokens, columns), dtype),
        compiler_params=pltpu.CompilerParams(vmem_limit_bytes=24 * MIB),
        cost_estimate=pl.CostEstimate(
            flops=2 * rows[0].shape[0] * len(rows) * depth * columns,
            bytes_accessed=2 * depth * columns,
            transcendentals=0,
        ),
        name="project",
    )(*operands)


def merge_kernel(heads, own, other, pieces, mine_ref, power_ref, bias_ref, *refs):
    parts, out_ref = refs[:-1], refs[-1]
    width = len(heads) * HD
    step = out_ref.shape[0] // pieces
    for piece in range(pieces):
        some = slice(piece * step, (piece + 1) * step)
        power = power_ref[some, :]
        for half in range(2):
            total = mine_ref[some, own[half] : own[half] + width]
            for part in parts[piece::pieces]:
                total = total + part[:, other[half] : other[half] + width].astype(jnp.float32)
            if half == 0:
                total = total * (power * (HD ** (-0.5) * LOG2E))
            else:
                first = heads[0] * HD
                total = total * power + bias_ref[:, first : first + width]
            out_ref[some, half * width : (half + 1) * width] = total.astype(jnp.bfloat16)


def merge(mine, power, bias, parts, pieces, heads, own, other):
    return pl.pallas_call(
        functools.partial(merge_kernel, heads, own, other, pieces),
        in_specs=[VMEM] * (3 + len(parts)),
        out_specs=VMEM,
        out_shape=jax.ShapeDtypeStruct((mine.shape[0], 2 * len(heads) * HD), jnp.bfloat16),
        compiler_params=pltpu.CompilerParams(vmem_limit_bytes=4 * MIB),
        name="merge",
    )(mine, power, bias, *parts)


def pick_kernel(even_ref, odd_ref, out_ref):
    odd = lax.rem(lax.axis_index("sp"), jnp.int32(2)) == 1

    @pl.when(odd)
    def _():
        out_ref[...] = odd_ref[...]

    @pl.when(jnp.logical_not(odd))
    def _():
        out_ref[...] = even_ref[...]


def pick(even, odd):
    return pl.pallas_call(
        pick_kernel,
        in_specs=[VMEM] * 2,
        out_specs=VMEM,
        out_shape=jax.ShapeDtypeStruct(even.shape, even.dtype),
        compiler_params=pltpu.CompilerParams(vmem_limit_bytes=4 * MIB),
        name="pick",
    )(even, odd)


def mask_kernel(reach, lengths_ref, out_ref):
    tokens, window = out_ref.shape
    first = lax.axis_index("sp") * tokens
    query_pos = first + lax.broadcasted_iota(jnp.int32, (tokens, HD), 0)
    start = jnp.zeros((tokens, HD), jnp.int32)
    end = jnp.int32(0)
    for i in range(lengths_ref.shape[1]):
        end = end + lengths_ref[0, i]
        start = jnp.where(query_pos >= end, end, start)
    for j in range(0, window, HD):
        key_pos = first - reach * tokens + j + lax.broadcasted_iota(jnp.int32, (tokens, HD), 1)
        allowed = (key_pos >= start) & (key_pos <= query_pos)
        out_ref[:, j : j + HD] = jnp.where(allowed, 0.0, MASKED).astype(jnp.float32)


def mask(lengths, tokens, reach):
    return pl.pallas_call(
        functools.partial(mask_kernel, reach),
        in_specs=[SMEM],
        out_specs=VMEM,
        out_shape=jax.ShapeDtypeStruct((tokens, (reach + 1) * tokens), jnp.float32),
        compiler_params=pltpu.CompilerParams(vmem_limit_bytes=4 * MIB),
        name="mask",
    )(lengths)


def attend_kernel(count, first, bias_ref, query_ref, *refs):
    blocks, (out_ref, scores, probs, tiles, sems) = refs[:count], refs[-5:]
    tokens = query_ref.shape[0]
    heads = blocks[0].shape[1] // (2 * HD)
    span = scores.shape[2]
    buffers = scores.shape[0]
    units = [(head, t) for head in range(heads) for t in range(0, tokens, TILE)]

    def spans(t):
        for b in range(count):
            a, z = max(t - b * tokens, 0), min(t + span - b * tokens, tokens)
            if a < z:
                yield b, a, z, b * tokens + a - t

    def score(u):
        head, t = units[u]
        wide = (first + head) * RATIO * HD
        queries = [
            query_ref[t : t + TILE, wide + h * HD : wide + (h + 1) * HD] for h in range(RATIO)
        ]
        queries = jnp.concatenate(queries, axis=0)
        for b, a, z, at in spans(t):
            scores[u % buffers, :, at : at + z - a] = lax.dot_general(
                queries,
                blocks[b][a:z, head * HD : (head + 1) * HD],
                (((1,), (1,)), ((), ())),
                preferred_element_type=jnp.float32,
            )

    def soften(u):
        t = units[u][1]
        for r in range(0, RATIO * TILE, STRIP):
            m = t + r % TILE
            some = scores[u % buffers, r : r + STRIP, :] + bias_ref[m : m + STRIP, t : t + span]
            highest = jnp.max(some, axis=1, keepdims=True)
            probs[u % buffers, r : r + STRIP, :] = jnp.exp2(some - highest).astype(jnp.bfloat16)

    def blend(u):
        head, t = units[u]
        total = None
        for b, a, z, at in spans(t):
            value = blocks[b][a:z, (heads + head) * HD : (heads + head + 1) * HD]
            value = jnp.concatenate([value, jnp.ones((z - a, HD), jnp.bfloat16)], axis=1)
            term = jnp.dot(
                probs[u % buffers, :, at : at + z - a], value, preferred_element_type=jnp.float32
            )
            total = term if total is None else total + term
        result = (total[:, :HD] / total[:, HD:]).astype(out_ref.dtype)
        for h in range(RATIO):
            tiles[u, :, h * HD : (h + 1) * HD] = result[h * TILE : (h + 1) * TILE]
        wide = (first + head) * RATIO * HD
        place = out_ref.at[t : t + TILE, wide : wide + RATIO * HD]
        copy = pltpu.make_async_copy(tiles.at[u], place, sems.at[u])
        copy.start()
        return copy

    for u in range(min(AHEAD, len(units))):
        score(u)
    copies = []
    for u in range(len(units)):
        if u + AHEAD < len(units):
            score(u + AHEAD)
        soften(u)
        copies.append(blend(u))
    for copy in copies:
        copy.wait()


def attend(bias, queries, blocks, heads, partial):
    tokens = queries.shape[0]
    in_specs = [VMEM] * (2 + len(blocks))
    operands = [bias, queries, *blocks]
    aliases = {}
    if partial is not None:
        aliases = {len(operands): 0}
        operands.append(in_hbm(partial))
        in_specs.append(HBM)
    span = (len(blocks) - 1) * tokens + TILE
    units = len(heads) * tokens // TILE
    return pl.pallas_call(
        functools.partial(attend_kernel, len(blocks), heads[0]),
        in_specs=in_specs,
        out_specs=HBM,
        out_shape=pltpu.HBM((tokens, QH * HD), jnp.bfloat16),
        scratch_shapes=[
            pltpu.VMEM((AHEAD + 1, RATIO * TILE, span), jnp.float32),
            pltpu.VMEM((AHEAD + 1, RATIO * TILE, span), jnp.bfloat16),
            pltpu.VMEM((units, TILE, RATIO * HD), jnp.bfloat16),
            pltpu.SemaphoreType.DMA((units,)),
        ],
        input_output_aliases=aliases,
        compiler_params=pltpu.CompilerParams(vmem_limit_bytes=24 * MIB),
        cost_estimate=pl.CostEstimate(
            flops=6 * tokens * len(heads) * RATIO * HD * span,
            bytes_accessed=4 * tokens * len(heads) * RATIO * HD,
            transcendentals=len(heads) * RATIO * tokens * span,
        ),
        name="attend",
    )(*operands)


def shards(hidden, queries, norm_gain, kv_weight, value_bias, doc_lengths):
    return layer(hidden[0], queries[0], norm_gain, kv_weight, value_bias, doc_lengths)[None]


def layer(hidden, queries, norm_gain, kv_weight, value_bias, doc_lengths):
    tokens = hidden.shape[0]
    parts = lax.axis_size("fsdp")
    length = lax.axis_size("sp")
    held = kv_weight.shape[0]
    pair = 2 if parts % 2 == 0 else 1
    groups = parts // pair
    reach = length // 4
    gain = norm_gain[None]

    arrived = []
    for d in range(1, groups):
        there = [(i, (i + d * pair) % parts) for i in range(parts)]
        arrived.append([])
        for p in range(PIECES):
            sent = away(hidden, gain, parts, pair, held, d, p)
            arrived[-1].append(lax.ppermute(sent, "fsdp", there))
    own, power, kept = home(hidden, gain, kv_weight, parts, pair)
    weights = [kept]
    if pair == 2:
        weights.append(lax.ppermute(kv_weight, "fsdp", [(i, i ^ 1) for i in range(parts)]))
    bias = mask(doc_lengths, tokens, reach)
    mine = project([own], weights, SUMS, jnp.float32)

    early = []
    for d in range(1, groups):
        early.append(project(arrived[d - 1][:1], weights, SUMS[1:], jnp.bfloat16))

    returned = []
    skip = 0
    for c, heads in enumerate(SUMS):
        returned.append([])
        for d in range(1, groups):
            back = [(i, (i - d * pair) % parts) for i in range(parts)]
            for p in range(PIECES if c == 0 else 1):
                if c == 0:
                    part = project(arrived[d - 1][p : p + 1], weights, [heads], jnp.bfloat16)
                else:
                    rows, ready = arrived[d - 1][1:], early[d - 1 : d]
                    part = project(rows, weights, [heads], jnp.bfloat16, ready, skip)
                returned[-1].append(lax.ppermute(part, "fsdp", back))
        skip += 2 * len(heads) * HD if c else 0

    sums = []
    for heads in BLOCKS:
        source = [i for i, some in enumerate(SUMS) if heads[0] in some][0]
        held_heads = SUMS[source]
        own_start = sum(2 * len(some) * HD for some in SUMS[:source])
        first = (heads[0] - held_heads[0]) * HD
        other_columns = (first, first + len(held_heads) * HD)
        own_columns = tuple(own_start + x for x in other_columns)
        sums.append(
            merge(
                mine,
                power,
                value_bias[None],
                returned[source],
                PIECES if source == 0 else 1,
                heads,
                own_columns,
                other_columns,
            )
        )

    out = None
    for c, heads in enumerate(BLOCKS):
        chain = [sums[c]]
        shifts = range(1, reach + 1)
        swaps = reach % 2 == 0 and length % 2 == 0
        if swaps:
            shifts = range(2, reach + 1, 2)
        for b in shifts:
            ahead = [(i, (i + b) % length) for i in range(length)]
            chain.append(lax.ppermute(sums[c], "sp", ahead))
        blocks = chain
        if swaps:
            blocks = [chain[0]]
            swap = [(i, i ^ 1) for i in range(length)]
            for b in range(reach // 2):
                near = lax.ppermute(pick(chain[b], chain[b + 1]), "sp", swap)
                blocks += [near, chain[b + 1]]
        out = attend(bias, queries, blocks[::-1], heads, out)
    return out


def solution(mesh):
    in_specs = (
        P("fsdp", "sp", None),
        P("fsdp", "sp", None),
        P(),
        P("fsdp", None),
        P(),
        P("fsdp", None),
    )
    out_specs = P("fsdp", "sp", None)
    return jax.shard_map(shards, mesh=mesh, in_specs=in_specs, out_specs=out_specs, check_vma=False)
```

time: 271 us -> 86 us (0.32)
  the two profiles are of different devices: /device:TPU:8 before, /device:TPU:0 now
where the time goes in v3:
time: 86 us; the launch traced here: 85.7 us
  waiting for transfers between devices  33 us (38%)
  Pallas kernels  27.1 us (32%)
  starting transfers between devices  25.1 us (29%)
    ppermute x2, waiting for transfers between devices, layer(): arrived[-1].append(lax.ppermute(sent, 'fsdp', there))  22.3 us
    pallas_call x5, Pallas kernels, attend(): pl.pallas_call(functools.partial(attend_kernel, len(blocks), heads[0]), i...  12.8 us
    ppermute x5, starting transfers between devices, layer(): returned[-1].append(lax.ppermute(part, 'fsdp', back))  7.88 us
    ppermute x5, starting transfers between devices, layer(): near = lax.ppermute(pick(chain[b], chain[b + 1]), 'sp', swap)  7.34 us
    pallas_call x7, Pallas kernels, project(): pl.pallas_call(functools.partial(project_kernel, runs, skip, (len(ready),...  6.8 us
    ppermute x5, starting transfers between devices, layer(): chain.append(lax.ppermute(sums[c], 'sp', ahead))  6.7 us
    ppermute x5, waiting for transfers between devices, layer(): returned[-1].append(lax.ppermute(part, 'fsdp', back))  5.42 us
    ppermute x5, waiting for transfers between devices, layer(): chain.append(lax.ppermute(sums[c], 'sp', ahead))  5.27 us
  transfers between devices with their start and end apart: 18, of which 7 were waited for; matrix products, arithmetic and copies ran while one was open for 0% of the time, Pallas kernels for 29%

profile of v3, /device:TPU:0, one launch (start us, length us, event | category | flops | bytes accessed | tf_op | source)
XLA Modules:
  0.0 85.7 jit_solution(1881289722670180299)
XLA Ops:
  0.0 0.5 collective-permute-start
  0.5 1.2 %away.2 = bf16[128,2560]{1,0:T(8,128)(2,1)S(1)} custom-call(bf16[256,5120]{1,0:T(8,128)(2,1)} %bitcast.15, f32[1,5120]{1,0:T(1,128)} %bitcast.18), custom_call_target="tpu_custom_call" | custom-call | tf_op jit(solution)/shard_map/away/pallas_call | solution.py:73
  1.7 2.6 %collective-permute-start.1 = (bf16[128,2560]{1,0:T(8,128)(2,1)S(1)}, bf16[128,2560]{1,0:T(8,128)(2,1)S(1)}, u32[]{:S(2)}, u32[]{:S(2)}) collective-permute-start(bf16[128,2560]{1,0:T(8,128)(2,1)S(1)} %away.2), channel_id=1, source_target_pairs={{0,16},{8,24},{16,0},{24,8},{1,17},{9,25},{17,1},{25,9},{2,18},{10... | collective-permute-start | bytes 1966088 | tf_op jit(solution)/shard_map/ppermute | solution.py:386
  4.3 1.2 %away.3 = bf16[128,2560]{1,0:T(8,128)(2,1)S(1)} custom-call(bf16[256,5120]{1,0:T(8,128)(2,1)} %bitcast.16, f32[1,5120]{1,0:T(1,128)} %bitcast.19), custom_call_target="tpu_custom_call" | custom-call | tf_op jit(solution)/shard_map/away/pallas_call | solution.py:73
  5.5 0.1 collective-permute-start.2
  5.6 3.3 %home.1 = (bf16[256,2560]{1,0:T(8,128)(2,1)S(1)}, f32[256,1]{1,0:T(8,128)S(1)}, bf16[1280,2048]{1,0:T(8,128)(2,1)S(1)}) custom-call(bf16[256,5120]{1,0:T(8,128)(2,1)} %bitcast.17, f32[1,5120]{1,0:T(1,128)} %bitcast.20, bf16[1280,2048]{1,0:T(8,128)(2,1)} %weight_ref.1), custom_call_target="tpu_custom_call" | custom-call | tf_op jit(solution)/shard_map/home/pallas_call | solution.py:115
  9.0 10.9 %collective-permute-done.1.refs_0_ = bf16[128,2560]{1,0:T(8,128)(2,1)S(1)} collective-permute-done((bf16[128,2560]{1,0:T(8,128)(2,1)S(1)}, bf16[128,2560]{1,0:T(8,128)(2,1)S(1)}, u32[]{:S(2)}, u32[]{:S(2)}) %collective-permute-start.1) | collective-permute-done | bytes 655392 | tf_op jit(solution)/shard_map/ppermute | solution.py:386
  19.9 0.0 collective-permute-done.refs_2_.refs_3_
  19.9 0.5 project.12
  20.4 2.1 %collective-permute-start.14 = (bf16[128,512]{1,0:T(8,128)(2,1)S(1)}, bf16[128,512]{1,0:T(8,128)(2,1)S(1)}, u32[]{:S(2)}, u32[]{:S(2)}) collective-permute-start(bf16[128,512]{1,0:T(8,128)(2,1)S(1)} %project.12), channel_id=1, source_target_pairs={{0,16},{8,24},{16,0},{24,8},{1,17},{9,25},{17,1},{25,9},{2,18},{10... | collective-permute-start | bytes 393224 | tf_op jit(solution)/shard_map/ppermute | solution.py:410
  22.5 11.4 %collective-permute-done.2.refs_1_.refs_0_ = bf16[128,2560]{1,0:T(8,128)(2,1)S(1)} collective-permute-done((bf16[128,2560]{1,0:T(8,128)(2,1)S(1)}, bf16[128,2560]{1,0:T(8,128)(2,1)S(1)}, u32[]{:S(2)}, u32[]{:S(2)}) %collective-permute-start.2) | collective-permute-done | bytes 655392 | tf_op jit(solution)/shard_map/ppermute | solution.py:386
  33.9 0.5 project.13
  34.5 2.1 %collective-permute-start.15 = (bf16[128,512]{1,0:T(8,128)(2,1)S(1)}, bf16[128,512]{1,0:T(8,128)(2,1)S(1)}, u32[]{:S(2)}, u32[]{:S(2)}) collective-permute-start(bf16[128,512]{1,0:T(8,128)(2,1)S(1)} %project.13), channel_id=1, source_target_pairs={{0,16},{8,24},{16,0},{24,8},{1,17},{9,25},{17,1},{25,9},{2,18},{10... | collective-permute-start | bytes 393224 | tf_op jit(solution)/shard_map/ppermute | solution.py:410
  36.5 1.2 %project.8.refs_0_ = bf16[128,1536]{1,0:T(8,128)(2,1)S(1)} custom-call(bf16[128,2560]{1,0:T(8,128)(2,1)S(1)} %collective-permute-done.1.refs_0_, bf16[1280,2048]{1,0:T(8,128)(2,1)S(1)} %get-tuple-element.9.refs_1_.refs_2_, bf16[1280,2048]{1,0:T(8,128)(2,1)S(1)} %collective-permute-done.refs_2_.refs_3_), custom_call_target="tpu_custom_call" | custom-call | flops 1006632960 | bytes 7864320 | tf_op jit(solution)/shard_map/project/pallas_call | solution.py:171
  37.8 0.5 project.10
  38.3 0.1 collective-permute-start.8
  38.4 0.5 project.11
  39.0 2.1 %collective-permute-start.11 = (bf16[256,512]{1,0:T(8,128)(2,1)S(1)}, bf16[256,512]{1,0:T(8,128)(2,1)S(1)}, u32[]{:S(2)}, u32[]{:S(2)}) collective-permute-start(bf16[256,512]{1,0:T(8,128)(2,1)S(1)} %project.11), channel_id=1, source_target_pairs={{0,16},{8,24},{16,0},{24,8},{1,17},{9,25},{17,1},{25,9},{2,18},{10... | collective-permute-start | bytes 786440 | tf_op jit(solution)/shard_map/ppermute | solution.py:410
  41.0 0.0 copy-start.1
  41.0 2.9 %project.7.mine_ref = f32[256,2048]{1,0:T(8,128)S(1)} custom-call(bf16[256,2560]{1,0:T(8,128)(2,1)S(1)} %get-tuple-element.8.refs_0_, bf16[1280,2048]{1,0:T(8,128)(2,1)S(1)} %get-tuple-element.9.refs_1_.refs_2_, bf16[1280,2048]{1,0:T(8,128)(2,1)S(1)} %collective-permute-done.refs_2_.refs_3_), custom_call_target="tpu_custom_call" | custom-call | flops 2684354560 | bytes 10485760 | tf_op jit(solution)/shard_map/project/pallas_call | solution.py:171
  43.9 0.0 collective-permute-done.14.refs_0_
  43.9 0.0 collective-permute-done.15.refs_1_
  43.9 0.0 copy-done.1
  43.9 0.1 merge.9.even_ref.refs_2_
  44.1 1.6 %collective-permute-start.16 = (bf16[256,512]{1,0:T(8,128)(2,1)S(1)}, bf16[256,512]{1,0:T(8,128)(2,1)S(1)}, u32[]{:S(2)}, u32[]{:S(2)}) collective-permute-start(bf16[256,512]{1,0:T(8,128)(2,1)S(1)} %merge.9.even_ref.refs_2_), channel_id=1, source_target_pairs={{0,2},{1,3},{2,4},{3,5},{4,6},{5,7},{6,0},{7,1},{8,10},{9,11},{10,... | collective-permute-start | bytes 786440 | tf_op jit(solution)/shard_map/ppermute | solution.py:443
  45.7 5.4 %collective-permute-done.11.refs_0_ = bf16[256,512]{1,0:T(8,128)(2,1)S(1)} collective-permute-done((bf16[256,512]{1,0:T(8,128)(2,1)S(1)}, bf16[256,512]{1,0:T(8,128)(2,1)S(1)}, u32[]{:S(2)}, u32[]{:S(2)}) %collective-permute-start.11) | collective-permute-done | bytes 262176 | tf_op jit(solution)/shard_map/ppermute | solution.py:410
  51.1 0.1 merge.8.even_ref.refs_2_
  51.3 1.7 %collective-permute-start.12 = (bf16[256,512]{1,0:T(8,128)(2,1)S(1)}, bf16[256,512]{1,0:T(8,128)(2,1)S(1)}, u32[]{:S(2)}, u32[]{:S(2)}) collective-permute-start(bf16[256,512]{1,0:T(8,128)(2,1)S(1)} %merge.8.even_ref.refs_2_), channel_id=1, source_target_pairs={{0,2},{1,3},{2,4},{3,5},{4,6},{5,7},{6,0},{7,1},{8,10},{9,11},{10,... | collective-permute-start | bytes 786440 | tf_op jit(solution)/shard_map/ppermute | solution.py:443
  53.0 0.5 project.9
  53.6 1.6 %collective-permute-start.3 = (bf16[256,512]{1,0:T(8,128)(2,1)S(1)}, bf16[256,512]{1,0:T(8,128)(2,1)S(1)}, u32[]{:S(2)}, u32[]{:S(2)}) collective-permute-start(bf16[256,512]{1,0:T(8,128)(2,1)S(1)} %project.9), channel_id=1, source_target_pairs={{0,16},{8,24},{16,0},{24,8},{1,17},{9,25},{17,1},{25,9},{2,18},{10... | collective-permute-start | bytes 786440 | tf_op jit(solution)/shard_map/ppermute | solution.py:410
  55.1 0.0 collective-permute-done.8.refs_0_
  55.1 0.1 merge.7.even_ref.refs_2_
  55.3 1.6 %collective-permute-start.9 = (bf16[256,512]{1,0:T(8,128)(2,1)S(1)}, bf16[256,512]{1,0:T(8,128)(2,1)S(1)}, u32[]{:S(2)}, u32[]{:S(2)}) collective-permute-start(bf16[256,512]{1,0:T(8,128)(2,1)S(1)} %merge.7.even_ref.refs_2_), channel_id=1, source_target_pairs={{0,2},{1,3},{2,4},{3,5},{4,6},{5,7},{6,0},{7,1},{8,10},{9,11},{10,... | collective-permute-start | bytes 786440 | tf_op jit(solution)/shard_map/ppermute | solution.py:443
  56.9 0.0 collective-permute-done.16.odd_ref.refs_0_
  57.0 1.6 %collective-permute-start.17 = (bf16[256,512]{1,0:T(8,128)(2,1)S(1)}, bf16[256,512]{1,0:T(8,128)(2,1)S(1)}, u32[]{:S(2)}, u32[]{:S(2)}) collective-permute-start(bf16[256,512]{1,0:T(8,128)(2,1)S(1)} %pick.9), channel_id=1, source_target_pairs={{0,1},{1,0},{2,3},{3,2},{4,5},{5,4},{6,7},{7,6},{8,9},{9,8},{10,11... | collective-permute-start | bytes 786440 | tf_op jit(solution)/shard_map/ppermute | solution.py:449
  58.5 2.6 %collective-permute-done.12.odd_ref.refs_0_ = bf16[256,512]{1,0:T(8,128)(2,1)S(1)} collective-permute-done((bf16[256,512]{1,0:T(8,128)(2,1)S(1)}, bf16[256,512]{1,0:T(8,128)(2,1)S(1)}, u32[]{:S(2)}, u32[]{:S(2)}) %collective-permute-start.12) | collective-permute-done | bytes 262176 | tf_op jit(solution)/shard_map/ppermute | solution.py:443
  61.2 1.6 %collective-permute-start.13 = (bf16[256,512]{1,0:T(8,128)(2,1)S(1)}, bf16[256,512]{1,0:T(8,128)(2,1)S(1)}, u32[]{:S(2)}, u32[]{:S(2)}) collective-permute-start(bf16[256,512]{1,0:T(8,128)(2,1)S(1)} %pick.8), channel_id=1, source_target_pairs={{0,1},{1,0},{2,3},{3,2},{4,5},{5,4},{6,7},{7,6},{8,9},{9,8},{10,11... | collective-permute-start | bytes 786440 | tf_op jit(solution)/shard_map/ppermute | solution.py:449
  62.7 0.0 collective-permute-done.3.refs_0_
  62.7 0.1 merge.5.even_ref.refs_2_
  62.9 0.0 copy-start.2
  62.9 0.0 copy-start
  62.9 0.1 collective-permute-start.4
  63.0 0.1 merge.6.even_ref.refs_2_
  63.1 1.7 %collective-permute-start.6 = (bf16[256,256]{1,0:T(8,128)(2,1)S(1)}, bf16[256,256]{1,0:T(8,128)(2,1)S(1)}, u32[]{:S(2)}, u32[]{:S(2)}) collective-permute-start(bf16[256,256]{1,0:T(8,128)(2,1)S(1)} %merge.6.even_ref.refs_2_), channel_id=1, source_target_pairs={{0,2},{1,3},{2,4},{3,5},{4,6},{5,7},{6,0},{7,1},{8,10},{9,11},{10,... | collective-permute-start | bytes 393224 | tf_op jit(solution)/shard_map/ppermute | solution.py:443
  64.8 2.0 %collective-permute-done.9.odd_ref.refs_0_ = bf16[256,512]{1,0:T(8,128)(2,1)S(1)} collective-permute-done((bf16[256,512]{1,0:T(8,128)(2,1)S(1)}, bf16[256,512]{1,0:T(8,128)(2,1)S(1)}, u32[]{:S(2)}, u32[]{:S(2)}) %collective-permute-start.9) | collective-permute-done | bytes 262176 | tf_op jit(solution)/shard_map/ppermute | solution.py:443
  66.8 1.6 %collective-permute-start.10 = (bf16[256,512]{1,0:T(8,128)(2,1)S(1)}, bf16[256,512]{1,0:T(8,128)(2,1)S(1)}, u32[]{:S(2)}, u32[]{:S(2)}) collective-permute-start(bf16[256,512]{1,0:T(8,128)(2,1)S(1)} %pick.7), channel_id=1, source_target_pairs={{0,1},{1,0},{2,3},{3,2},{4,5},{5,4},{6,7},{7,6},{8,9},{9,8},{10,11... | collective-permute-start | bytes 786440 | tf_op jit(solution)/shard_map/ppermute | solution.py:449
  68.3 0.0 copy-done.2
  68.4 0.8 mask.1.bias_ref
  69.2 0.6 collective-permute-done.4.odd_ref.refs_0_
  69.7 1.3 %collective-permute-start.5 = (bf16[256,256]{1,0:T(8,128)(2,1)S(1)}, bf16[256,256]{1,0:T(8,128)(2,1)S(1)}, u32[]{:S(2)}, u32[]{:S(2)}) collective-permute-start(bf16[256,256]{1,0:T(8,128)(2,1)S(1)} %pick.5), channel_id=1, source_target_pairs={{0,1},{1,0},{2,3},{3,2},{4,5},{5,4},{6,7},{7,6},{8,9},{9,8},{10,11... | collective-permute-start | bytes 393224 | tf_op jit(solution)/shard_map/ppermute | solution.py:449
  71.1 0.1 collective-permute-done.6.odd_ref.refs_0_
  71.1 0.2 pick.6
  71.3 1.3 %collective-permute-start.7 = (bf16[256,256]{1,0:T(8,128)(2,1)S(1)}, bf16[256,256]{1,0:T(8,128)(2,1)S(1)}, u32[]{:S(2)}, u32[]{:S(2)}) collective-permute-start(bf16[256,256]{1,0:T(8,128)(2,1)S(1)} %pick.6), channel_id=1, source_target_pairs={{0,1},{1,0},{2,3},{3,2},{4,5},{5,4},{6,7},{7,6},{8,9},{9,8},{10,11... | collective-permute-start | bytes 393224 | tf_op jit(solution)/shard_map/ppermute | solution.py:449
  72.7 0.0 collective-permute-done.17.refs_1_
  72.7 0.0 copy-done
  72.7 2.9 %attend.5.refs_3_ = bf16[256,4096]{1,0:T(8,128)(2,1)} custom-call(f32[256,768]{1,0:T(8,128)S(1)} %mask.1.bias_ref, bf16[256,4096]{1,0:T(8,128)(2,1)S(1)} %bitcast.5, bf16[256,512]{1,0:T(8,128)(2,1)S(1)} %collective-permute-done.16.odd_ref.refs_0_, bf16[256,512]{1,0:T(8,128)(2,1)S(1)} %collective-permute-done.17.refs_1_, ...), custom_call_target="tpu_custom_call" | custom-call | flops 1006632960 | bytes 1048576 | tf_op jit(solution)/shard_map/attend/pallas_call | solution.py:344
  75.6 0.0 collective-permute-done.13.refs_1_
  75.6 2.9 %attend.6.refs_3_ = bf16[256,4096]{1,0:T(8,128)(2,1)} custom-call(f32[256,768]{1,0:T(8,128)S(1)} %mask.1.bias_ref, bf16[256,4096]{1,0:T(8,128)(2,1)S(1)} %bitcast.6, bf16[256,512]{1,0:T(8,128)(2,1)S(1)} %collective-permute-done.12.odd_ref.refs_0_, bf16[256,512]{1,0:T(8,128)(2,1)S(1)} %collective-permute-done.13.refs_1_, ...), custom_call_target="tpu_custom_call", output_to_operand_aliasing={{}: (5, {})} | custom-call | flops 1006632960 | bytes 1048576 | tf_op jit(solution)/shard_map/attend/pallas_call | solution.py:344
  78.5 0.0 collective-permute-done.10.refs_1_
  78.5 2.9 %attend.7.refs_3_ = bf16[256,4096]{1,0:T(8,128)(2,1)} custom-call(f32[256,768]{1,0:T(8,128)S(1)} %mask.1.bias_ref, bf16[256,4096]{1,0:T(8,128)(2,1)S(1)} %bitcast.7, bf16[256,512]{1,0:T(8,128)(2,1)S(1)} %collective-permute-done.9.odd_ref.refs_0_, bf16[256,512]{1,0:T(8,128)(2,1)S(1)} %collective-permute-done.10.refs_1_, ...), custom_call_target="tpu_custom_call", output_to_operand_aliasing={{}: (5, {})} | custom-call | flops 1006632960 | bytes 1048576 | tf_op jit(solution)/shard_map/attend/pallas_call | solution.py:344
  81.5 0.0 collective-permute-done.7.refs_1_
  81.5 2.0 %attend.8.refs_3_ = bf16[256,4096]{1,0:T(8,128)(2,1)} custom-call(f32[256,768]{1,0:T(8,128)S(1)} %mask.1.bias_ref, bf16[256,4096]{1,0:T(8,128)(2,1)S(1)} %bitcast.8, bf16[256,256]{1,0:T(8,128)(2,1)S(1)} %collective-permute-done.6.odd_ref.refs_0_, bf16[256,256]{1,0:T(8,128)(2,1)S(1)} %collective-permute-done.7.refs_1_, ...), custom_call_target="tpu_custom_call", output_to_operand_aliasing={{}: (5, {})} | custom-call | flops 503316480 | bytes 524288 | tf_op jit(solution)/shard_map/attend/pallas_call | solution.py:344
  83.5 0.0 collective-permute-done.5.refs_1_
  83.5 2.0 %attend.9 = bf16[256,4096]{1,0:T(8,128)(2,1)} custom-call(f32[256,768]{1,0:T(8,128)S(1)} %mask.1.bias_ref, bf16[256,4096]{1,0:T(8,128)(2,1)S(1)} %bitcast.9, bf16[256,256]{1,0:T(8,128)(2,1)S(1)} %collective-permute-done.4.odd_ref.refs_0_, bf16[256,256]{1,0:T(8,128)(2,1)S(1)} %collective-permute-done.5.refs_1_, ...), custom_call_target="tpu_custom_call", output_to_operand_aliasing={{}: (5, {})} | custom-call | flops 503316480 | bytes 524288 | tf_op jit(solution)/shard_map/attend/pallas_call | solution.py:344
  (4 shorter events, 0.1 us)
Async XLA Ops:
  0.0 19.9 %collective-permute-start = (bf16[1280,2048]{1,0:T(8,128)(2,1)}, bf16[1280,2048]{1,0:T(8,128)(2,1)S(1)}, u32[]{:S(2)}, u32[]{:S(2)}) collective-permute-start(bf16[1280,2048]{1,0:T(8,128)(2,1)} %weight_ref.1), channel_id=1, source_target_pairs={{0,8},{8,0},{16,24},{24,16},{1,9},{9,1},{17,25},{25,17},{2,10},{10... | collective-permute-start | bytes 15728648 | tf_op jit(solution)/shard_map/ppermute | solution.py:390
  1.7 18.2 %collective-permute-start.1 = (bf16[128,2560]{1,0:T(8,128)(2,1)S(1)}, bf16[128,2560]{1,0:T(8,128)(2,1)S(1)}, u32[]{:S(2)}, u32[]{:S(2)}) collective-permute-start(bf16[128,2560]{1,0:T(8,128)(2,1)S(1)} %away.2), channel_id=1, source_target_pairs={{0,16},{8,24},{16,0},{24,8},{1,17},{9,25},{17,1},{25,9},{2,18},{10... | collective-permute-start | bytes 1966088 | tf_op jit(solution)/shard_map/ppermute | solution.py:386
  5.5 28.4 %collective-permute-start.2 = (bf16[128,2560]{1,0:T(8,128)(2,1)S(1)}, bf16[128,2560]{1,0:T(8,128)(2,1)S(1)}, u32[]{:S(2)}, u32[]{:S(2)}) collective-permute-start(bf16[128,2560]{1,0:T(8,128)(2,1)S(1)} %away.3), channel_id=1, source_target_pairs={{0,16},{8,24},{16,0},{24,8},{1,17},{9,25},{17,1},{25,9},{2,18},{10... | collective-permute-start | bytes 1966088 | tf_op jit(solution)/shard_map/ppermute | solution.py:386
  20.4 23.5 %collective-permute-start.14 = (bf16[128,512]{1,0:T(8,128)(2,1)S(1)}, bf16[128,512]{1,0:T(8,128)(2,1)S(1)}, u32[]{:S(2)}, u32[]{:S(2)}) collective-permute-start(bf16[128,512]{1,0:T(8,128)(2,1)S(1)} %project.12), channel_id=1, source_target_pairs={{0,16},{8,24},{16,0},{24,8},{1,17},{9,25},{17,1},{25,9},{2,18},{10... | collective-permute-start | bytes 393224 | tf_op jit(solution)/shard_map/ppermute | solution.py:410
  34.5 9.5 %collective-permute-start.15 = (bf16[128,512]{1,0:T(8,128)(2,1)S(1)}, bf16[128,512]{1,0:T(8,128)(2,1)S(1)}, u32[]{:S(2)}, u32[]{:S(2)}) collective-permute-start(bf16[128,512]{1,0:T(8,128)(2,1)S(1)} %project.13), channel_id=1, source_target_pairs={{0,16},{8,24},{16,0},{24,8},{1,17},{9,25},{17,1},{25,9},{2,18},{10... | collective-permute-start | bytes 393224 | tf_op jit(solution)/shard_map/ppermute | solution.py:410
  38.3 16.8 %collective-permute-start.8 = (bf16[256,512]{1,0:T(8,128)(2,1)S(1)}, bf16[256,512]{1,0:T(8,128)(2,1)S(1)}, u32[]{:S(2)}, u32[]{:S(2)}) collective-permute-start(bf16[256,512]{1,0:T(8,128)(2,1)S(1)} %project.10), channel_id=1, source_target_pairs={{0,16},{8,24},{16,0},{24,8},{1,17},{9,25},{17,1},{25,9},{2,18},{10... | collective-permute-start | bytes 786440 | tf_op jit(solution)/shard_map/ppermute | solution.py:410
  39.0 12.2 %collective-permute-start.11 = (bf16[256,512]{1,0:T(8,128)(2,1)S(1)}, bf16[256,512]{1,0:T(8,128)(2,1)S(1)}, u32[]{:S(2)}, u32[]{:S(2)}) collective-permute-start(bf16[256,512]{1,0:T(8,128)(2,1)S(1)} %project.11), channel_id=1, source_target_pairs={{0,16},{8,24},{16,0},{24,8},{1,17},{9,25},{17,1},{25,9},{2,18},{10... | collective-permute-start | bytes 786440 | tf_op jit(solution)/shard_map/ppermute | solution.py:410
  41.0 2.9 %copy-start.1 = (f32[1024]{0:T(1024)S(1)}, f32[1024]{0:T(1024)}, u32[]{:S(2)}) copy-start(f32[1024]{0:T(1024)} %param.10) | copy-start | bytes 12292
  44.1 12.8 %collective-permute-start.16 = (bf16[256,512]{1,0:T(8,128)(2,1)S(1)}, bf16[256,512]{1,0:T(8,128)(2,1)S(1)}, u32[]{:S(2)}, u32[]{:S(2)}) collective-permute-start(bf16[256,512]{1,0:T(8,128)(2,1)S(1)} %merge.9.even_ref.refs_2_), channel_id=1, source_target_pairs={{0,2},{1,3},{2,4},{3,5},{4,6},{5,7},{6,0},{7,1},{8,10},{9,11},{10,... | collective-permute-start | bytes 786440 | tf_op jit(solution)/shard_map/ppermute | solution.py:443
  51.3 9.9 %collective-permute-start.12 = (bf16[256,512]{1,0:T(8,128)(2,1)S(1)}, bf16[256,512]{1,0:T(8,128)(2,1)S(1)}, u32[]{:S(2)}, u32[]{:S(2)}) collective-permute-start(bf16[256,512]{1,0:T(8,128)(2,1)S(1)} %merge.8.even_ref.refs_2_), channel_id=1, source_target_pairs={{0,2},{1,3},{2,4},{3,5},{4,6},{5,7},{6,0},{7,1},{8,10},{9,11},{10,... | collective-permute-start | bytes 786440 | tf_op jit(solution)/shard_map/ppermute | solution.py:443
  53.6 9.2 %collective-permute-start.3 = (bf16[256,512]{1,0:T(8,128)(2,1)S(1)}, bf16[256,512]{1,0:T(8,128)(2,1)S(1)}, u32[]{:S(2)}, u32[]{:S(2)}) collective-permute-start(bf16[256,512]{1,0:T(8,128)(2,1)S(1)} %project.9), channel_id=1, source_target_pairs={{0,16},{8,24},{16,0},{24,8},{1,17},{9,25},{17,1},{25,9},{2,18},{10... | collective-permute-start | bytes 786440 | tf_op jit(solution)/shard_map/ppermute | solution.py:410
  55.3 11.5 %collective-permute-start.9 = (bf16[256,512]{1,0:T(8,128)(2,1)S(1)}, bf16[256,512]{1,0:T(8,128)(2,1)S(1)}, u32[]{:S(2)}, u32[]{:S(2)}) collective-permute-start(bf16[256,512]{1,0:T(8,128)(2,1)S(1)} %merge.7.even_ref.refs_2_), channel_id=1, source_target_pairs={{0,2},{1,3},{2,4},{3,5},{4,6},{5,7},{6,0},{7,1},{8,10},{9,11},{10,... | collective-permute-start | bytes 786440 | tf_op jit(solution)/shard_map/ppermute | solution.py:443
  57.0 15.7 %collective-permute-start.17 = (bf16[256,512]{1,0:T(8,128)(2,1)S(1)}, bf16[256,512]{1,0:T(8,128)(2,1)S(1)}, u32[]{:S(2)}, u32[]{:S(2)}) collective-permute-start(bf16[256,512]{1,0:T(8,128)(2,1)S(1)} %pick.9), channel_id=1, source_target_pairs={{0,1},{1,0},{2,3},{3,2},{4,5},{5,4},{6,7},{7,6},{8,9},{9,8},{10,11... | collective-permute-start | bytes 786440 | tf_op jit(solution)/shard_map/ppermute | solution.py:449
  61.2 14.4 %collective-permute-start.13 = (bf16[256,512]{1,0:T(8,128)(2,1)S(1)}, bf16[256,512]{1,0:T(8,128)(2,1)S(1)}, u32[]{:S(2)}, u32[]{:S(2)}) collective-permute-start(bf16[256,512]{1,0:T(8,128)(2,1)S(1)} %pick.8), channel_id=1, source_target_pairs={{0,1},{1,0},{2,3},{3,2},{4,5},{5,4},{6,7},{7,6},{8,9},{9,8},{10,11... | collective-permute-start | bytes 786440 | tf_op jit(solution)/shard_map/ppermute | solution.py:449
  62.9 5.5 %copy-start.2 = (s32[1,16]{1,0:T(1,128)S(1)}, s32[1,16]{1,0:T(1,128)}, u32[]{:S(2)}) copy-start(s32[1,16]{1,0:T(1,128)} %lengths_ref.1) | copy-start | bytes 196
  62.9 9.8 %copy-start = (bf16[1,256,4096]{2,1,0:T(8,128)(2,1)S(1)}, bf16[1,256,4096]{2,1,0:T(8,128)(2,1)}, u32[]{:S(2)}) copy-start(bf16[1,256,4096]{2,1,0:T(8,128)(2,1)} %param.7) | copy-start | bytes 6291460
  62.9 6.8 %collective-permute-start.4 = (bf16[256,256]{1,0:T(8,128)(2,1)S(1)}, bf16[256,256]{1,0:T(8,128)(2,1)S(1)}, u32[]{:S(2)}, u32[]{:S(2)}) collective-permute-start(bf16[256,256]{1,0:T(8,128)(2,1)S(1)} %merge.5.even_ref.refs_2_), channel_id=1, source_target_pairs={{0,2},{1,3},{2,4},{3,5},{4,6},{5,7},{6,0},{7,1},{8,10},{9,11},{10,... | collective-permute-start | bytes 393224 | tf_op jit(solution)/shard_map/ppermute | solution.py:443
  63.1 8.0 %collective-permute-start.6 = (bf16[256,256]{1,0:T(8,128)(2,1)S(1)}, bf16[256,256]{1,0:T(8,128)(2,1)S(1)}, u32[]{:S(2)}, u32[]{:S(2)}) collective-permute-start(bf16[256,256]{1,0:T(8,128)(2,1)S(1)} %merge.6.even_ref.refs_2_), channel_id=1, source_target_pairs={{0,2},{1,3},{2,4},{3,5},{4,6},{5,7},{6,0},{7,1},{8,10},{9,11},{10,... | collective-permute-start | bytes 393224 | tf_op jit(solution)/shard_map/ppermute | solution.py:443
  66.8 11.7 %collective-permute-start.10 = (bf16[256,512]{1,0:T(8,128)(2,1)S(1)}, bf16[256,512]{1,0:T(8,128)(2,1)S(1)}, u32[]{:S(2)}, u32[]{:S(2)}) collective-permute-start(bf16[256,512]{1,0:T(8,128)(2,1)S(1)} %pick.7), channel_id=1, source_target_pairs={{0,1},{1,0},{2,3},{3,2},{4,5},{5,4},{6,7},{7,6},{8,9},{9,8},{10,11... | collective-permute-start | bytes 786440 | tf_op jit(solution)/shard_map/ppermute | solution.py:449
  69.7 13.8 %collective-permute-start.5 = (bf16[256,256]{1,0:T(8,128)(2,1)S(1)}, bf16[256,256]{1,0:T(8,128)(2,1)S(1)}, u32[]{:S(2)}, u32[]{:S(2)}) collective-permute-start(bf16[256,256]{1,0:T(8,128)(2,1)S(1)} %pick.5), channel_id=1, source_target_pairs={{0,1},{1,0},{2,3},{3,2},{4,5},{5,4},{6,7},{7,6},{8,9},{9,8},{10,11... | collective-permute-start | bytes 393224 | tf_op jit(solution)/shard_map/ppermute | solution.py:449
  71.3 10.1 %collective-permute-start.7 = (bf16[256,256]{1,0:T(8,128)(2,1)S(1)}, bf16[256,256]{1,0:T(8,128)(2,1)S(1)}, u32[]{:S(2)}, u32[]{:S(2)}) collective-permute-start(bf16[256,256]{1,0:T(8,128)(2,1)S(1)} %pick.6), channel_id=1, source_target_pairs={{0,1},{1,0},{2,3},{3,2},{4,5},{5,4},{6,7},{7,6},{8,9},{9,8},{10,11... | collective-permute-start | bytes 393224 | tf_op jit(solution)/shard_map/ppermute | solution.py:449

commit v4 on v3

--- a/solution.py
+++ b/solution.py
@@ -16,6 +16,7 @@
 SUMS = ((0, 1), (2, 3), (4, 5), (6, 7))
 BLOCKS = ((0, 1), (2, 3), (4, 5), (6,), (7,))
 PIECES = 2
+FIRST = 3, 4
 TILE = 128
 STRIP = 32
 AHEAD = 2
@@ -26,6 +27,11 @@
 HBM = pl.BlockSpec(memory_space=pltpu.HBM)
 
 
+def across(place, ahead, parts, pair):
+    group, core = divmod(place, pair)
+    return (group + ahead) % (parts // pair) * pair + (pair - 1 - core)
+
+
 def in_hbm(value):
     return pltpu.with_memory_space_constraint(value, pltpu.HBM)
 
@@ -52,11 +58,16 @@
             out_ref[:, b : b + held] = scaled.astype(jnp.bfloat16)
 
 
-def away_kernel(parts, pair, ahead, piece, hidden_ref, gain_ref, out_ref, rows, gains, sems):
+def bounds_of(tokens):
+    cut = tokens * FIRST[0] // FIRST[1]
+    return (0, cut, tokens)
+
+
+def away_kernel(parts, pair, ahead, start, hidden_ref, gain_ref, out_ref, rows, gains, sems):
     step, width = rows.shape
     first, core = place_of(parts, pair, ahead, width // pair)
     columns = pl.ds(first, width)
-    some = pl.ds(piece * step, step)
+    some = pl.ds(start, step)
     copies = [
         pltpu.make_async_copy(gain_ref.at[:, columns], gains, sems.at[0]),
         pltpu.make_async_copy(hidden_ref.at[some, columns], rows, sems.at[1]),
@@ -65,22 +76,23 @@
         copy.start()
     for copy in copies:
         copy.wait()
-    put_scaled(out_ref, rows, gains, slice(None), core)
+    put_scaled(out_ref, rows, gains, slice(None), pair - 1 - core)
 
 
 def away(hidden, gain, parts, pair, held, ahead, piece):
-    step, width = hidden.shape[0] // PIECES, pair * held
-    return pl.pallas_call(
-        functools.partial(away_kernel, parts, pair, ahead, piece),
+    start, stop = bounds_of(hidden.shape[0])[piece : piece + 2]
+    step, width = stop - start, pair * held
+    return pl.pallas_call(
+        functools.partial(away_kernel, parts, pair, ahead, start),
         in_specs=[HBM, HBM],
         out_specs=VMEM,
-        out_shape=jax.ShapeDtypeStruct((step, width), jnp.bfloat16),
+        out_shape=pltpu.VMEM((step, width), jnp.bfloat16),
         scratch_shapes=[
             pltpu.VMEM((step, width), jnp.bfloat16),
             pltpu.VMEM((1, width), jnp.float32),
             pltpu.SemaphoreType.DMA((2,)),
         ],
-        compiler_params=pltpu.CompilerParams(vmem_limit_bytes=8 * MIB),
+        compiler_params=pltpu.CompilerParams(vmem_limit_bytes=58 * MIB),
         name="away",
     )(in_hbm(hidden), in_hbm(gain))
 
@@ -186,9 +198,9 @@
 def merge_kernel(heads, own, other, pieces, mine_ref, power_ref, bias_ref, *refs):
     parts, out_ref = refs[:-1], refs[-1]
     width = len(heads) * HD
-    step = out_ref.shape[0] // pieces
+    bounds = bounds_of(out_ref.shape[0]) if pieces > 1 else (0, out_ref.shape[0])
     for piece in range(pieces):
-        some = slice(piece * step, (piece + 1) * step)
+        some = slice(bounds[piece], bounds[piece + 1])
         power = power_ref[some, :]
         for half in range(2):
             total = mine_ref[some, own[half] : own[half] + width]
@@ -262,8 +274,29 @@
     )(lengths)
 
 
-def attend_kernel(count, first, bias_ref, query_ref, *refs):
-    blocks, (out_ref, scores, probs, tiles, sems) = refs[:count], refs[-5:]
+def flush(tiles, out_ref, sems, first):
+    per_head = out_ref.shape[0] // TILE
+    copies = []
+    for u in range(tiles.shape[0]):
+        t = u % per_head * TILE
+        wide = (first + u // per_head) * RATIO * HD
+        place = out_ref.at[t : t + TILE, wide : wide + RATIO * HD]
+        copies.append(pltpu.make_async_copy(tiles.at[u], place, sems.at[u]))
+    return copies
+
+
+def attend_kernel(count, first, before, aliased, last, bias_ref, query_ref, *refs):
+    blocks, refs = refs[:count], list(refs[count:])
+    out_ref, copies = None, []
+    if before is not None:
+        older = refs.pop(0)
+        if aliased:
+            refs.pop(0)
+        out_ref = refs.pop(0)
+        copies = flush(older, out_ref, refs[-1], before)
+        for copy in copies:
+            copy.start()
+    tiles, scores, probs = refs[:3]
     tokens = query_ref.shape[0]
     heads = blocks[0].shape[1] // (2 * HD)
     span = scores.shape[2]
@@ -309,49 +342,72 @@
                 probs[u % buffers, :, at : at + z - a], value, preferred_element_type=jnp.float32
             )
             total = term if total is None else total + term
-        result = (total[:, :HD] / total[:, HD:]).astype(out_ref.dtype)
+        result = (total[:, :HD] / total[:, HD:]).astype(tiles.dtype)
         for h in range(RATIO):
             tiles[u, :, h * HD : (h + 1) * HD] = result[h * TILE : (h + 1) * TILE]
-        wide = (first + head) * RATIO * HD
-        place = out_ref.at[t : t + TILE, wide : wide + RATIO * HD]
-        copy = pltpu.make_async_copy(tiles.at[u], place, sems.at[u])
-        copy.start()
-        return copy
-
+
+    ours = flush(tiles, out_ref, refs[3], first) if last else []
     for u in range(min(AHEAD, len(units))):
         score(u)
-    copies = []
     for u in range(len(units)):
         if u + AHEAD < len(units):
             score(u + AHEAD)
         soften(u)
-        copies.append(blend(u))
-    for copy in copies:
+        blend(u)
+        if last:
+            ours[u].start()
+    for copy in copies + ours:
         copy.wait()
 
 
-def attend(bias, queries, blocks, heads, partial):
+def attend(bias, queries, blocks, heads, before, last):
     tokens = queries.shape[0]
-    in_specs = [VMEM] * (2 + len(blocks))
     operands = [bias, queries, *blocks]
-    aliases = {}
-    if partial is not None:
-        aliases = {len(operands): 0}
-        operands.append(in_hbm(partial))
-        in_specs.append(HBM)
+    in_specs = [VMEM] * len(operands)
     span = (len(blocks) - 1) * tokens + TILE
     units = len(heads) * tokens // TILE
-    return pl.pallas_call(
-        functools.partial(attend_kernel, len(blocks), heads[0]),
+    tile = (TILE, RATIO * HD)
+    aliases = {}
+    out_specs, out_shape, scratch = [], [], []
+    older_heads = None
+    older_units = 0
+    if before is not None:
+        older_heads, older, partial = before
+        older_units = older.shape[0]
+        operands.append(older)
+        in_specs.append(VMEM)
+        if partial is not None:
+            aliases = {len(operands): 0}
+            operands.append(in_hbm(partial))
+            in_specs.append(HBM)
+        out_specs.append(HBM)
+        out_shape.append(pltpu.HBM((tokens, QH * HD), jnp.bfloat16))
+    if last:
+        scratch.append(pltpu.VMEM((units, *tile), jnp.bfloat16))
+    else:
+        out_specs.append(VMEM)
+        out_shape.append(pltpu.VMEM((units, *tile), jnp.bfloat16))
+    scratch += [
+        pltpu.VMEM((AHEAD + 1, RATIO * TILE, span), jnp.float32),
+        pltpu.VMEM((AHEAD + 1, RATIO * TILE, span), jnp.bfloat16),
+    ]
+    if last:
+        scratch.append(pltpu.SemaphoreType.DMA((units,)))
+    if before is not None:
+        scratch.append(pltpu.SemaphoreType.DMA((older_units,)))
+    return pl.pallas_call(
+        functools.partial(
+            attend_kernel,
+            len(blocks),
+            heads[0],
+            None if before is None else older_heads[0],
+            bool(aliases),
+            last,
+        ),
         in_specs=in_specs,
-        out_specs=HBM,
-        out_shape=pltpu.HBM((tokens, QH * HD), jnp.bfloat16),
-        scratch_shapes=[
-            pltpu.VMEM((AHEAD + 1, RATIO * TILE, span), jnp.float32),
-            pltpu.VMEM((AHEAD + 1, RATIO * TILE, span), jnp.bfloat16),
-            pltpu.VMEM((units, TILE, RATIO * HD), jnp.bfloat16),
-            pltpu.SemaphoreType.DMA((units,)),
-        ],
+        out_specs=out_specs,
+        out_shape=out_shape,
+        scratch_shapes=scratch,
         input_output_aliases=aliases,
         compiler_params=pltpu.CompilerParams(vmem_limit_bytes=24 * MIB),
         cost_estimate=pl.CostEstimate(
@@ -379,7 +435,7 @@
 
     arrived = []
     for d in range(1, groups):
-        there = [(i, (i + d * pair) % parts) for i in range(parts)]
+        there = [(i, across(i, d, parts, pair)) for i in range(parts)]
         arrived.append([])
         for p in range(PIECES):
             sent = away(hidden, gain, parts, pair, held, d, p)
@@ -400,7 +456,7 @@
     for c, heads in enumerate(SUMS):
         returned.append([])
         for d in range(1, groups):
-            back = [(i, (i - d * pair) % parts) for i in range(parts)]
+            back = [(across(i, d, parts, pair), i) for i in range(parts)]
             for p in range(PIECES if c == 0 else 1):
                 if c == 0:
                     part = project(arrived[d - 1][p : p + 1], weights, [heads], jnp.bfloat16)
@@ -431,7 +487,7 @@
             )
         )
 
-    out = None
+    before = None
     for c, heads in enumerate(BLOCKS):
         chain = [sums[c]]
         shifts = range(1, reach + 1)
@@ -448,8 +504,10 @@
             for b in range(reach // 2):
                 near = lax.ppermute(pick(chain[b], chain[b + 1]), "sp", swap)
                 blocks += [near, chain[b + 1]]
-        out = attend(bias, queries, blocks[::-1], heads, out)
-    return out
+        last = c == len(BLOCKS) - 1
+        results = attend(bias, queries, blocks[::-1], heads, before, last)
+        before = (heads, results[-1], results[0] if before is not None else None)
+    return results[0]
 
 
 def solution(mesh):

time: 86 us -> 91.5 us (1.064)
  waiting for transfers between devices: 33 us -> 40.5 us
  starting transfers between devices: 25.1 us -> 21.4 us
  Pallas kernels: 27.1 us -> 28.9 us
    ppermute x5, starting transfers between devices: 7.88 us -> 4.41 us  [layer(): returned[-1].append(lax.ppermute(part, 'fsdp', back))]
    pallas_call x7, Pallas kernels: 6.8 us -> 9.97 us  [project(): pl.pallas_call(functools.partial(project_kernel, runs, skip, (len(ready),...]
    ppermute x5, waiting for transfers between devices: 5.27 us -> 8.07 us  [layer(): chain.append(lax.ppermute(sums[c], 'sp', ahead))]
    ppermute x2, waiting for transfers between devices: 22.3 us -> 24.9 us  [layer(): arrived[-1].append(lax.ppermute(sent, 'fsdp', there))]
    ppermute x5, waiting for transfers between devices: 5.42 us -> 7.53 us  [layer(): returned[-1].append(lax.ppermute(part, 'fsdp', back))]
    pallas_call x7, Pallas kernels: 15.3 us -> 13.9 us  [the longest x5 10.5 us: attend(): pl.pallas_call(functools.partial(attend_kernel, len(blocks), heads[0], No...]
  transfers between devices with their start and end apart: 18 -> 18, of which waited for: 7 -> 5; matrix products, arithmetic and copies ran while one was open for 0% -> 0% of each run, Pallas kernels for 29% -> 29%
where the time goes in v4:
time: 91.5 us; the launch traced here: 91.2 us
  waiting for transfers between devices  40.5 us (44%)
  Pallas kernels  28.9 us (32%)
  starting transfers between devices  21.4 us (23%)
    ppermute x2, waiting for transfers between devices, layer(): arrived[-1].append(lax.ppermute(sent, 'fsdp', there))  24.9 us
    pallas_call x5, Pallas kernels, attend(): pl.pallas_call(functools.partial(attend_kernel, len(blocks), heads[0], No...  10.5 us
    pallas_call x7, Pallas kernels, project(): pl.pallas_call(functools.partial(project_kernel, runs, skip, (len(ready),...  9.97 us
    ppermute x5, waiting for transfers between devices, layer(): chain.append(lax.ppermute(sums[c], 'sp', ahead))  8.07 us
    ppermute x5, starting transfers between devices, layer(): near = lax.ppermute(pick(chain[b], chain[b + 1]), 'sp', swap)  7.7 us
    ppermute x5, waiting for transfers between devices, layer(): returned[-1].append(lax.ppermute(part, 'fsdp', back))  7.53 us
    ppermute x5, starting transfers between devices, layer(): chain.append(lax.ppermute(sums[c], 'sp', ahead))  6.01 us
    ppermute x5, starting transfers between devices, layer(): returned[-1].append(lax.ppermute(part, 'fsdp', back))  4.41 us
  transfers between devices with their start and end apart: 18, of which 5 were waited for; matrix products, arithmetic and copies ran while one was open for 0% of the time, Pallas kernels for 29%

profile of v4, /device:TPU:0, one launch (start us, length us, event | category | flops | bytes accessed | tf_op | source)
XLA Modules:
  0.0 91.2 jit_solution(2379711644121191425)
XLA Ops:
  0.0 0.5 collective-permute-start
  0.5 2.3 %away.2 = bf16[192,2560]{1,0:T(8,128)(2,1)} custom-call(bf16[256,5120]{1,0:T(8,128)(2,1)} %bitcast.15, f32[1,5120]{1,0:T(1,128)} %bitcast.18), custom_call_target="tpu_custom_call" | custom-call | tf_op jit(solution)/shard_map/away/pallas_call | solution.py:85
  2.8 2.7 %collective-permute-start.1 = (bf16[192,2560]{1,0:T(8,128)(2,1)}, bf16[192,2560]{1,0:T(8,128)(2,1)}, u32[]{:S(2)}, u32[]{:S(2)}) collective-permute-start(bf16[192,2560]{1,0:T(8,128)(2,1)} %away.2), channel_id=1, source_target_pairs={{0,24},{8,16},{16,8},{24,0},{1,25},{9,17},{17,9},{25,1},{2,26},{10... | collective-permute-start | bytes 2949128 | tf_op jit(solution)/shard_map/ppermute | solution.py:442
  5.5 1.1 %away.3 = bf16[64,2560]{1,0:T(8,128)(2,1)S(1)} custom-call(bf16[256,5120]{1,0:T(8,128)(2,1)} %bitcast.16, f32[1,5120]{1,0:T(1,128)} %bitcast.19), custom_call_target="tpu_custom_call" | custom-call | tf_op jit(solution)/shard_map/away/pallas_call | solution.py:85
  6.6 0.1 collective-permute-start.2
  6.7 3.3 %home.1 = (bf16[256,2560]{1,0:T(8,128)(2,1)S(1)}, f32[256,1]{1,0:T(8,128)S(1)}, bf16[1280,2048]{1,0:T(8,128)(2,1)S(1)}) custom-call(bf16[256,5120]{1,0:T(8,128)(2,1)} %bitcast.17, f32[1,5120]{1,0:T(1,128)} %bitcast.20, bf16[1280,2048]{1,0:T(8,128)(2,1)} %weight_ref.1), custom_call_target="tpu_custom_call" | custom-call | tf_op jit(solution)/shard_map/home/pallas_call | solution.py:127
  10.0 24.9 %collective-permute-done.2.refs_1_.refs_0_ = bf16[64,2560]{1,0:T(8,128)(2,1)S(1)} collective-permute-done((bf16[64,2560]{1,0:T(8,128)(2,1)S(1)}, bf16[64,2560]{1,0:T(8,128)(2,1)S(1)}, u32[]{:S(2)}, u32[]{:S(2)}) %collective-permute-start.2) | collective-permute-done | bytes 327712 | tf_op jit(solution)/shard_map/ppermute | solution.py:442
  34.9 0.0 collective-permute-done.refs_2_.refs_3_
  34.9 0.6 project.13
  35.5 1.3 %collective-permute-start.15 = (bf16[64,512]{1,0:T(8,128)(2,1)S(1)}, bf16[64,512]{1,0:T(8,128)(2,1)S(1)}, u32[]{:S(2)}, u32[]{:S(2)}) collective-permute-start(bf16[64,512]{1,0:T(8,128)(2,1)S(1)} %project.13), channel_id=1, source_target_pairs={{24,0},{16,8},{8,16},{0,24},{25,1},{17,9},{9,17},{1,25},{26,2},{18... | collective-permute-start | bytes 196616 | tf_op jit(solution)/shard_map/ppermute | solution.py:466
  36.8 0.0 collective-permute-done.1.refs_0_
  36.8 1.9 %project.12 = bf16[192,512]{1,0:T(8,128)(2,1)S(1)} custom-call(bf16[192,2560]{1,0:T(8,128)(2,1)} %collective-permute-done.1.refs_0_, bf16[1280,2048]{1,0:T(8,128)(2,1)S(1)} %get-tuple-element.15.refs_1_.refs_2_, bf16[1280,2048]{1,0:T(8,128)(2,1)S(1)} %collective-permute-done.refs_2_.refs_3_), custom_call_target="tpu_custom_call" | custom-call | flops 503316480 | bytes 2621440 | tf_op jit(solution)/shard_map/project/pallas_call | solution.py:183
  38.7 0.6 collective-permute-start.14
  39.2 2.9 %project.8.refs_0_ = bf16[192,1536]{1,0:T(8,128)(2,1)S(1)} custom-call(bf16[192,2560]{1,0:T(8,128)(2,1)} %collective-permute-done.1.refs_0_, bf16[1280,2048]{1,0:T(8,128)(2,1)S(1)} %get-tuple-element.15.refs_1_.refs_2_, bf16[1280,2048]{1,0:T(8,128)(2,1)S(1)} %collective-permute-done.refs_2_.refs_3_), custom_call_target="tpu_custom_call" | custom-call | flops 1509949440 | bytes 7864320 | tf_op jit(solution)/shard_map/project/pallas_call | solution.py:183
  42.2 0.6 project.10
  42.7 1.3 %collective-permute-start.8 = (bf16[256,512]{1,0:T(8,128)(2,1)S(1)}, bf16[256,512]{1,0:T(8,128)(2,1)S(1)}, u32[]{:S(2)}, u32[]{:S(2)}) collective-permute-start(bf16[256,512]{1,0:T(8,128)(2,1)S(1)} %project.10), channel_id=1, source_target_pairs={{24,0},{16,8},{8,16},{0,24},{25,1},{17,9},{9,17},{1,25},{26,2},{18... | collective-permute-start | bytes 786440 | tf_op jit(solution)/shard_map/ppermute | solution.py:466
  44.0 0.6 project.11
  44.6 0.6 collective-permute-start.11
  45.2 0.0 copy-start.1
  45.2 2.9 %project.7.mine_ref = f32[256,2048]{1,0:T(8,128)S(1)} custom-call(bf16[256,2560]{1,0:T(8,128)(2,1)S(1)} %get-tuple-element.14.refs_0_, bf16[1280,2048]{1,0:T(8,128)(2,1)S(1)} %get-tuple-element.15.refs_1_.refs_2_, bf16[1280,2048]{1,0:T(8,128)(2,1)S(1)} %collective-permute-done.refs_2_.refs_3_), custom_call_target="tpu_custom_call" | custom-call | flops 2684354560 | bytes 10485760 | tf_op jit(solution)/shard_map/project/pallas_call | solution.py:183
  48.1 0.0 collective-permute-done.15.refs_1_
  48.1 0.0 collective-permute-done.14.refs_0_
  48.1 0.0 copy-done.1
  48.1 0.1 merge.9.even_ref.refs_2_
  48.3 1.2 %collective-permute-start.16 = (bf16[256,512]{1,0:T(8,128)(2,1)S(1)}, bf16[256,512]{1,0:T(8,128)(2,1)S(1)}, u32[]{:S(2)}, u32[]{:S(2)}) collective-permute-start(bf16[256,512]{1,0:T(8,128)(2,1)S(1)} %merge.9.even_ref.refs_2_), channel_id=1, source_target_pairs={{0,2},{1,3},{2,4},{3,5},{4,6},{5,7},{6,0},{7,1},{8,10},{9,11},{10,... | collective-permute-start | bytes 786440 | tf_op jit(solution)/shard_map/ppermute | solution.py:499
  49.5 7.5 %collective-permute-done.11.refs_0_ = bf16[256,512]{1,0:T(8,128)(2,1)S(1)} collective-permute-done((bf16[256,512]{1,0:T(8,128)(2,1)S(1)}, bf16[256,512]{1,0:T(8,128)(2,1)S(1)}, u32[]{:S(2)}, u32[]{:S(2)}) %collective-permute-start.11) | collective-permute-done | bytes 262176 | tf_op jit(solution)/shard_map/ppermute | solution.py:466
  57.0 0.1 merge.8.even_ref.refs_2_
  57.2 1.6 %collective-permute-start.12 = (bf16[256,512]{1,0:T(8,128)(2,1)S(1)}, bf16[256,512]{1,0:T(8,128)(2,1)S(1)}, u32[]{:S(2)}, u32[]{:S(2)}) collective-permute-start(bf16[256,512]{1,0:T(8,128)(2,1)S(1)} %merge.8.even_ref.refs_2_), channel_id=1, source_target_pairs={{0,2},{1,3},{2,4},{3,5},{4,6},{5,7},{6,0},{7,1},{8,10},{9,11},{10,... | collective-permute-start | bytes 786440 | tf_op jit(solution)/shard_map/ppermute | solution.py:499
  58.8 0.6 project.9
  59.4 0.6 collective-permute-start.3
  60.0 0.0 collective-permute-done.8.refs_0_
  60.0 0.1 merge.7.even_ref.refs_2_
  60.2 1.6 %collective-permute-start.9 = (bf16[256,512]{1,0:T(8,128)(2,1)S(1)}, bf16[256,512]{1,0:T(8,128)(2,1)S(1)}, u32[]{:S(2)}, u32[]{:S(2)}) collective-permute-start(bf16[256,512]{1,0:T(8,128)(2,1)S(1)} %merge.7.even_ref.refs_2_), channel_id=1, source_target_pairs={{0,2},{1,3},{2,4},{3,5},{4,6},{5,7},{6,0},{7,1},{8,10},{9,11},{10,... | collective-permute-start | bytes 786440 | tf_op jit(solution)/shard_map/ppermute | solution.py:499
  61.8 0.0 collective-permute-done.16.odd_ref.refs_0_
  61.8 1.6 %collective-permute-start.17 = (bf16[256,512]{1,0:T(8,128)(2,1)S(1)}, bf16[256,512]{1,0:T(8,128)(2,1)S(1)}, u32[]{:S(2)}, u32[]{:S(2)}) collective-permute-start(bf16[256,512]{1,0:T(8,128)(2,1)S(1)} %pick.9), channel_id=1, source_target_pairs={{0,1},{1,0},{2,3},{3,2},{4,5},{5,4},{6,7},{7,6},{8,9},{9,8},{10,11... | collective-permute-start | bytes 786440 | tf_op jit(solution)/shard_map/ppermute | solution.py:505
  63.4 4.8 %collective-permute-done.12.odd_ref.refs_0_ = bf16[256,512]{1,0:T(8,128)(2,1)S(1)} collective-permute-done((bf16[256,512]{1,0:T(8,128)(2,1)S(1)}, bf16[256,512]{1,0:T(8,128)(2,1)S(1)}, u32[]{:S(2)}, u32[]{:S(2)}) %collective-permute-start.12) | collective-permute-done | bytes 262176 | tf_op jit(solution)/shard_map/ppermute | solution.py:499
  68.2 1.5 %collective-permute-start.13 = (bf16[256,512]{1,0:T(8,128)(2,1)S(1)}, bf16[256,512]{1,0:T(8,128)(2,1)S(1)}, u32[]{:S(2)}, u32[]{:S(2)}) collective-permute-start(bf16[256,512]{1,0:T(8,128)(2,1)S(1)} %pick.8), channel_id=1, source_target_pairs={{0,1},{1,0},{2,3},{3,2},{4,5},{5,4},{6,7},{7,6},{8,9},{9,8},{10,11... | collective-permute-start | bytes 786440 | tf_op jit(solution)/shard_map/ppermute | solution.py:505
  69.7 0.0 collective-permute-done.3.refs_0_
  69.7 0.1 merge.5.even_ref.refs_2_
  69.9 0.0 copy-start.2
  69.9 0.0 copy-start
  69.9 0.1 collective-permute-start.4
  70.0 0.1 merge.6.even_ref.refs_2_
  70.1 1.5 %collective-permute-start.6 = (bf16[256,256]{1,0:T(8,128)(2,1)S(1)}, bf16[256,256]{1,0:T(8,128)(2,1)S(1)}, u32[]{:S(2)}, u32[]{:S(2)}) collective-permute-start(bf16[256,256]{1,0:T(8,128)(2,1)S(1)} %merge.6.even_ref.refs_2_), channel_id=1, source_target_pairs={{0,2},{1,3},{2,4},{3,5},{4,6},{5,7},{6,0},{7,1},{8,10},{9,11},{10,... | collective-permute-start | bytes 393224 | tf_op jit(solution)/shard_map/ppermute | solution.py:499
  71.6 1.8 %collective-permute-done.9.odd_ref.refs_0_ = bf16[256,512]{1,0:T(8,128)(2,1)S(1)} collective-permute-done((bf16[256,512]{1,0:T(8,128)(2,1)S(1)}, bf16[256,512]{1,0:T(8,128)(2,1)S(1)}, u32[]{:S(2)}, u32[]{:S(2)}) %collective-permute-start.9) | collective-permute-done | bytes 262176 | tf_op jit(solution)/shard_map/ppermute | solution.py:499
  73.4 1.7 %collective-permute-start.10 = (bf16[256,512]{1,0:T(8,128)(2,1)S(1)}, bf16[256,512]{1,0:T(8,128)(2,1)S(1)}, u32[]{:S(2)}, u32[]{:S(2)}) collective-permute-start(bf16[256,512]{1,0:T(8,128)(2,1)S(1)} %pick.7), channel_id=1, source_target_pairs={{0,1},{1,0},{2,3},{3,2},{4,5},{5,4},{6,7},{7,6},{8,9},{9,8},{10,11... | collective-permute-start | bytes 786440 | tf_op jit(solution)/shard_map/ppermute | solution.py:505
  75.0 0.0 copy-done.2
  75.0 0.8 mask.1.bias_ref
  75.9 1.5 %collective-permute-done.4.odd_ref.refs_0_ = bf16[256,256]{1,0:T(8,128)(2,1)S(1)} collective-permute-done((bf16[256,256]{1,0:T(8,128)(2,1)S(1)}, bf16[256,256]{1,0:T(8,128)(2,1)S(1)}, u32[]{:S(2)}, u32[]{:S(2)}) %collective-permute-start.4) | collective-permute-done | bytes 131104 | tf_op jit(solution)/shard_map/ppermute | solution.py:499
  77.3 1.4 %collective-permute-start.5 = (bf16[256,256]{1,0:T(8,128)(2,1)S(1)}, bf16[256,256]{1,0:T(8,128)(2,1)S(1)}, u32[]{:S(2)}, u32[]{:S(2)}) collective-permute-start(bf16[256,256]{1,0:T(8,128)(2,1)S(1)} %pick.5), channel_id=1, source_target_pairs={{0,1},{1,0},{2,3},{3,2},{4,5},{5,4},{6,7},{7,6},{8,9},{9,8},{10,11... | collective-permute-start | bytes 393224 | tf_op jit(solution)/shard_map/ppermute | solution.py:505
  78.8 0.0 collective-permute-done.6.odd_ref.refs_0_
  78.8 0.2 pick.6
  79.0 1.5 %collective-permute-start.7 = (bf16[256,256]{1,0:T(8,128)(2,1)S(1)}, bf16[256,256]{1,0:T(8,128)(2,1)S(1)}, u32[]{:S(2)}, u32[]{:S(2)}) collective-permute-start(bf16[256,256]{1,0:T(8,128)(2,1)S(1)} %pick.6), channel_id=1, source_target_pairs={{0,1},{1,0},{2,3},{3,2},{4,5},{5,4},{6,7},{7,6},{8,9},{9,8},{10,11... | collective-permute-start | bytes 393224 | tf_op jit(solution)/shard_map/ppermute | solution.py:505
  80.5 0.0 collective-permute-done.17.refs_1_
  80.5 0.0 copy-done
  80.5 2.2 %attend.5.refs_3_ = bf16[4,128,512]{2,1,0:T(8,128)(2,1)S(1)} custom-call(f32[256,768]{1,0:T(8,128)S(1)} %mask.1.bias_ref, bf16[256,4096]{1,0:T(8,128)(2,1)S(1)} %bitcast.5, bf16[256,512]{1,0:T(8,128)(2,1)S(1)} %collective-permute-done.16.odd_ref.refs_0_, bf16[256,512]{1,0:T(8,128)(2,1)S(1)} %collective-permute-done.17.refs_1_, ...), custom_call_target="tpu_custom_call" | custom-call | flops 1006632960 | bytes 1048576 | tf_op jit(solution)/shard_map/attend/pallas_call | solution.py:398
  82.7 0.0 collective-permute-done.13.refs_1_
  82.7 2.5 %attend.6 = (bf16[256,4096]{1,0:T(8,128)(2,1)}, bf16[4,128,512]{2,1,0:T(8,128)(2,1)S(1)}) custom-call(f32[256,768]{1,0:T(8,128)S(1)} %mask.1.bias_ref, bf16[256,4096]{1,0:T(8,128)(2,1)S(1)} %bitcast.6, bf16[256,512]{1,0:T(8,128)(2,1)S(1)} %collective-permute-done.12.odd_ref.refs_0_, bf16[256,512]{1,0:T(8,128)(2,1)S(1)} %collective-permute-done.13.refs_1_, ...), custom_call_target="tpu_custom_call" | custom-call | flops 1006632960 | bytes 1048576 | tf_op jit(solution)/shard_map/attend/pallas_call | solution.py:398
  85.2 0.0 collective-permute-done.10.refs_1_
  85.2 2.3 %attend.7 = (bf16[256,4096]{1,0:T(8,128)(2,1)}, bf16[4,128,512]{2,1,0:T(8,128)(2,1)S(1)}) custom-call(f32[256,768]{1,0:T(8,128)S(1)} %mask.1.bias_ref, bf16[256,4096]{1,0:T(8,128)(2,1)S(1)} %bitcast.7, bf16[256,512]{1,0:T(8,128)(2,1)S(1)} %collective-permute-done.9.odd_ref.refs_0_, ...), custom_call_target="tpu_custom_call", output_to_operand_aliasing={{0}: (6, {})} | custom-call | flops 1006632960 | bytes 1048576 | tf_op jit(solution)/shard_map/attend/pallas_call | solution.py:398
  87.5 0.0 collective-permute-done.7.refs_1_
  87.5 1.5 %attend.8 = (bf16[256,4096]{1,0:T(8,128)(2,1)}, bf16[2,128,512]{2,1,0:T(8,128)(2,1)S(1)}) custom-call(f32[256,768]{1,0:T(8,128)S(1)} %mask.1.bias_ref, bf16[256,4096]{1,0:T(8,128)(2,1)S(1)} %bitcast.8, bf16[256,256]{1,0:T(8,128)(2,1)S(1)} %collective-permute-done.6.odd_ref.refs_0_, ...), custom_call_target="tpu_custom_call", output_to_operand_aliasing={{0}: (6, {})} | custom-call | flops 503316480 | bytes 524288 | tf_op jit(solution)/shard_map/attend/pallas_call | solution.py:398
  89.0 0.0 collective-permute-done.5.refs_1_
  89.0 2.1 %attend.9 = bf16[256,4096]{1,0:T(8,128)(2,1)} custom-call(f32[256,768]{1,0:T(8,128)S(1)} %mask.1.bias_ref, bf16[256,4096]{1,0:T(8,128)(2,1)S(1)} %bitcast.9, bf16[256,256]{1,0:T(8,128)(2,1)S(1)} %collective-permute-done.4.odd_ref.refs_0_, bf16[256,256]{1,0:T(8,128)(2,1)S(1)} %collective-permute-done.5.refs_1_, ...), custom_call_target="tpu_custom_call", output_to_operand_aliasing={{}: (6, {})} | custom-call | flops 503316480 | bytes 524288 | tf_op jit(solution)/shard_map/attend/pallas_call | solution.py:398
  (4 shorter events, 0.1 us)
Async XLA Ops:
  0.0 34.9 %collective-permute-start = (bf16[1280,2048]{1,0:T(8,128)(2,1)}, bf16[1280,2048]{1,0:T(8,128)(2,1)S(1)}, u32[]{:S(2)}, u32[]{:S(2)}) collective-permute-start(bf16[1280,2048]{1,0:T(8,128)(2,1)} %weight_ref.1), channel_id=1, source_target_pairs={{0,8},{8,0},{16,24},{24,16},{1,9},{9,1},{17,25},{25,17},{2,10},{10... | collective-permute-start | bytes 15728648 | tf_op jit(solution)/shard_map/ppermute | solution.py:446
  2.8 33.9 %collective-permute-start.1 = (bf16[192,2560]{1,0:T(8,128)(2,1)}, bf16[192,2560]{1,0:T(8,128)(2,1)}, u32[]{:S(2)}, u32[]{:S(2)}) collective-permute-start(bf16[192,2560]{1,0:T(8,128)(2,1)} %away.2), channel_id=1, source_target_pairs={{0,24},{8,16},{16,8},{24,0},{1,25},{9,17},{17,9},{25,1},{2,26},{10... | collective-permute-start | bytes 2949128 | tf_op jit(solution)/shard_map/ppermute | solution.py:442
  6.6 28.3 %collective-permute-start.2 = (bf16[64,2560]{1,0:T(8,128)(2,1)S(1)}, bf16[64,2560]{1,0:T(8,128)(2,1)S(1)}, u32[]{:S(2)}, u32[]{:S(2)}) collective-permute-start(bf16[64,2560]{1,0:T(8,128)(2,1)S(1)} %away.3), channel_id=1, source_target_pairs={{0,24},{8,16},{16,8},{24,0},{1,25},{9,17},{17,9},{25,1},{2,26},{10... | collective-permute-start | bytes 983048 | tf_op jit(solution)/shard_map/ppermute | solution.py:442
  35.5 12.6 %collective-permute-start.15 = (bf16[64,512]{1,0:T(8,128)(2,1)S(1)}, bf16[64,512]{1,0:T(8,128)(2,1)S(1)}, u32[]{:S(2)}, u32[]{:S(2)}) collective-permute-start(bf16[64,512]{1,0:T(8,128)(2,1)S(1)} %project.13), channel_id=1, source_target_pairs={{24,0},{16,8},{8,16},{0,24},{25,1},{17,9},{9,17},{1,25},{26,2},{18... | collective-permute-start | bytes 196616 | tf_op jit(solution)/shard_map/ppermute | solution.py:466
  38.7 9.4 %collective-permute-start.14 = (bf16[192,512]{1,0:T(8,128)(2,1)S(1)}, bf16[192,512]{1,0:T(8,128)(2,1)S(1)}, u32[]{:S(2)}, u32[]{:S(2)}) collective-permute-start(bf16[192,512]{1,0:T(8,128)(2,1)S(1)} %project.12), channel_id=1, source_target_pairs={{24,0},{16,8},{8,16},{0,24},{25,1},{17,9},{9,17},{1,25},{26,2},{18... | collective-permute-start | bytes 589832 | tf_op jit(solution)/shard_map/ppermute | solution.py:466
  42.7 17.3 %collective-permute-start.8 = (bf16[256,512]{1,0:T(8,128)(2,1)S(1)}, bf16[256,512]{1,0:T(8,128)(2,1)S(1)}, u32[]{:S(2)}, u32[]{:S(2)}) collective-permute-start(bf16[256,512]{1,0:T(8,128)(2,1)S(1)} %project.10), channel_id=1, source_target_pairs={{24,0},{16,8},{8,16},{0,24},{25,1},{17,9},{9,17},{1,25},{26,2},{18... | collective-permute-start | bytes 786440 | tf_op jit(solution)/shard_map/ppermute | solution.py:466
  44.6 12.4 %collective-permute-start.11 = (bf16[256,512]{1,0:T(8,128)(2,1)S(1)}, bf16[256,512]{1,0:T(8,128)(2,1)S(1)}, u32[]{:S(2)}, u32[]{:S(2)}) collective-permute-start(bf16[256,512]{1,0:T(8,128)(2,1)S(1)} %project.11), channel_id=1, source_target_pairs={{24,0},{16,8},{8,16},{0,24},{25,1},{17,9},{9,17},{1,25},{26,2},{18... | collective-permute-start | bytes 786440 | tf_op jit(solution)/shard_map/ppermute | solution.py:466
  45.2 2.9 %copy-start.1 = (f32[1024]{0:T(1024)S(1)}, f32[1024]{0:T(1024)}, u32[]{:S(2)}) copy-start(f32[1024]{0:T(1024)} %param.10) | copy-start | bytes 12292
  48.3 13.5 %collective-permute-start.16 = (bf16[256,512]{1,0:T(8,128)(2,1)S(1)}, bf16[256,512]{1,0:T(8,128)(2,1)S(1)}, u32[]{:S(2)}, u32[]{:S(2)}) collective-permute-start(bf16[256,512]{1,0:T(8,128)(2,1)S(1)} %merge.9.even_ref.refs_2_), channel_id=1, source_target_pairs={{0,2},{1,3},{2,4},{3,5},{4,6},{5,7},{6,0},{7,1},{8,10},{9,11},{10,... | collective-permute-start | bytes 786440 | tf_op jit(solution)/shard_map/ppermute | solution.py:499
  57.2 11.0 %collective-permute-start.12 = (bf16[256,512]{1,0:T(8,128)(2,1)S(1)}, bf16[256,512]{1,0:T(8,128)(2,1)S(1)}, u32[]{:S(2)}, u32[]{:S(2)}) collective-permute-start(bf16[256,512]{1,0:T(8,128)(2,1)S(1)} %merge.8.even_ref.refs_2_), channel_id=1, source_target_pairs={{0,2},{1,3},{2,4},{3,5},{4,6},{5,7},{6,0},{7,1},{8,10},{9,11},{10,... | collective-permute-start | bytes 786440 | tf_op jit(solution)/shard_map/ppermute | solution.py:499
  59.4 10.4 %collective-permute-start.3 = (bf16[256,512]{1,0:T(8,128)(2,1)S(1)}, bf16[256,512]{1,0:T(8,128)(2,1)S(1)}, u32[]{:S(2)}, u32[]{:S(2)}) collective-permute-start(bf16[256,512]{1,0:T(8,128)(2,1)S(1)} %project.9), channel_id=1, source_target_pairs={{24,0},{16,8},{8,16},{0,24},{25,1},{17,9},{9,17},{1,25},{26,2},{18... | collective-permute-start | bytes 786440 | tf_op jit(solution)/shard_map/ppermute | solution.py:466
  60.2 13.2 %collective-permute-start.9 = (bf16[256,512]{1,0:T(8,128)(2,1)S(1)}, bf16[256,512]{1,0:T(8,128)(2,1)S(1)}, u32[]{:S(2)}, u32[]{:S(2)}) collective-permute-start(bf16[256,512]{1,0:T(8,128)(2,1)S(1)} %merge.7.even_ref.refs_2_), channel_id=1, source_target_pairs={{0,2},{1,3},{2,4},{3,5},{4,6},{5,7},{6,0},{7,1},{8,10},{9,11},{10,... | collective-permute-start | bytes 786440 | tf_op jit(solution)/shard_map/ppermute | solution.py:499
  61.8 18.7 %collective-permute-start.17 = (bf16[256,512]{1,0:T(8,128)(2,1)S(1)}, bf16[256,512]{1,0:T(8,128)(2,1)S(1)}, u32[]{:S(2)}, u32[]{:S(2)}) collective-permute-start(bf16[256,512]{1,0:T(8,128)(2,1)S(1)} %pick.9), channel_id=1, source_target_pairs={{0,1},{1,0},{2,3},{3,2},{4,5},{5,4},{6,7},{7,6},{8,9},{9,8},{10,11... | collective-permute-start | bytes 786440 | tf_op jit(solution)/shard_map/ppermute | solution.py:505
  68.2 14.5 %collective-permute-start.13 = (bf16[256,512]{1,0:T(8,128)(2,1)S(1)}, bf16[256,512]{1,0:T(8,128)(2,1)S(1)}, u32[]{:S(2)}, u32[]{:S(2)}) collective-permute-start(bf16[256,512]{1,0:T(8,128)(2,1)S(1)} %pick.8), channel_id=1, source_target_pairs={{0,1},{1,0},{2,3},{3,2},{4,5},{5,4},{6,7},{7,6},{8,9},{9,8},{10,11... | collective-permute-start | bytes 786440 | tf_op jit(solution)/shard_map/ppermute | solution.py:505
  69.9 5.2 %copy-start.2 = (s32[1,16]{1,0:T(1,128)S(1)}, s32[1,16]{1,0:T(1,128)}, u32[]{:S(2)}) copy-start(s32[1,16]{1,0:T(1,128)} %lengths_ref.1) | copy-start | bytes 196
  69.9 10.6 %copy-start = (bf16[1,256,4096]{2,1,0:T(8,128)(2,1)S(1)}, bf16[1,256,4096]{2,1,0:T(8,128)(2,1)}, u32[]{:S(2)}) copy-start(bf16[1,256,4096]{2,1,0:T(8,128)(2,1)} %param.7) | copy-start | bytes 6291460
  69.9 7.4 %collective-permute-start.4 = (bf16[256,256]{1,0:T(8,128)(2,1)S(1)}, bf16[256,256]{1,0:T(8,128)(2,1)S(1)}, u32[]{:S(2)}, u32[]{:S(2)}) collective-permute-start(bf16[256,256]{1,0:T(8,128)(2,1)S(1)} %merge.5.even_ref.refs_2_), channel_id=1, source_target_pairs={{0,2},{1,3},{2,4},{3,5},{4,6},{5,7},{6,0},{7,1},{8,10},{9,11},{10,... | collective-permute-start | bytes 393224 | tf_op jit(solution)/shard_map/ppermute | solution.py:499
  70.1 8.7 %collective-permute-start.6 = (bf16[256,256]{1,0:T(8,128)(2,1)S(1)}, bf16[256,256]{1,0:T(8,128)(2,1)S(1)}, u32[]{:S(2)}, u32[]{:S(2)}) collective-permute-start(bf16[256,256]{1,0:T(8,128)(2,1)S(1)} %merge.6.even_ref.refs_2_), channel_id=1, source_target_pairs={{0,2},{1,3},{2,4},{3,5},{4,6},{5,7},{6,0},{7,1},{8,10},{9,11},{10,... | collective-permute-start | bytes 393224 | tf_op jit(solution)/shard_map/ppermute | solution.py:499
  73.4 11.8 %collective-permute-start.10 = (bf16[256,512]{1,0:T(8,128)(2,1)S(1)}, bf16[256,512]{1,0:T(8,128)(2,1)S(1)}, u32[]{:S(2)}, u32[]{:S(2)}) collective-permute-start(bf16[256,512]{1,0:T(8,128)(2,1)S(1)} %pick.7), channel_id=1, source_target_pairs={{0,1},{1,0},{2,3},{3,2},{4,5},{5,4},{6,7},{7,6},{8,9},{9,8},{10,11... | collective-permute-start | bytes 786440 | tf_op jit(solution)/shard_map/ppermute | solution.py:505
  77.3 11.7 %collective-permute-start.5 = (bf16[256,256]{1,0:T(8,128)(2,1)S(1)}, bf16[256,256]{1,0:T(8,128)(2,1)S(1)}, u32[]{:S(2)}, u32[]{:S(2)}) collective-permute-start(bf16[256,256]{1,0:T(8,128)(2,1)S(1)} %pick.5), channel_id=1, source_target_pairs={{0,1},{1,0},{2,3},{3,2},{4,5},{5,4},{6,7},{7,6},{8,9},{9,8},{10,11... | collective-permute-start | bytes 393224 | tf_op jit(solution)/shard_map/ppermute | solution.py:505
  79.0 8.5 %collective-permute-start.7 = (bf16[256,256]{1,0:T(8,128)(2,1)S(1)}, bf16[256,256]{1,0:T(8,128)(2,1)S(1)}, u32[]{:S(2)}, u32[]{:S(2)}) collective-permute-start(bf16[256,256]{1,0:T(8,128)(2,1)S(1)} %pick.6), channel_id=1, source_target_pairs={{0,1},{1,0},{2,3},{3,2},{4,5},{5,4},{6,7},{7,6},{8,9},{9,8},{10,11... | collective-permute-start | bytes 393224 | tf_op jit(solution)/shard_map/ppermute | solution.py:505

commit v5 on v4

--- a/solution.py
+++ b/solution.py
@@ -13,10 +13,9 @@
 EPS = 1e-06
 RATIO = QH // KVH
 LOG2E = 1.4426950408889634
-SUMS = ((0, 1), (2, 3), (4, 5), (6, 7))
-BLOCKS = ((0, 1), (2, 3), (4, 5), (6,), (7,))
+GROUPS = ((0, 1, 2), (3, 4, 5), (6, 7))
+CHUNKS = ((0, 0), (0, 1), (1, 0), (1, 1), (0, 2), (1, 2))
 PIECES = 2
-FIRST = 3, 4
 TILE = 128
 STRIP = 32
 AHEAD = 2
@@ -56,11 +55,6 @@
             wide = rows_ref[some, a : a + held].astype(jnp.float32)
             scaled = wide * gain_ref[:, a : a + held]
             out_ref[:, b : b + held] = scaled.astype(jnp.bfloat16)
-
-
-def bounds_of(tokens):
-    cut = tokens * FIRST[0] // FIRST[1]
-    return (0, cut, tokens)
 
 
 def away_kernel(parts, pair, ahead, start, hidden_ref, gain_ref, out_ref, rows, gains, sems):
@@ -80,8 +74,8 @@
 
 
 def away(hidden, gain, parts, pair, held, ahead, piece):
-    start, stop = bounds_of(hidden.shape[0])[piece : piece + 2]
-    step, width = stop - start, pair * held
+    step, width = hidden.shape[0] // PIECES, pair * held
+    start = piece * step
     return pl.pallas_call(
         functools.partial(away_kernel, parts, pair, ahead, start),
         in_specs=[HBM, HBM],
@@ -143,83 +137,71 @@
     )(in_hbm(hidden), in_hbm(gain), in_hbm(weight))
 
 
-def columns_of(chunks):
+def columns_of(groups):
     return [
-        (half * KVH * HD + heads[0] * HD, len(heads) * HD) for heads in chunks for half in range(2)
+        (half * KVH * HD + heads[0] * HD, len(heads) * HD) for heads in groups for half in range(2)
     ]
 
 
-def project_kernel(runs, skip, counts, *refs):
-    ready, rows = refs[: counts[0]], refs[counts[0] : sum(counts[:2])]
-    weights, out_ref = refs[sum(counts[:2]) : -1], refs[-1]
+def project_kernel(runs, rows_ref, *refs):
+    weights, out_ref = refs[:-1], refs[-1]
     depth = weights[0].shape[0]
-    row = 0
-    for ready_ref in ready:
-        row = ready_ref.shape[0]
-        out_ref[:row, :] = ready_ref[:, skip : skip + out_ref.shape[1]]
-    for rows_ref in rows:
-        some = slice(row, row + rows_ref.shape[0])
-        row = some.stop
-        column = 0
-        for start, width in runs:
-            total = None
-            for w, weight in enumerate(weights):
-                term = jnp.dot(
-                    rows_ref[:, w * depth : (w + 1) * depth],
-                    weight[:, start : start + width],
-                    preferred_element_type=jnp.float32,
-                )
-                total = term if total is None else total + term
-            out_ref[some, column : column + width] = total.astype(out_ref.dtype)
-            column += width
-
-
-def project(rows, weights, chunks, dtype, ready=(), skip=0):
-    tokens = sum(r.shape[0] for r in (*ready, *rows))
-    depth = rows[0].shape[1]
-    runs = columns_of(chunks)
+    column = 0
+    for start, width in runs:
+        total = None
+        for w, weight in enumerate(weights):
+            term = jnp.dot(
+                rows_ref[:, w * depth : (w + 1) * depth],
+                weight[:, start : start + width],
+                preferred_element_type=jnp.float32,
+            )
+            total = term if total is None else total + term
+        out_ref[:, column : column + width] = total.astype(out_ref.dtype)
+        column += width
+
+
+def project(rows, weights, groups, dtype):
+    tokens, depth = rows.shape
+    runs = columns_of(groups)
     columns = sum(width for _, width in runs)
-    operands = [*ready, *rows, *weights]
-    return pl.pallas_call(
-        functools.partial(project_kernel, runs, skip, (len(ready), len(rows))),
-        in_specs=[VMEM] * len(operands),
+    return pl.pallas_call(
+        functools.partial(project_kernel, runs),
+        in_specs=[VMEM] * (1 + len(weights)),
         out_specs=VMEM,
         out_shape=jax.ShapeDtypeStruct((tokens, columns), dtype),
         compiler_params=pltpu.CompilerParams(vmem_limit_bytes=24 * MIB),
         cost_estimate=pl.CostEstimate(
-            flops=2 * rows[0].shape[0] * len(rows) * depth * columns,
+            flops=2 * tokens * depth * columns,
             bytes_accessed=2 * depth * columns,
             transcendentals=0,
         ),
         name="project",
-    )(*operands)
-
-
-def merge_kernel(heads, own, other, pieces, mine_ref, power_ref, bias_ref, *refs):
+    )(rows, *weights)
+
+
+def merge_kernel(row, start, heads, mine_ref, power_ref, bias_ref, *refs):
     parts, out_ref = refs[:-1], refs[-1]
-    width = len(heads) * HD
-    bounds = bounds_of(out_ref.shape[0]) if pieces > 1 else (0, out_ref.shape[0])
-    for piece in range(pieces):
-        some = slice(bounds[piece], bounds[piece + 1])
-        power = power_ref[some, :]
-        for half in range(2):
-            total = mine_ref[some, own[half] : own[half] + width]
-            for part in parts[piece::pieces]:
-                total = total + part[:, other[half] : other[half] + width].astype(jnp.float32)
-            if half == 0:
-                total = total * (power * (HD ** (-0.5) * LOG2E))
-            else:
-                first = heads[0] * HD
-                total = total * power + bias_ref[:, first : first + width]
-            out_ref[some, half * width : (half + 1) * width] = total.astype(jnp.bfloat16)
-
-
-def merge(mine, power, bias, parts, pieces, heads, own, other):
-    return pl.pallas_call(
-        functools.partial(merge_kernel, heads, own, other, pieces),
+    rows, width = out_ref.shape[0], len(heads) * HD
+    some = slice(row, row + rows)
+    power = power_ref[some, :]
+    for half in range(2):
+        ours = slice(half * width, (half + 1) * width)
+        total = mine_ref[some, start + half * width : start + (half + 1) * width]
+        for part in parts:
+            total = total + part[:, ours].astype(jnp.float32)
+        if half == 0:
+            total = total * (power * (HD ** (-0.5) * LOG2E))
+        else:
+            total = total * power + bias_ref[:, heads[0] * HD : heads[0] * HD + width]
+        out_ref[:, ours] = total.astype(jnp.bfloat16)
+
+
+def merge(mine, power, bias, parts, row, start, heads):
+    return pl.pallas_call(
+        functools.partial(merge_kernel, row, start, heads),
         in_specs=[VMEM] * (3 + len(parts)),
         out_specs=VMEM,
-        out_shape=jax.ShapeDtypeStruct((mine.shape[0], 2 * len(heads) * HD), jnp.bfloat16),
+        out_shape=jax.ShapeDtypeStruct(parts[0].shape, jnp.bfloat16),
         compiler_params=pltpu.CompilerParams(vmem_limit_bytes=4 * MIB),
         name="merge",
     )(mine, power, bias, *parts)
@@ -299,15 +281,18 @@
     tiles, scores, probs = refs[:3]
     tokens = query_ref.shape[0]
     heads = blocks[0].shape[1] // (2 * HD)
+    piece = blocks[0].shape[0]
     span = scores.shape[2]
     buffers = scores.shape[0]
     units = [(head, t) for head in range(heads) for t in range(0, tokens, TILE)]
 
-    def spans(t):
-        for b in range(count):
-            a, z = max(t - b * tokens, 0), min(t + span - b * tokens, tokens)
+    def window(t, column):
+        picked = []
+        for i, block in enumerate(blocks):
+            a, z = max(t - i * piece, 0), min(t + span - i * piece, piece)
             if a < z:
-                yield b, a, z, b * tokens + a - t
+                picked.append(block[a:z, column : column + HD])
+        return jnp.concatenate(picked, axis=0)
 
     def score(u):
         head, t = units[u]
@@ -315,14 +300,12 @@
         queries = [
             query_ref[t : t + TILE, wide + h * HD : wide + (h + 1) * HD] for h in range(RATIO)
         ]
-        queries = jnp.concatenate(queries, axis=0)
-        for b, a, z, at in spans(t):
-            scores[u % buffers, :, at : at + z - a] = lax.dot_general(
-                queries,
-                blocks[b][a:z, head * HD : (head + 1) * HD],
-                (((1,), (1,)), ((), ())),
-                preferred_element_type=jnp.float32,
-            )
+        scores[u % buffers] = lax.dot_general(
+            jnp.concatenate(queries, axis=0),
+            window(t, head * HD),
+            (((1,), (1,)), ((), ())),
+            preferred_element_type=jnp.float32,
+        )
 
     def soften(u):
         t = units[u][1]
@@ -334,14 +317,9 @@
 
     def blend(u):
         head, t = units[u]
-        total = None
-        for b, a, z, at in spans(t):
-            value = blocks[b][a:z, (heads + head) * HD : (heads + head + 1) * HD]
-            value = jnp.concatenate([value, jnp.ones((z - a, HD), jnp.bfloat16)], axis=1)
-            term = jnp.dot(
-                probs[u % buffers, :, at : at + z - a], value, preferred_element_type=jnp.float32
-            )
-            total = term if total is None else total + term
+        values = window(t, (heads + head) * HD)
+        values = jnp.concatenate([values, jnp.ones_like(values)], axis=1)
+        total = jnp.dot(probs[u % buffers], values, preferred_element_type=jnp.float32)
         result = (total[:, :HD] / total[:, HD:]).astype(tiles.dtype)
         for h in range(RATIO):
             tiles[u, :, h * HD : (h + 1) * HD] = result[h * TILE : (h + 1) * TILE]
@@ -364,7 +342,7 @@
     tokens = queries.shape[0]
     operands = [bias, queries, *blocks]
     in_specs = [VMEM] * len(operands)
-    span = (len(blocks) - 1) * tokens + TILE
+    span = len(blocks) * blocks[0].shape[0] - tokens + TILE
     units = len(heads) * tokens // TILE
     tile = (TILE, RATIO * HD)
     aliases = {}
@@ -445,67 +423,38 @@
     if pair == 2:
         weights.append(lax.ppermute(kv_weight, "fsdp", [(i, i ^ 1) for i in range(parts)]))
     bias = mask(doc_lengths, tokens, reach)
-    mine = project([own], weights, SUMS, jnp.float32)
-
-    early = []
-    for d in range(1, groups):
-        early.append(project(arrived[d - 1][:1], weights, SUMS[1:], jnp.bfloat16))
-
-    returned = []
-    skip = 0
-    for c, heads in enumerate(SUMS):
-        returned.append([])
+    mine = project(own, weights, GROUPS, jnp.float32)
+
+    starts = [sum(2 * len(heads) * HD for heads in GROUPS[:g]) for g in range(len(GROUPS))]
+    swaps = reach % 2 == 0 and length % 2 == 0
+    finished = {}
+    for piece, g in CHUNKS:
+        heads = GROUPS[g]
+        returned = []
         for d in range(1, groups):
             back = [(across(i, d, parts, pair), i) for i in range(parts)]
-            for p in range(PIECES if c == 0 else 1):
-                if c == 0:
-                    part = project(arrived[d - 1][p : p + 1], weights, [heads], jnp.bfloat16)
-                else:
-                    rows, ready = arrived[d - 1][1:], early[d - 1 : d]
-                    part = project(rows, weights, [heads], jnp.bfloat16, ready, skip)
-                returned[-1].append(lax.ppermute(part, "fsdp", back))
-        skip += 2 * len(heads) * HD if c else 0
-
-    sums = []
-    for heads in BLOCKS:
-        source = [i for i, some in enumerate(SUMS) if heads[0] in some][0]
-        held_heads = SUMS[source]
-        own_start = sum(2 * len(some) * HD for some in SUMS[:source])
-        first = (heads[0] - held_heads[0]) * HD
-        other_columns = (first, first + len(held_heads) * HD)
-        own_columns = tuple(own_start + x for x in other_columns)
-        sums.append(
-            merge(
-                mine,
-                power,
-                value_bias[None],
-                returned[source],
-                PIECES if source == 0 else 1,
-                heads,
-                own_columns,
-                other_columns,
-            )
-        )
-
-    before = None
-    for c, heads in enumerate(BLOCKS):
-        chain = [sums[c]]
-        shifts = range(1, reach + 1)
-        swaps = reach % 2 == 0 and length % 2 == 0
-        if swaps:
-            shifts = range(2, reach + 1, 2)
-        for b in shifts:
+            part = project(arrived[d - 1][piece], weights, [heads], jnp.bfloat16)
+            returned.append(lax.ppermute(part, "fsdp", back))
+        row = piece * (tokens // PIECES)
+        done = merge(mine, power, value_bias[None], returned, row, starts[g], heads)
+        chain = [done]
+        for b in range(2, reach + 1, 2) if swaps else range(1, reach + 1):
             ahead = [(i, (i + b) % length) for i in range(length)]
-            chain.append(lax.ppermute(sums[c], "sp", ahead))
+            chain.append(lax.ppermute(done, "sp", ahead))
         blocks = chain
         if swaps:
-            blocks = [chain[0]]
+            blocks = [done]
             swap = [(i, i ^ 1) for i in range(length)]
             for b in range(reach // 2):
                 near = lax.ppermute(pick(chain[b], chain[b + 1]), "sp", swap)
                 blocks += [near, chain[b + 1]]
-        last = c == len(BLOCKS) - 1
-        results = attend(bias, queries, blocks[::-1], heads, before, last)
+        finished[piece, g] = blocks
+
+    before = None
+    for g, heads in enumerate(GROUPS):
+        blocks = [finished[p, g][b] for b in range(reach, -1, -1) for p in range(PIECES)]
+        last = g == len(GROUPS) - 1
+        results = attend(bias, queries, blocks, heads, before, last)
         before = (heads, results[-1], results[0] if before is not None else None)
     return results[0]
 

time: 91.5 us -> 89 us (0.973)
  waiting for transfers between devices: 40.5 us -> 33.5 us
  starting transfers between devices: 21.4 us -> 25 us
    ppermute x2, waiting for transfers between devices: 24.9 us -> 18.6 us  [layer(): arrived[-1].append(lax.ppermute(sent, 'fsdp', there))]
    ppermute x10 -> x12, starting transfers between devices: 10.4 us -> 14.5 us  [the longest x6 8.35 us: layer(): chain.append(lax.ppermute(done, 'sp', ahead))]
    ppermute x10 -> x12, waiting for transfers between devices: 15.6 us -> 13.8 us  [the longest x6 8.56 us: layer(): returned.append(lax.ppermute(part, 'fsdp', back))]
    pallas_call x12 -> x13, Pallas kernels: 10.6 us -> 11.9 us  [the longest x7 11.3 us: project(): pl.pallas_call(functools.partial(project_kernel, runs), in_specs=[VMEM] *...]
    ppermute x5 -> x6, waiting for transfers between devices: 0.01 us -> 1.13 us  [layer(): near = lax.ppermute(pick(chain[b], chain[b + 1]), 'sp', swap)]
    ppermute x5 -> x6, starting transfers between devices: 7.7 us -> 7.24 us  [layer(): near = lax.ppermute(pick(chain[b], chain[b + 1]), 'sp', swap)]
    pallas_call x5 -> x3, Pallas kernels: 10.5 us -> 10.2 us  [attend(): pl.pallas_call(functools.partial(attend_kernel, len(blocks), heads[0], No...]
  transfers between devices with their start and end apart: 18 -> 21, of which waited for: 5 -> 11; matrix products, arithmetic and copies ran while one was open for 0% -> 0% of each run, Pallas kernels for 29% -> 30%
where the time goes in v5:
time: 89 us; the launch traced here: 88.7 us
  waiting for transfers between devices  33.5 us (38%)
  Pallas kernels  29.7 us (33%)
  starting transfers between devices  25 us (28%)
    ppermute x2, waiting for transfers between devices, layer(): arrived[-1].append(lax.ppermute(sent, 'fsdp', there))  18.6 us
    pallas_call x7, Pallas kernels, project(): pl.pallas_call(functools.partial(project_kernel, runs), in_specs=[VMEM] *...  11.3 us
    pallas_call x3, Pallas kernels, attend(): pl.pallas_call(functools.partial(attend_kernel, len(blocks), heads[0], No...  10.2 us
    ppermute x6, waiting for transfers between devices, layer(): returned.append(lax.ppermute(part, 'fsdp', back))  8.56 us
    ppermute x6, starting transfers between devices, layer(): chain.append(lax.ppermute(done, 'sp', ahead))  8.35 us
    ppermute x6, starting transfers between devices, layer(): near = lax.ppermute(pick(chain[b], chain[b + 1]), 'sp', swap)  7.24 us
    ppermute x6, starting transfers between devices, layer(): returned.append(lax.ppermute(part, 'fsdp', back))  6.18 us
    ppermute x6, waiting for transfers between devices, layer(): chain.append(lax.ppermute(done, 'sp', ahead))  5.23 us
  transfers between devices with their start and end apart: 21, of which 11 were waited for; matrix products, arithmetic and copies ran while one was open for 0% of the time, Pallas kernels for 30%

profile of v5, /device:TPU:0, one launch (start us, length us, event | category | flops | bytes accessed | tf_op | source)
XLA Modules:
  0.0 88.7 jit_solution(16601572088865378341)
XLA Ops:
  0.0 0.5 collective-permute-start
  0.5 2.1 %away.2 = bf16[128,2560]{1,0:T(8,128)(2,1)} custom-call(bf16[256,5120]{1,0:T(8,128)(2,1)} %bitcast.14, f32[1,5120]{1,0:T(1,128)} %bitcast.17), custom_call_target="tpu_custom_call" | custom-call | tf_op jit(solution)/shard_map/away/pallas_call | solution.py:79
  2.6 2.7 %collective-permute-start.1 = (bf16[128,2560]{1,0:T(8,128)(2,1)}, bf16[128,2560]{1,0:T(8,128)(2,1)}, u32[]{:S(2)}, u32[]{:S(2)}) collective-permute-start(bf16[128,2560]{1,0:T(8,128)(2,1)} %away.2), channel_id=1, source_target_pairs={{0,24},{8,16},{16,8},{24,0},{1,25},{9,17},{17,9},{25,1},{2,26},{10... | collective-permute-start | bytes 1966088 | tf_op jit(solution)/shard_map/ppermute | solution.py:420
  5.2 1.2 %away.3 = bf16[128,2560]{1,0:T(8,128)(2,1)S(1)} custom-call(bf16[256,5120]{1,0:T(8,128)(2,1)} %bitcast.15, f32[1,5120]{1,0:T(1,128)} %bitcast.18), custom_call_target="tpu_custom_call" | custom-call | tf_op jit(solution)/shard_map/away/pallas_call | solution.py:79
  6.5 0.1 collective-permute-start.4
  6.6 3.3 %home.1 = (bf16[256,2560]{1,0:T(8,128)(2,1)S(1)}, f32[256,1]{1,0:T(8,128)S(1)}, bf16[1280,2048]{1,0:T(8,128)(2,1)S(1)}) custom-call(bf16[256,5120]{1,0:T(8,128)(2,1)} %bitcast.16, f32[1,5120]{1,0:T(1,128)} %bitcast.19, bf16[1280,2048]{1,0:T(8,128)(2,1)} %weight_ref.1), custom_call_target="tpu_custom_call" | custom-call | tf_op jit(solution)/shard_map/home/pallas_call | solution.py:121
  9.9 10.8 %collective-permute-done.1.rows_ref = bf16[128,2560]{1,0:T(8,128)(2,1)} collective-permute-done((bf16[128,2560]{1,0:T(8,128)(2,1)}, bf16[128,2560]{1,0:T(8,128)(2,1)}, u32[]{:S(2)}, u32[]{:S(2)}) %collective-permute-start.1) | collective-permute-done | bytes 655392 | tf_op jit(solution)/shard_map/ppermute | solution.py:420
  20.7 0.0 collective-permute-done.refs_1_
  20.7 1.9 %project.10 = bf16[128,768]{1,0:T(8,128)(2,1)S(1)} custom-call(bf16[128,2560]{1,0:T(8,128)(2,1)} %collective-permute-done.1.rows_ref, bf16[1280,2048]{1,0:T(8,128)(2,1)S(1)} %get-tuple-element.11.refs_0_, bf16[1280,2048]{1,0:T(8,128)(2,1)S(1)} %collective-permute-done.refs_1_), custom_call_target="tpu_custom_call" | custom-call | flops 503316480 | bytes 3932160 | tf_op jit(solution)/shard_map/project/pallas_call | solution.py:167
  22.6 2.2 %collective-permute-start.9 = (bf16[128,768]{1,0:T(8,128)(2,1)S(1)}, bf16[128,768]{1,0:T(8,128)(2,1)S(1)}, u32[]{:S(2)}, u32[]{:S(2)}) collective-permute-start(bf16[128,768]{1,0:T(8,128)(2,1)S(1)} %project.10), channel_id=1, source_target_pairs={{24,0},{16,8},{8,16},{0,24},{25,1},{17,9},{9,17},{1,25},{26,2},{18... | collective-permute-start | bytes 589832 | tf_op jit(solution)/shard_map/ppermute | solution.py:437
  24.8 1.9 %project.12 = bf16[128,768]{1,0:T(8,128)(2,1)S(1)} custom-call(bf16[128,2560]{1,0:T(8,128)(2,1)} %collective-permute-done.1.rows_ref, bf16[1280,2048]{1,0:T(8,128)(2,1)S(1)} %get-tuple-element.11.refs_0_, bf16[1280,2048]{1,0:T(8,128)(2,1)S(1)} %collective-permute-done.refs_1_), custom_call_target="tpu_custom_call" | custom-call | flops 503316480 | bytes 3932160 | tf_op jit(solution)/shard_map/project/pallas_call | solution.py:167
  26.7 0.1 collective-permute-start.15
  26.8 7.8 %collective-permute-done.4.rows_ref = bf16[128,2560]{1,0:T(8,128)(2,1)S(1)} collective-permute-done((bf16[128,2560]{1,0:T(8,128)(2,1)S(1)}, bf16[128,2560]{1,0:T(8,128)(2,1)S(1)}, u32[]{:S(2)}, u32[]{:S(2)}) %collective-permute-start.4) | collective-permute-done | bytes 655392 | tf_op jit(solution)/shard_map/ppermute | solution.py:420
  34.6 0.8 project.11
  35.5 2.3 %collective-permute-start.11 = (bf16[128,768]{1,0:T(8,128)(2,1)S(1)}, bf16[128,768]{1,0:T(8,128)(2,1)S(1)}, u32[]{:S(2)}, u32[]{:S(2)}) collective-permute-start(bf16[128,768]{1,0:T(8,128)(2,1)S(1)} %project.11), channel_id=1, source_target_pairs={{24,0},{16,8},{8,16},{0,24},{25,1},{17,9},{9,17},{1,25},{26,2},{18... | collective-permute-start | bytes 589832 | tf_op jit(solution)/shard_map/ppermute | solution.py:437
  37.7 0.8 project.13
  38.6 0.1 collective-permute-start.17
  38.7 0.0 copy-start.1
  38.7 3.6 %project.7.mine_ref = f32[256,2048]{1,0:T(8,128)S(1)} custom-call(bf16[256,2560]{1,0:T(8,128)(2,1)S(1)} %get-tuple-element.10.rows_ref, bf16[1280,2048]{1,0:T(8,128)(2,1)S(1)} %get-tuple-element.11.refs_0_, bf16[1280,2048]{1,0:T(8,128)(2,1)S(1)} %collective-permute-done.refs_1_), custom_call_target="tpu_custom_call" | custom-call | flops 2684354560 | bytes 10485760 | tf_op jit(solution)/shard_map/project/pallas_call | solution.py:167
  42.2 0.8 collective-permute-done.15.refs_0_
  43.1 0.1 merge.10.even_ref.refs_4_
  43.2 1.6 %collective-permute-start.16 = (bf16[128,768]{1,0:T(8,128)(2,1)S(1)}, bf16[128,768]{1,0:T(8,128)(2,1)S(1)}, u32[]{:S(2)}, u32[]{:S(2)}) collective-permute-start(bf16[128,768]{1,0:T(8,128)(2,1)S(1)} %merge.10.even_ref.refs_4_), channel_id=1, source_target_pairs={{0,2},{1,3},{2,4},{3,5},{4,6},{5,7},{6,0},{7,1},{8,10},{9,11},{10,... | collective-permute-start | bytes 589832 | tf_op jit(solution)/shard_map/ppermute | solution.py:443
  44.8 6.7 %collective-permute-done.17.refs_0_ = bf16[128,768]{1,0:T(8,128)(2,1)S(1)} collective-permute-done((bf16[128,768]{1,0:T(8,128)(2,1)S(1)}, bf16[128,768]{1,0:T(8,128)(2,1)S(1)}, u32[]{:S(2)}, u32[]{:S(2)}) %collective-permute-start.17) | collective-permute-done | bytes 196640 | tf_op jit(solution)/shard_map/ppermute | solution.py:437
  51.5 0.1 merge.11.even_ref.refs_5_
  51.6 1.2 %collective-permute-start.18 = (bf16[128,768]{1,0:T(8,128)(2,1)S(1)}, bf16[128,768]{1,0:T(8,128)(2,1)S(1)}, u32[]{:S(2)}, u32[]{:S(2)}) collective-permute-start(bf16[128,768]{1,0:T(8,128)(2,1)S(1)} %merge.11.even_ref.refs_5_), channel_id=1, source_target_pairs={{0,2},{1,3},{2,4},{3,5},{4,6},{5,7},{6,0},{7,1},{8,10},{9,11},{10,... | collective-permute-start | bytes 589832 | tf_op jit(solution)/shard_map/ppermute | solution.py:443
  52.8 1.6 %project.8 = bf16[128,512]{1,0:T(8,128)(2,1)S(1)} custom-call(bf16[128,2560]{1,0:T(8,128)(2,1)} %collective-permute-done.1.rows_ref, bf16[1280,2048]{1,0:T(8,128)(2,1)S(1)} %get-tuple-element.11.refs_0_, bf16[1280,2048]{1,0:T(8,128)(2,1)S(1)} %collective-permute-done.refs_1_), custom_call_target="tpu_custom_call" | custom-call | flops 335544320 | bytes 2621440 | tf_op jit(solution)/shard_map/project/pallas_call | solution.py:167
  54.4 1.4 %collective-permute-start.2 = (bf16[128,512]{1,0:T(8,128)(2,1)S(1)}, bf16[128,512]{1,0:T(8,128)(2,1)S(1)}, u32[]{:S(2)}, u32[]{:S(2)}) collective-permute-start(bf16[128,512]{1,0:T(8,128)(2,1)S(1)} %project.8), channel_id=1, source_target_pairs={{24,0},{16,8},{8,16},{0,24},{25,1},{17,9},{9,17},{1,25},{26,2},{18... | collective-permute-start | bytes 393224 | tf_op jit(solution)/shard_map/ppermute | solution.py:437
  55.9 0.0 collective-permute-done.9.refs_0_
  55.9 0.1 merge.8.even_ref.refs_4_
  56.0 1.6 %collective-permute-start.10 = (bf16[128,768]{1,0:T(8,128)(2,1)S(1)}, bf16[128,768]{1,0:T(8,128)(2,1)S(1)}, u32[]{:S(2)}, u32[]{:S(2)}) collective-permute-start(bf16[128,768]{1,0:T(8,128)(2,1)S(1)} %merge.8.even_ref.refs_4_), channel_id=1, source_target_pairs={{0,2},{1,3},{2,4},{3,5},{4,6},{5,7},{6,0},{7,1},{8,10},{9,11},{10,... | collective-permute-start | bytes 589832 | tf_op jit(solution)/shard_map/ppermute | solution.py:443
  57.6 0.5 project.9
  58.2 0.0 collective-permute-done.11.refs_0_
  58.2 0.2 collective-permute-start.5
  58.3 0.1 merge.9.even_ref.refs_5_
  58.5 0.0 collective-permute-done.16.odd_ref.refs_0_
  58.5 1.6 %collective-permute-start.12 = (bf16[128,768]{1,0:T(8,128)(2,1)S(1)}, bf16[128,768]{1,0:T(8,128)(2,1)S(1)}, u32[]{:S(2)}, u32[]{:S(2)}) collective-permute-start(bf16[128,768]{1,0:T(8,128)(2,1)S(1)} %merge.9.even_ref.refs_5_), channel_id=1, source_target_pairs={{0,2},{1,3},{2,4},{3,5},{4,6},{5,7},{6,0},{7,1},{8,10},{9,11},{10,... | collective-permute-start | bytes 589832 | tf_op jit(solution)/shard_map/ppermute | solution.py:443
  60.1 0.4 collective-permute-done.18.odd_ref.refs_1_
  60.5 1.6 %collective-permute-start.19 = (bf16[128,768]{1,0:T(8,128)(2,1)S(1)}, bf16[128,768]{1,0:T(8,128)(2,1)S(1)}, u32[]{:S(2)}, u32[]{:S(2)}) collective-permute-start(bf16[128,768]{1,0:T(8,128)(2,1)S(1)} %pick.10), channel_id=1, source_target_pairs={{0,1},{1,0},{2,3},{3,2},{4,5},{5,4},{6,7},{7,6},{8,9},{9,8},{10,11... | collective-permute-start | bytes 589832 | tf_op jit(solution)/shard_map/ppermute | solution.py:449
  62.1 0.0 collective-permute-done.2.refs_0_
  62.2 0.5 collective-permute-start.20
  62.7 0.1 merge.6.even_ref.refs_4_
  62.8 0.0 copy-start.2
  62.8 0.0 copy-start
  62.8 1.1 %collective-permute-done.5.refs_0_ = bf16[128,512]{1,0:T(8,128)(2,1)S(1)} collective-permute-done((bf16[128,512]{1,0:T(8,128)(2,1)S(1)}, bf16[128,512]{1,0:T(8,128)(2,1)S(1)}, u32[]{:S(2)}, u32[]{:S(2)}) %collective-permute-start.5) | collective-permute-done | bytes 131104 | tf_op jit(solution)/shard_map/ppermute | solution.py:437
  63.9 1.5 %collective-permute-start.3 = (bf16[128,512]{1,0:T(8,128)(2,1)S(1)}, bf16[128,512]{1,0:T(8,128)(2,1)S(1)}, u32[]{:S(2)}, u32[]{:S(2)}) collective-permute-start(bf16[128,512]{1,0:T(8,128)(2,1)S(1)} %merge.6.even_ref.refs_4_), channel_id=1, source_target_pairs={{0,2},{1,3},{2,4},{3,5},{4,6},{5,7},{6,0},{7,1},{8,10},{9,11},{10,... | collective-permute-start | bytes 393224 | tf_op jit(solution)/shard_map/ppermute | solution.py:443
  65.4 0.1 merge.7.even_ref.refs_5_
  65.5 0.1 collective-permute-done.10.odd_ref.refs_0_
  65.6 0.7 collective-permute-start.6
  66.3 3.4 %collective-permute-done.12.odd_ref.refs_1_ = bf16[128,768]{1,0:T(8,128)(2,1)S(1)} collective-permute-done((bf16[128,768]{1,0:T(8,128)(2,1)S(1)}, bf16[128,768]{1,0:T(8,128)(2,1)S(1)}, u32[]{:S(2)}, u32[]{:S(2)}) %collective-permute-start.12) | collective-permute-done | bytes 196640 | tf_op jit(solution)/shard_map/ppermute | solution.py:443
  69.7 1.5 %collective-permute-start.13 = (bf16[128,768]{1,0:T(8,128)(2,1)S(1)}, bf16[128,768]{1,0:T(8,128)(2,1)S(1)}, u32[]{:S(2)}, u32[]{:S(2)}) collective-permute-start(bf16[128,768]{1,0:T(8,128)(2,1)S(1)} %pick.8), channel_id=1, source_target_pairs={{0,1},{1,0},{2,3},{3,2},{4,5},{5,4},{6,7},{7,6},{8,9},{9,8},{10,11... | collective-permute-start | bytes 589832 | tf_op jit(solution)/shard_map/ppermute | solution.py:449
  71.2 1.3 %collective-permute-done.3.odd_ref.refs_0_ = bf16[128,512]{1,0:T(8,128)(2,1)S(1)} collective-permute-done((bf16[128,512]{1,0:T(8,128)(2,1)S(1)}, bf16[128,512]{1,0:T(8,128)(2,1)S(1)}, u32[]{:S(2)}, u32[]{:S(2)}) %collective-permute-start.3) | collective-permute-done | bytes 131104 | tf_op jit(solution)/shard_map/ppermute | solution.py:443
  72.5 1.5 %collective-permute-start.14 = (bf16[128,768]{1,0:T(8,128)(2,1)S(1)}, bf16[128,768]{1,0:T(8,128)(2,1)S(1)}, u32[]{:S(2)}, u32[]{:S(2)}) collective-permute-start(bf16[128,768]{1,0:T(8,128)(2,1)S(1)} %pick.9), channel_id=1, source_target_pairs={{0,1},{1,0},{2,3},{3,2},{4,5},{5,4},{6,7},{7,6},{8,9},{9,8},{10,11... | collective-permute-start | bytes 589832 | tf_op jit(solution)/shard_map/ppermute | solution.py:449
  74.0 0.8 mask.1.bias_ref
  74.9 0.0 collective-permute-done.6.odd_ref.refs_1_
  74.9 1.4 %collective-permute-start.7 = (bf16[128,512]{1,0:T(8,128)(2,1)S(1)}, bf16[128,512]{1,0:T(8,128)(2,1)S(1)}, u32[]{:S(2)}, u32[]{:S(2)}) collective-permute-start(bf16[128,512]{1,0:T(8,128)(2,1)S(1)} %pick.6), channel_id=1, source_target_pairs={{0,1},{1,0},{2,3},{3,2},{4,5},{5,4},{6,7},{7,6},{8,9},{9,8},{10,11... | collective-permute-start | bytes 393224 | tf_op jit(solution)/shard_map/ppermute | solution.py:449
  76.2 0.2 pick.7
  76.4 0.0 collective-permute-done.19.refs_2_
  76.4 0.8 collective-permute-start.8
  77.2 0.0 collective-permute-done.20.refs_3_
  77.2 3.3 %attend.3.refs_6_ = bf16[6,128,512]{2,1,0:T(8,128)(2,1)S(1)} custom-call(f32[256,768]{1,0:T(8,128)S(1)} %mask.1.bias_ref, bf16[256,4096]{1,0:T(8,128)(2,1)S(1)} %bitcast.5, bf16[128,768]{1,0:T(8,128)(2,1)S(1)} %collective-permute-done.16.odd_ref.refs_0_, bf16[128,768]{1,0:T(8,128)(2,1)S(1)} %collective-permute-done.18.odd_ref.refs_1_, ...), custom_call_target="tpu_custom_call" | custom-call | flops 1509949440 | bytes 1572864 | tf_op jit(solution)/shard_map/attend/pallas_call | solution.py:376
  80.5 0.9 %collective-permute-done.14.refs_3_ = bf16[128,768]{1,0:T(8,128)(2,1)S(1)} collective-permute-done((bf16[128,768]{1,0:T(8,128)(2,1)S(1)}, bf16[128,768]{1,0:T(8,128)(2,1)S(1)}, u32[]{:S(2)}, u32[]{:S(2)}) %collective-permute-start.14) | collective-permute-done | bytes 196640 | tf_op jit(solution)/shard_map/ppermute | solution.py:449
  81.5 3.8 %attend.4 = (bf16[256,4096]{1,0:T(8,128)(2,1)}, bf16[6,128,512]{2,1,0:T(8,128)(2,1)S(1)}) custom-call(f32[256,768]{1,0:T(8,128)S(1)} %mask.1.bias_ref, bf16[256,4096]{1,0:T(8,128)(2,1)S(1)} %bitcast.6, bf16[128,768]{1,0:T(8,128)(2,1)S(1)} %collective-permute-done.10.odd_ref.refs_0_, bf16[128,768]{1,0:T(8,128)(2,1)S(1)} %collective-permute-done.12.odd_ref.refs_1_, ...), custom_call_target="tpu_custom_call" | custom-call | flops 1509949440 | bytes 1572864 | tf_op jit(solution)/shard_map/attend/pallas_call | solution.py:376
  85.3 0.2 collective-permute-done.8.refs_3_
  85.5 3.1 %attend.5 = bf16[256,4096]{1,0:T(8,128)(2,1)} custom-call(f32[256,768]{1,0:T(8,128)S(1)} %mask.1.bias_ref, bf16[256,4096]{1,0:T(8,128)(2,1)S(1)} %bitcast.7, bf16[128,512]{1,0:T(8,128)(2,1)S(1)} %collective-permute-done.3.odd_ref.refs_0_, bf16[128,512]{1,0:T(8,128)(2,1)S(1)} %collective-permute-done.6.odd_ref.refs_1_, ...), custom_call_target="tpu_custom_call", output_to_operand_aliasing={{}: (9, {})} | custom-call | flops 1006632960 | bytes 1048576 | tf_op jit(solution)/shard_map/attend/pallas_call | solution.py:376
  (10 shorter events, 0.1 us)
Async XLA Ops:
  0.0 20.7 %collective-permute-start = (bf16[1280,2048]{1,0:T(8,128)(2,1)}, bf16[1280,2048]{1,0:T(8,128)(2,1)S(1)}, u32[]{:S(2)}, u32[]{:S(2)}) collective-permute-start(bf16[1280,2048]{1,0:T(8,128)(2,1)} %weight_ref.1), channel_id=1, source_target_pairs={{0,8},{8,0},{16,24},{24,16},{1,9},{9,1},{17,25},{25,17},{2,10},{10... | collective-permute-start | bytes 15728648 | tf_op jit(solution)/shard_map/ppermute | solution.py:424
  2.6 18.1 %collective-permute-start.1 = (bf16[128,2560]{1,0:T(8,128)(2,1)}, bf16[128,2560]{1,0:T(8,128)(2,1)}, u32[]{:S(2)}, u32[]{:S(2)}) collective-permute-start(bf16[128,2560]{1,0:T(8,128)(2,1)} %away.2), channel_id=1, source_target_pairs={{0,24},{8,16},{16,8},{24,0},{1,25},{9,17},{17,9},{25,1},{2,26},{10... | collective-permute-start | bytes 1966088 | tf_op jit(solution)/shard_map/ppermute | solution.py:420
  6.5 28.1 %collective-permute-start.4 = (bf16[128,2560]{1,0:T(8,128)(2,1)S(1)}, bf16[128,2560]{1,0:T(8,128)(2,1)S(1)}, u32[]{:S(2)}, u32[]{:S(2)}) collective-permute-start(bf16[128,2560]{1,0:T(8,128)(2,1)S(1)} %away.3), channel_id=1, source_target_pairs={{0,24},{8,16},{16,8},{24,0},{1,25},{9,17},{17,9},{25,1},{2,26},{10... | collective-permute-start | bytes 1966088 | tf_op jit(solution)/shard_map/ppermute | solution.py:420
  22.6 33.2 %collective-permute-start.9 = (bf16[128,768]{1,0:T(8,128)(2,1)S(1)}, bf16[128,768]{1,0:T(8,128)(2,1)S(1)}, u32[]{:S(2)}, u32[]{:S(2)}) collective-permute-start(bf16[128,768]{1,0:T(8,128)(2,1)S(1)} %project.10), channel_id=1, source_target_pairs={{24,0},{16,8},{8,16},{0,24},{25,1},{17,9},{9,17},{1,25},{26,2},{18... | collective-permute-start | bytes 589832 | tf_op jit(solution)/shard_map/ppermute | solution.py:437
  26.7 16.3 %collective-permute-start.15 = (bf16[128,768]{1,0:T(8,128)(2,1)S(1)}, bf16[128,768]{1,0:T(8,128)(2,1)S(1)}, u32[]{:S(2)}, u32[]{:S(2)}) collective-permute-start(bf16[128,768]{1,0:T(8,128)(2,1)S(1)} %project.12), channel_id=1, source_target_pairs={{24,0},{16,8},{8,16},{0,24},{25,1},{17,9},{9,17},{1,25},{26,2},{18... | collective-permute-start | bytes 589832 | tf_op jit(solution)/shard_map/ppermute | solution.py:437
  35.5 22.7 %collective-permute-start.11 = (bf16[128,768]{1,0:T(8,128)(2,1)S(1)}, bf16[128,768]{1,0:T(8,128)(2,1)S(1)}, u32[]{:S(2)}, u32[]{:S(2)}) collective-permute-start(bf16[128,768]{1,0:T(8,128)(2,1)S(1)} %project.11), channel_id=1, source_target_pairs={{24,0},{16,8},{8,16},{0,24},{25,1},{17,9},{9,17},{1,25},{26,2},{18... | collective-permute-start | bytes 589832 | tf_op jit(solution)/shard_map/ppermute | solution.py:437
  38.6 12.9 %collective-permute-start.17 = (bf16[128,768]{1,0:T(8,128)(2,1)S(1)}, bf16[128,768]{1,0:T(8,128)(2,1)S(1)}, u32[]{:S(2)}, u32[]{:S(2)}) collective-permute-start(bf16[128,768]{1,0:T(8,128)(2,1)S(1)} %project.13), channel_id=1, source_target_pairs={{24,0},{16,8},{8,16},{0,24},{25,1},{17,9},{9,17},{1,25},{26,2},{18... | collective-permute-start | bytes 589832 | tf_op jit(solution)/shard_map/ppermute | solution.py:437
  38.7 4.4 %copy-start.1 = (f32[1024]{0:T(1024)S(1)}, f32[1024]{0:T(1024)}, u32[]{:S(2)}) copy-start(f32[1024]{0:T(1024)} %param.10) | copy-start | bytes 12292
  43.2 15.3 %collective-permute-start.16 = (bf16[128,768]{1,0:T(8,128)(2,1)S(1)}, bf16[128,768]{1,0:T(8,128)(2,1)S(1)}, u32[]{:S(2)}, u32[]{:S(2)}) collective-permute-start(bf16[128,768]{1,0:T(8,128)(2,1)S(1)} %merge.10.even_ref.refs_4_), channel_id=1, source_target_pairs={{0,2},{1,3},{2,4},{3,5},{4,6},{5,7},{6,0},{7,1},{8,10},{9,11},{10,... | collective-permute-start | bytes 589832 | tf_op jit(solution)/shard_map/ppermute | solution.py:443
  51.6 9.0 %collective-permute-start.18 = (bf16[128,768]{1,0:T(8,128)(2,1)S(1)}, bf16[128,768]{1,0:T(8,128)(2,1)S(1)}, u32[]{:S(2)}, u32[]{:S(2)}) collective-permute-start(bf16[128,768]{1,0:T(8,128)(2,1)S(1)} %merge.11.even_ref.refs_5_), channel_id=1, source_target_pairs={{0,2},{1,3},{2,4},{3,5},{4,6},{5,7},{6,0},{7,1},{8,10},{9,11},{10,... | collective-permute-start | bytes 589832 | tf_op jit(solution)/shard_map/ppermute | solution.py:443
  54.4 7.7 %collective-permute-start.2 = (bf16[128,512]{1,0:T(8,128)(2,1)S(1)}, bf16[128,512]{1,0:T(8,128)(2,1)S(1)}, u32[]{:S(2)}, u32[]{:S(2)}) collective-permute-start(bf16[128,512]{1,0:T(8,128)(2,1)S(1)} %project.8), channel_id=1, source_target_pairs={{24,0},{16,8},{8,16},{0,24},{25,1},{17,9},{9,17},{1,25},{26,2},{18... | collective-permute-start | bytes 393224 | tf_op jit(solution)/shard_map/ppermute | solution.py:437
  56.0 9.6 %collective-permute-start.10 = (bf16[128,768]{1,0:T(8,128)(2,1)S(1)}, bf16[128,768]{1,0:T(8,128)(2,1)S(1)}, u32[]{:S(2)}, u32[]{:S(2)}) collective-permute-start(bf16[128,768]{1,0:T(8,128)(2,1)S(1)} %merge.8.even_ref.refs_4_), channel_id=1, source_target_pairs={{0,2},{1,3},{2,4},{3,5},{4,6},{5,7},{6,0},{7,1},{8,10},{9,11},{10,... | collective-permute-start | bytes 589832 | tf_op jit(solution)/shard_map/ppermute | solution.py:443
  58.2 5.7 %collective-permute-start.5 = (bf16[128,512]{1,0:T(8,128)(2,1)S(1)}, bf16[128,512]{1,0:T(8,128)(2,1)S(1)}, u32[]{:S(2)}, u32[]{:S(2)}) collective-permute-start(bf16[128,512]{1,0:T(8,128)(2,1)S(1)} %project.9), channel_id=1, source_target_pairs={{24,0},{16,8},{8,16},{0,24},{25,1},{17,9},{9,17},{1,25},{26,2},{18... | collective-permute-start | bytes 393224 | tf_op jit(solution)/shard_map/ppermute | solution.py:437
  58.5 11.3 %collective-permute-start.12 = (bf16[128,768]{1,0:T(8,128)(2,1)S(1)}, bf16[128,768]{1,0:T(8,128)(2,1)S(1)}, u32[]{:S(2)}, u32[]{:S(2)}) collective-permute-start(bf16[128,768]{1,0:T(8,128)(2,1)S(1)} %merge.9.even_ref.refs_5_), channel_id=1, source_target_pairs={{0,2},{1,3},{2,4},{3,5},{4,6},{5,7},{6,0},{7,1},{8,10},{9,11},{10,... | collective-permute-start | bytes 589832 | tf_op jit(solution)/shard_map/ppermute | solution.py:443
  60.5 15.9 %collective-permute-start.19 = (bf16[128,768]{1,0:T(8,128)(2,1)S(1)}, bf16[128,768]{1,0:T(8,128)(2,1)S(1)}, u32[]{:S(2)}, u32[]{:S(2)}) collective-permute-start(bf16[128,768]{1,0:T(8,128)(2,1)S(1)} %pick.10), channel_id=1, source_target_pairs={{0,1},{1,0},{2,3},{3,2},{4,5},{5,4},{6,7},{7,6},{8,9},{9,8},{10,11... | collective-permute-start | bytes 589832 | tf_op jit(solution)/shard_map/ppermute | solution.py:449
  62.2 15.1 %collective-permute-start.20 = (bf16[128,768]{1,0:T(8,128)(2,1)S(1)}, bf16[128,768]{1,0:T(8,128)(2,1)S(1)}, u32[]{:S(2)}, u32[]{:S(2)}) collective-permute-start(bf16[128,768]{1,0:T(8,128)(2,1)S(1)} %pick.11), channel_id=1, source_target_pairs={{0,1},{1,0},{2,3},{3,2},{4,5},{5,4},{6,7},{7,6},{8,9},{9,8},{10,11... | collective-permute-start | bytes 589832 | tf_op jit(solution)/shard_map/ppermute | solution.py:449
  62.8 11.3 %copy-start.2 = (s32[1,16]{1,0:T(1,128)S(1)}, s32[1,16]{1,0:T(1,128)}, u32[]{:S(2)}) copy-start(s32[1,16]{1,0:T(1,128)} %lengths_ref.1) | copy-start | bytes 196
  62.8 14.5 %copy-start = (bf16[1,256,4096]{2,1,0:T(8,128)(2,1)S(1)}, bf16[1,256,4096]{2,1,0:T(8,128)(2,1)}, u32[]{:S(2)}) copy-start(bf16[1,256,4096]{2,1,0:T(8,128)(2,1)} %param.7) | copy-start | bytes 6291460
  63.9 8.7 %collective-permute-start.3 = (bf16[128,512]{1,0:T(8,128)(2,1)S(1)}, bf16[128,512]{1,0:T(8,128)(2,1)S(1)}, u32[]{:S(2)}, u32[]{:S(2)}) collective-permute-start(bf16[128,512]{1,0:T(8,128)(2,1)S(1)} %merge.6.even_ref.refs_4_), channel_id=1, source_target_pairs={{0,2},{1,3},{2,4},{3,5},{4,6},{5,7},{6,0},{7,1},{8,10},{9,11},{10,... | collective-permute-start | bytes 393224 | tf_op jit(solution)/shard_map/ppermute | solution.py:443
  65.6 9.3 %collective-permute-start.6 = (bf16[128,512]{1,0:T(8,128)(2,1)S(1)}, bf16[128,512]{1,0:T(8,128)(2,1)S(1)}, u32[]{:S(2)}, u32[]{:S(2)}) collective-permute-start(bf16[128,512]{1,0:T(8,128)(2,1)S(1)} %merge.7.even_ref.refs_5_), channel_id=1, source_target_pairs={{0,2},{1,3},{2,4},{3,5},{4,6},{5,7},{6,0},{7,1},{8,10},{9,11},{10,... | collective-permute-start | bytes 393224 | tf_op jit(solution)/shard_map/ppermute | solution.py:443
  69.7 10.8 %collective-permute-start.13 = (bf16[128,768]{1,0:T(8,128)(2,1)S(1)}, bf16[128,768]{1,0:T(8,128)(2,1)S(1)}, u32[]{:S(2)}, u32[]{:S(2)}) collective-permute-start(bf16[128,768]{1,0:T(8,128)(2,1)S(1)} %pick.8), channel_id=1, source_target_pairs={{0,1},{1,0},{2,3},{3,2},{4,5},{5,4},{6,7},{7,6},{8,9},{9,8},{10,11... | collective-permute-start | bytes 589832 | tf_op jit(solution)/shard_map/ppermute | solution.py:449
  72.5 8.9 %collective-permute-start.14 = (bf16[128,768]{1,0:T(8,128)(2,1)S(1)}, bf16[128,768]{1,0:T(8,128)(2,1)S(1)}, u32[]{:S(2)}, u32[]{:S(2)}) collective-permute-start(bf16[128,768]{1,0:T(8,128)(2,1)S(1)} %pick.9), channel_id=1, source_target_pairs={{0,1},{1,0},{2,3},{3,2},{4,5},{5,4},{6,7},{7,6},{8,9},{9,8},{10,11... | collective-permute-start | bytes 589832 | tf_op jit(solution)/shard_map/ppermute | solution.py:449
  74.9 10.4 %collective-permute-start.7 = (bf16[128,512]{1,0:T(8,128)(2,1)S(1)}, bf16[128,512]{1,0:T(8,128)(2,1)S(1)}, u32[]{:S(2)}, u32[]{:S(2)}) collective-permute-start(bf16[128,512]{1,0:T(8,128)(2,1)S(1)} %pick.6), channel_id=1, source_target_pairs={{0,1},{1,0},{2,3},{3,2},{4,5},{5,4},{6,7},{7,6},{8,9},{9,8},{10,11... | collective-permute-start | bytes 393224 | tf_op jit(solution)/shard_map/ppermute | solution.py:449
  76.4 9.0 %collective-permute-start.8 = (bf16[128,512]{1,0:T(8,128)(2,1)S(1)}, bf16[128,512]{1,0:T(8,128)(2,1)S(1)}, u32[]{:S(2)}, u32[]{:S(2)}) collective-permute-start(bf16[128,512]{1,0:T(8,128)(2,1)S(1)} %pick.7), channel_id=1, source_target_pairs={{0,1},{1,0},{2,3},{3,2},{4,5},{5,4},{6,7},{7,6},{8,9},{9,8},{10,11... | collective-permute-start | bytes 393224 | tf_op jit(solution)/shard_map/ppermute | solution.py:449
